TPU v7x, 512 devices: a whole 4x8x8 slice. The times are simulated.
512 devices in a mesh: grp: 128 (over y, x_lo, z), blk: 4 (over x_hi, core).
Axes of the slice: x: 4 (x_hi: 2, x_lo: 2; x = x_hi * 2 + x_lo), y: 8, z: 8, core: 2. Of those that a mesh axis runs over, the one named last changes fastest.
Arguments:
- amplitudes: bfloat16 [2048, 128, 512], P('grp', 'blk'), may hold values from -6 to 6
- integrals: float32 [2048, 12, 128, 128], P(('grp', 'blk')), may hold values from -0.15625 to 0.15625
- tile_rows: int32 [2048, 12], P(('grp', 'blk')), may hold values from 0 to 2047, as said below
- destinations: int32 [2048, 4], replicated, may hold values from 0 to 127, as said below
- source_terms: bfloat16 [262144, 512], P(('grp', 'blk')), may hold values from -6 to 6
- occ_energy: float32 [512], replicated, may hold values from 0.5 to 4
- virt_energy: float32 [262144], P(('grp', 'blk')), may hold values from 0.5 to 4
Outputs:
- new_amplitudes: bfloat16 [262144, 512], P(('grp', 'blk'))
Inputs may be any that keep to these rules, and one draw needn't show every extreme that they name: `destinations`: each row names 4 different groups. Every group is named by exactly 64 rows in all. Among the 16 rows k of one owning group k // 16, no group is named by more than 2 rows, and that many is reached. `tile_rows`: the 12 entries of a row are different.
All inputs are finite; a program needn't handle non-finite values.
Results may differ from a plain program's by a relative error of at most 0.001.
Values may be sent and summed in bfloat16 or wider, within the bound.
No kernel may reach another device: no remote copies, remote signals or barrier semaphores. Data moves between devices by JAX's collectives and lax.ppermute only.
A program may use at most 64 MiB of HBM per device.

v0:
```python
import jax
import jax.numpy as jnp
from jax import lax
from jax.sharding import PartitionSpec as P

DEST = 4


def per_device(
    amplitudes, integrals, tile_rows, destinations, source_terms, occ_energy, virt_energy
):
    groups = lax.axis_size("grp")
    own_group = lax.axis_index("grp")
    owned_tiles = amplitudes.shape[0]
    quarter = amplitudes.shape[1]
    pair_width = amplitudes.shape[2]
    all_tiles = destinations.shape[0]
    slot_count = max(2, owned_tiles * DEST // groups)
    my_dest = lax.dynamic_slice_in_dim(destinations, own_group * owned_tiles, owned_tiles, 0)
    targets = jnp.arange(groups, dtype=jnp.int32)
    named_mine = jnp.any(my_dest[:, :, None] == targets[None, None, :], axis=1).astype(jnp.int32)
    before = jnp.cumsum(named_mine, axis=0) - named_mine
    slot_of = jnp.take_along_axis(before, my_dest, axis=1)
    send_place = my_dest * slot_count + slot_of
    select = jnp.any(
        jnp.arange(groups * slot_count, dtype=jnp.int32)[:, None, None] == send_place[None, :, :],
        axis=2,
    )
    select = select.astype(jnp.bfloat16)
    outgoing = jnp.dot(
        select,
        amplitudes.reshape(owned_tiles, quarter * pair_width),
        preferred_element_type=jnp.float32,
    )
    outgoing = outgoing.astype(jnp.bfloat16).reshape(groups * slot_count, quarter, pair_width)
    named_all = jnp.any(destinations == own_group, axis=1).astype(jnp.int32)
    per_source = named_all.reshape(groups, owned_tiles)
    slot_all = (jnp.cumsum(per_source, axis=1) - per_source).reshape(all_tiles)
    source_of = jnp.arange(all_tiles, dtype=jnp.int32) // owned_tiles
    position = source_of * slot_count + slot_all
    compact_of = jnp.cumsum(named_all) - named_all
    received = owned_tiles * DEST
    matches = (compact_of[None, :] == jnp.arange(received, dtype=jnp.int32)[:, None]) & (
        named_all[None, :] == 1
    )
    pick_rows = jnp.sum(jnp.where(matches, position[None, :], 0), axis=1)
    delivered = named_all[tile_rows]
    slots_used = jnp.where(delivered == 1, compact_of[tile_rows], 0)
    weights = integrals * delivered.astype(jnp.float32)[:, :, None, None]
    columns, row_tiles = tile_rows.shape
    tile_size = integrals.shape[3]
    flat_slots = slots_used.reshape(columns * row_tiles)
    incoming = lax.all_to_all(outgoing, "grp", split_axis=0, concat_axis=0, tiled=True)
    gathered_rows = jnp.take(incoming, pick_rows, axis=0)
    arrived = lax.all_gather(gathered_rows, "blk", axis=1, tiled=True)
    rows_here = arrived.shape[1]
    width_here = arrived.shape[2]
    picked = jnp.take(arrived, flat_slots, axis=0).reshape(
        columns, row_tiles, rows_here, width_here
    )
    picked = picked.astype(jnp.float32)
    ladder = jnp.einsum("crqk,crqp->ckp", weights, picked, precision=lax.Precision.HIGHEST)
    ladder = ladder.reshape(columns * tile_size, pair_width)
    denominator = virt_energy[:, None] + occ_energy[None, :]
    return ((source_terms.astype(jnp.float32) + ladder) / denominator).astype(jnp.bfloat16)


def solution(mesh):
    in_specs = (
        P("grp", "blk", None),
        P(("grp", "blk"), None, None, None),
        P(("grp", "blk"), None),
        P(),
        P(("grp", "blk"), None),
        P(),
        P(("grp", "blk")),
    )
    out_specs = P(("grp", "blk"), None)
    return jax.shard_map(
        per_device, mesh=mesh, in_specs=in_specs, out_specs=out_specs, check_vma=False
    )
```

profile of v0, /device:TPU:1, one launch (start us, length us, event | category | flops | bytes accessed | tf_op | source)
XLA Modules:
  0.0 397.3 jit_solution(89998441502436940)
XLA Ops:
  6.5 0.0 copy-start
  6.5 0.8 constant_dynamic-slice_fusion
  7.3 0.1 fusion.10
  7.4 0.1 copy.28
  7.6 0.1 copy.22
  7.7 0.1 copy.23
  7.8 0.1 reshape.189
  7.8 0.8 gather_fusion.4
  8.6 0.1 reshape.192
  8.7 0.1 copy.24
  8.8 0.1 fusion.9
  8.9 0.0 copy-done
  8.9 0.3 copy.29
  9.2 5.6 %convolution_convert_fusion = bf16[256,16384]{1,0:T(8,128)(2,1)} fusion(pred[256,16]{0,1:T(8,128)(4,1)S(1)} %fusion.9, bf16[16,16384]{1,0:T(8,128)(2,1)S(1)} %bitcast.35), kind=kOutput, calls=%fused_computation.5 | convolution fusion | flops 138412032 | bytes 8916992 | tf_op jit(solution)/shard_map/dot_general | solution.py:30
  14.8 10.4 %copy.30 = bf16[32,8,32,512]{3,2,1,0:T(8,128)(2,1)} copy(bf16[32,8,32,512]{3,1,2,0:T(8,128)(2,1)} %bitcast.33) | data formatting | bytes 16777216
  25.2 0.0 copy-start.2
  25.2 19.9 %all-to-all-start = ((bf16[256,32,512]{2,1,0:T(8,128)(2,1)}), bf16[256,32,512]{2,1,0:T(8,128)(2,1)}, u32[]{:S(2)}, u32[]{:S(2)}) async-start(bf16[256,32,512]{2,1,0:T(8,128)(2,1)} %bitcast.32), calls=%async_computation | async-start | bytes 16777216 | tf_op jit(solution)/shard_map/all_to_all | solution.py:53
  45.2 0.0 copy-start.3
  45.2 0.2 all-gather.2.cloned.1.call-start
  45.4 0.0 copy-done.2
  45.5 0.1 reshape.156
  45.5 0.1 copy.18
  45.6 0.1 reduce_window_sum.45
  45.6 0.1 copy.19
  45.8 0.1 reduce_window_sum.46
  45.8 0.3 reduce-window.9
  46.1 0.1 slice.19
  46.2 0.1 slice_reduce_fusion
  46.3 0.1 convert_subtract_fusion.1
  46.4 0.2 select_reduce_fusion
  46.7 220.9 %all-to-all-done = bf16[256,32,512]{2,1,0:T(8,128)(2,1)} async-done(((bf16[256,32,512]{2,1,0:T(8,128)(2,1)}), bf16[256,32,512]{2,1,0:T(8,128)(2,1)}, u32[]{:S(2)}, u32[]{:S(2)}) %all-to-all-start) | async-done | bytes 8388640 | tf_op jit(solution)/shard_map/all_to_all | solution.py:53
  267.6 4.1 %gather_fusion.2 = bf16[64,32,512]{2,1,0:T(8,128)(2,1)S(1)} fusion(bf16[256,32,512]{2,1,0:T(8,128)(2,1)} %all-to-all-done, s32[1024]{0:T(1024)S(1)} %pad_clamp_fusion.1), kind=kCustom, calls=%fused_computation.2 | custom fusion | bytes 4194560 | tf_op jit(solution)/shard_map/jit(_take)/gather | solution.py:54
  271.6 1.6 broadcast_select_fusion
  273.3 0.0 all-gather.2.cloned.1.call-update
  273.3 0.0 copy-done.3
  273.3 0.1 reshape.159
  273.4 0.8 gather_fusion.1
  274.2 0.8 gather_fusion
  275.0 0.1 reshape.206
  275.1 0.1 reshape.199
  275.2 0.0 copy-start.6
  275.2 100.1 %all-gather.2.cloned.1.call-done = bf16[64,128,512]{2,1,0:T(8,128)(2,1)} async-done(((bf16[64,32,512]{2,1,0:T(8,128)(2,1)}), bf16[64,128,512]{2,1,0:T(8,128)(2,1)}) %all-gather.2.cloned.1.call-update) | async-done | bytes 8388624 | tf_op jit(solution)/shard_map/all_gather | solution.py:55
  375.3 8.4 %gather_fusion.3 = bf16[48,128,512]{2,1,0:T(8,128)(2,1)} fusion(bf16[64,128,512]{2,1,0:T(8,128)(2,1)} %all-gather.2.cloned.1.call-done, s32[1024]{0:T(1024)S(1)} %pad_clamp_fusion), kind=kCustom, calls=%fused_computation.3 | custom fusion | bytes 12583104 | tf_op jit(solution)/shard_map/jit(_take)/gather | solution.py:58
  383.7 0.0 copy-start.1
  383.7 0.0 copy-start.4
  383.7 0.0 copy-start.5
  383.7 0.0 copy-done.6
  383.7 5.7 %fusion = f32[4,128,512,1]{2,1,3,0:T(8,128)S(1)} fusion(bf16[4,12,128,512]{3,2,1,0:T(8,128)(2,1)} %bitcast.34, pred[4,12]{1,0:T(4,128)(4,1)S(1)} %compare_and_fusion.1, f32[4,12,128,128]{3,2,1,0:T(8,128)S(1)} %copy-done.6, f32[4,12]{1,0:T(4,128)S(1)} %reshape.199), kind=kOutput, calls=%fused_computation.6 | convolution fusion | flops 4835770368 | bytes 10486000 | tf_op jit(solution)/shard_map/crqk,crqp->ckp/dot_general | solution.py:62
  389.4 0.0 copy-done.1
  389.4 0.0 copy-done.4
  389.4 0.0 copy-done.5
  389.5 1.0 fusion.7
  (18 shorter events, 0.2 us)
Async XLA Ops:
  6.5 2.4 copy-start
  25.2 20.2 %copy-start.2 = (s32[2048,4]{0,1:T(4,128)S(1)}, s32[2048,4]{0,1:T(4,128)}, u32[]{:S(2)}) copy-start(s32[2048,4]{0,1:T(4,128)} %param.10) | copy-start | bytes 98308
  25.2 242.4 %all-to-all-start = ((bf16[256,32,512]{2,1,0:T(8,128)(2,1)}), bf16[256,32,512]{2,1,0:T(8,128)(2,1)}, u32[]{:S(2)}, u32[]{:S(2)}) async-start(bf16[256,32,512]{2,1,0:T(8,128)(2,1)} %bitcast.32), calls=%async_computation | async-start | bytes 16777216 | tf_op jit(solution)/shard_map/all_to_all | solution.py:53
  45.2 228.2 %copy-start.3 = (s32[4,12]{1,0:T(4,128)S(1)}, s32[4,12]{1,0:T(4,128)}, u32[]{:S(2)}) copy-start(s32[4,12]{1,0:T(4,128)} %param.9) | copy-start | bytes 580
  45.2 330.1 %all-gather.2.cloned.1.call-start = ((), (), s32[]{:S(2)}) async-start(), calls=%async_computation.1 | async-start | bytes 10485760 | tf_op jit(solution)/shard_map/all_gather | solution.py:55
  275.2 108.5 %copy-start.6 = (f32[4,12,128,128]{3,2,1,0:T(8,128)S(1)}, f32[4,12,128,128]{3,2,1,0:T(8,128)}, u32[]{:S(2)}) copy-start(f32[4,12,128,128]{3,2,1,0:T(8,128)} %param.8) | copy-start | bytes 9437188
  383.7 5.7 %copy-start.1 = (bf16[512,512]{1,0:T(8,128)(2,1)S(1)}, bf16[512,512]{1,0:T(8,128)(2,1)}, u32[]{:S(2)}) copy-start(bf16[512,512]{1,0:T(8,128)(2,1)} %param.11) | copy-start | bytes 1572868
  383.7 5.7 %copy-start.4 = (f32[512]{0:T(512)S(1)}, f32[512]{0:T(512)}, u32[]{:S(2)}) copy-start(f32[512]{0:T(512)} %param.12) | copy-start | bytes 6148
  383.7 5.7 %copy-start.5 = (f32[512]{0:T(512)S(1)}, f32[512]{0:T(512)}, u32[]{:S(2)}) copy-start(f32[512]{0:T(512)} %param.13) | copy-start | bytes 6148
Sparse Core Ops, SparseCore 0:
  273.4 101.8 all-gather.1
where the time goes:
time: 398 us; the launch traced here: 397 us
  waiting for transfers between devices  321 us (81%)
  local copies, waits for them, and re-layouts  27.6 us (7%)
  starting transfers between devices  20.2 us (5%)
  between operations  13.6 us (3%)
  matrix products  11.3 us (3%)
    all_to_all x1, waiting for transfers between devices, per_device(): lax.all_to_all(outgoing, 'grp', split_axis=0, concat_axis=0, tiled=True)  221 us
    all_gather x1, waiting for transfers between devices, per_device(): arrived = lax.all_gather(gathered_rows, 'blk', axis=1, tiled=True)  100 us
    all_to_all x1, starting transfers between devices, per_device(): lax.all_to_all(outgoing, 'grp', split_axis=0, concat_axis=0, tiled=True)  19.9 us
    unnamed x17, local copies, waits for them, and re-layouts  10.8 us
    gather x1, local copies, waits for them, and re-layouts, per_device(): jnp.take(arrived, flat_slots, axis=0)  8.39 us
  transfers between devices with their start and end apart: 2, of which 2 were waited for; matrix products, arithmetic and copies ran while one was open for 1% of the time, Pallas kernels for 0%

commit v1 on v0

v1 whole, which is shorter than its diff:
```python
import jax
import jax.numpy as jnp
from jax import lax
from jax.experimental import pallas as pl
from jax.experimental.pallas import tpu as pltpu
from jax.sharding import Mesh, PartitionSpec as P

GRP = ("y", "xl", "z")
BLK = ("xh", "k")
SPREAD_A = ("y", "xh", "k")
SPREAD_B = ("xl", "z")
BF = jnp.bfloat16
F32 = jnp.float32


def route_kernel(groups, slots, tiles, width):
    step = 8
    lanes = 128

    def body(own_ref, dest_ref, table_ref, out_ref, mine_ref, slot_ref):
        ids = lax.broadcasted_iota(jnp.int32, (groups, lanes), 0)
        before = lax.broadcasted_iota(jnp.int32, (lanes, lanes), 0)
        after = lax.broadcasted_iota(jnp.int32, (lanes, lanes), 1)
        tri = (before < after).astype(F32).astype(BF)
        carry = jnp.zeros((groups, 1), F32)
        for i in range(tiles // lanes):
            named = dest_ref[0:1, pl.ds(i * lanes, lanes)] == ids
            for l in range(1, dest_ref.shape[0]):
                named = named | (dest_ref[l : l + 1, pl.ds(i * lanes, lanes)] == ids)
            ones = named.astype(F32)
            earlier = jnp.dot(ones.astype(BF), tri, preferred_element_type=F32) + carry
            slot_ref[:, pl.ds(i * lanes, lanes)] = jnp.where(named, earlier, -1.0)
            carry = carry + jnp.sum(ones, axis=1, keepdims=True)
        mine_ref[...] = slot_ref[pl.ds(own_ref[0], 1), :].astype(jnp.int32)
        place = lax.broadcasted_iota(jnp.int32, (1, slots, tiles), 1).astype(F32)

        def some_groups(g, _):
            rows = slot_ref[pl.ds(g * step, step), :]
            pick = (rows[:, None, :] == place).astype(F32).astype(BF)
            pick = pick.reshape(step * slots, tiles)
            got = jnp.dot(pick, table_ref[...], preferred_element_type=F32)
            out_ref[pl.ds(g * step * slots, step * slots), :] = got.astype(BF)
            return 0

        lax.fori_loop(0, groups // step, some_groups, 0)

    def call(own, dest, table):
        return pl.pallas_call(
            body,
            grid_spec=pltpu.PrefetchScalarGridSpec(
                num_scalar_prefetch=1,
                grid=(1,),
                in_specs=[
                    pl.BlockSpec(dest.shape, lambda i, s: (0, 0)),
                    pl.BlockSpec(table.shape, lambda i, s: (0, 0)),
                ],
                out_specs=[
                    pl.BlockSpec((groups * slots, width), lambda i, s: (0, 0)),
                    pl.BlockSpec((1, tiles), lambda i, s: (0, 0)),
                ],
                scratch_shapes=[pltpu.VMEM((groups, tiles), F32)],
            ),
            out_shape=[
                jax.ShapeDtypeStruct((groups * slots, width), BF),
                jax.ShapeDtypeStruct((1, tiles), jnp.int32),
            ],
            compiler_params=pltpu.CompilerParams(vmem_limit_bytes=48 * 1024 * 1024),
            name="route",
        )(own, dest, table)

    return call


def ladder_call(slot, weights, tiles):
    columns, listed, depth, size = weights.shape
    held, _, width = tiles.shape

    def body(slot_ref, w_ref, t_ref, out_ref):
        n = pl.program_id(0)
        his, los, ts = [], [], []
        for r in range(listed):
            s = slot_ref[n * listed + r]
            w = jnp.where(s >= 0, w_ref[0, r], 0.0)
            hi = w.astype(BF)
            his.append(hi)
            los.append((w - hi.astype(F32)).astype(BF))
            ts.append(t_ref[jnp.maximum(s, 0)])
        hi = jnp.concatenate(his, axis=0)
        lo = jnp.concatenate(los, axis=0)
        t = jnp.concatenate(ts, axis=0)
        both = jnp.concatenate([hi, lo], axis=1)
        acc = lax.dot_general(both, t, (((0,), (0,)), ((), ())), preferred_element_type=F32)
        out_ref[0] = acc[:size] + acc[size:]

    return pl.pallas_call(
        body,
        grid_spec=pltpu.PrefetchScalarGridSpec(
            num_scalar_prefetch=1,
            grid=(columns,),
            in_specs=[
                pl.BlockSpec((1, listed, depth, size), lambda n, s: (n, 0, 0, 0)),
                pl.BlockSpec((held, depth, width), lambda n, s: (0, 0, 0)),
            ],
            out_specs=pl.BlockSpec((1, size, width), lambda n, s: (n, 0, 0)),
        ),
        out_shape=jax.ShapeDtypeStruct((columns, size, width), F32),
        compiler_params=pltpu.CompilerParams(vmem_limit_bytes=48 * 1024 * 1024),
        name="ladder",
    )(slot, weights, tiles)


def per_device(amplitudes, integrals, tile_rows, destinations, source_terms, occ_energy, virt_energy):
    ny, nx, nz = (lax.axis_size(a) for a in GRP)
    nblk = lax.axis_size("xh") * lax.axis_size("k")
    groups = ny * nx * nz
    own = lax.axis_index(GRP).astype(jnp.int32)
    owned, rows, full_width = amplitudes.shape
    all_tiles, dest = destinations.shape
    width = full_width // nblk
    nc = nx * nz
    sub = rows // ny
    depth = rows * nblk
    slots = all_tiles * dest // groups
    columns, listed, _, size = integrals.shape

    weights = lax.all_gather(integrals, BLK, axis=0, tiled=True)
    named_tiles = lax.all_gather(tile_rows, BLK, axis=0, tiled=True)

    x = amplitudes.reshape(owned, ny, sub, nblk, width).transpose(1, 3, 2, 0, 4)
    x = x.reshape(ny * nblk, sub, owned, width)
    x = lax.all_to_all(x, SPREAD_A, 0, 0, tiled=True)
    x = x.reshape(ny, nblk * sub, owned, width).transpose(1, 0, 2, 3)
    x = lax.all_to_all(x, SPREAD_B, 0, 0, tiled=True)
    table = x.reshape(nc * ny * owned, width)

    dest_t = destinations.reshape(ny, nc, owned, dest).transpose(3, 1, 0, 2).reshape(dest, all_tiles)
    outgoing, mine = route_kernel(groups, slots, all_tiles, width)(own.reshape(1), dest_t, table)
    incoming = lax.all_to_all(outgoing.reshape(groups, slots, width), GRP, 0, 0, tiled=True)

    tiles = incoming.reshape(ny, nblk, sub, slots, width).transpose(3, 1, 0, 2, 4)
    tiles = tiles.reshape(slots, depth, width)

    y_of = named_tiles // (nc * owned)
    c_of = (named_tiles // owned) % nc
    at = c_of * (ny * owned) + y_of * owned + named_tiles % owned
    where = jnp.arange(all_tiles, dtype=jnp.int32)
    slot = jnp.max(jnp.where(at[:, :, None] == where, mine.reshape(1, 1, all_tiles), -1), axis=2)

    ladder = ladder_call(slot.reshape(-1), weights, tiles)
    ladder = ladder.reshape(nblk, columns * size, width)
    ladder = lax.all_to_all(ladder, BLK, 0, 0, tiled=True)
    ladder = ladder.transpose(1, 0, 2).reshape(columns * size, full_width)
    denominator = virt_energy[:, None] + occ_energy[None, :]
    return ((source_terms.astype(F32) + ladder) / denominator).astype(BF)


def solution(mesh):
    n_grp = mesh.shape["grp"]
    fine = Mesh(mesh.devices.reshape(8, 2, n_grp // 16, 2, 2), GRP + BLK)
    ALL = GRP + BLK
    in_specs = (
        P(GRP, BLK, None),
        P(ALL, None, None, None),
        P(ALL, None),
        P(),
        P(ALL, None),
        P(),
        P(ALL),
    )
    return jax.shard_map(
        per_device, mesh=fine, in_specs=in_specs, out_specs=P(ALL, None), check_vma=False
    )
```

time: 398 us -> 183 us (0.46)
  waiting for transfers between devices: 321 us -> 54 us
  blocking collectives: 0 us -> 56.9 us
  Pallas kernels: 0 us -> 27.1 us
  local copies, waits for them, and re-layouts: 27.6 us -> 5.49 us
  matrix products: 11.3 us -> 0 us
    all_to_all x1 -> x2, waiting for transfers between devices: 221 us -> 53.3 us  [the longest x1 40.8 us: per_device(): lax.all_to_all(outgoing.reshape(groups, slots, width), GRP, 0, 0, tiled=T...]
    all_gather x1, waiting for transfers between devices: 100 us -> 0.02 us  [per_device(): weights = lax.all_gather(integrals, BLK, axis=0, tiled=True)]
    all_to_all x0 -> x2, blocking collectives: none -> 49.1 us  [the longest x1 27.9 us: per_device(): x = lax.all_to_all(x, SPREAD_A, 0, 0, tiled=True)]
    pallas_call x0 -> x2, Pallas kernels: none -> 27.1 us  [the longest x1 13.7 us: ladder_call(): pl.pallas_call(body, grid_spec=pltpu.PrefetchScalarGridSpec(num_scalar_pr...]
    gather x9 -> x0, local copies, waits for them, and re-layouts: 15.1 us -> none  [the longest x1 8.39 us: per_device(): jnp.take(arrived, flat_slots, axis=0)]
    dot_general x2 -> x0, matrix products: 11.3 us -> none  [the longest x1 5.71 us: per_device(): jnp.einsum('crqk,crqp->ckp', weights, picked, precision=lax.Precision.HIG...]
    unnamed x17 -> x12, local copies, waits for them, and re-layouts: 10.8 us -> 0.35 us
    all_gather x0 -> x1, blocking collectives: none -> 7.86 us  [per_device(): named_tiles = lax.all_gather(tile_rows, BLK, axis=0, tiled=True)]
  transfers between devices with their start and end apart: 2 -> 3, of which waited for: 2 -> 2; matrix products, arithmetic and copies ran while one was open for 1% -> 3% of each run, Pallas kernels for 0% -> 7%
where the time goes in v1:
time: 183 us; the launch traced here: 182 us
  blocking collectives  56.9 us (31%)
  waiting for transfers between devices  54 us (30%)
  Pallas kernels  27.1 us (15%)
  starting transfers between devices  23.5 us (13%)
  between operations  13.5 us (7%)
  local copies, waits for them, and re-layouts  5.49 us (3%)
    all_to_all x1, waiting for transfers between devices, per_device(): lax.all_to_all(outgoing.reshape(groups, slots, width), GRP, 0, 0, tiled=T...  40.8 us
    all_to_all x1, blocking collectives, per_device(): x = lax.all_to_all(x, SPREAD_A, 0, 0, tiled=True)  27.9 us
    all_to_all x1, blocking collectives, per_device(): ladder = lax.all_to_all(ladder, BLK, 0, 0, tiled=True)  21.2 us
    pallas_call x1, Pallas kernels, ladder_call(): pl.pallas_call(body, grid_spec=pltpu.PrefetchScalarGridSpec(num_scalar_pr...  13.7 us
    pallas_call x1, Pallas kernels, call(): pl.pallas_call(body, grid_spec=pltpu.PrefetchScalarGridSpec(num_scalar_pr...  13.3 us
    all_to_all x1, starting transfers between devices, per_device(): lax.all_to_all(outgoing.reshape(groups, slots, width), GRP, 0, 0, tiled=T...  13.3 us
    all_to_all x1, waiting for transfers between devices, per_device(): x = lax.all_to_all(x, SPREAD_B, 0, 0, tiled=True)  12.5 us
    all_to_all x1, starting transfers between devices, per_device(): x = lax.all_to_all(x, SPREAD_B, 0, 0, tiled=True)  10.2 us
  transfers between devices with their start and end apart: 3, of which 2 were waited for; matrix products, arithmetic and copies ran while one was open for 3% of the time, Pallas kernels for 7%

profile of v1, /device:TPU:1, one launch (start us, length us, event | category | flops | bytes accessed | tf_op | source)
XLA Modules:
  0.0 182.1 jit_solution(12638321440528145157)
XLA Ops:
  6.5 0.0 copy-start
  6.5 0.0 all-gather.3.cloned.1.call-start
  6.5 0.7 all-gather.3.cloned.1.call-update
  7.3 0.3 copy-done
  7.6 0.1 reshape.47
  7.7 0.0 copy-start.2
  7.7 0.3 copy.32
  8.1 27.9 %all_to_all.20 = bf16[32,4,16,128]{3,2,1,0:T(8,128)(2,1)S(1)} all-to-all(bf16[32,4,16,128]{3,2,1,0:T(8,128)(2,1)S(1)} %bitcast.37), channel_id=1, replica_groups=mesh['y'=8,'xl'=2,'z'=8,'xh'=2,'k'=2] {'y','xh','k'}, dimensions={0} | all-to-all | bytes 1048576 | tf_op jit(solution)/shard_map/all_to_all | solution.py:131
  35.9 0.8 copy.33
  36.8 10.2 %all-to-all-start.1 = ((bf16[16,8,16,128]{3,2,1,0:T(8,128)(2,1)}), bf16[16,8,16,128]{3,2,1,0:T(8,128)(2,1)S(1)}, u32[]{:S(2)}, u32[]{:S(2)}) async-start(bf16[16,8,16,128]{3,2,1,0:T(8,128)(2,1)} %copy.33), calls=%async_computation.1 | async-start | bytes 1048576 | tf_op jit(solution)/shard_map/all_to_all | solution.py:133
  47.0 0.0 copy-done.2
  47.0 0.1 reshape.45
  47.1 0.1 copy.40
  47.2 0.2 reshape.46.dest_ref
  47.4 12.5 %all-to-all-done.1 = bf16[16,8,16,128]{3,2,1,0:T(8,128)(2,1)S(1)} async-done(((bf16[16,8,16,128]{3,2,1,0:T(8,128)(2,1)}), bf16[16,8,16,128]{3,2,1,0:T(8,128)(2,1)S(1)}, u32[]{:S(2)}, u32[]{:S(2)}) %all-to-all-start.1) | async-done | bytes 524320 | tf_op jit(solution)/shard_map/all_to_all | solution.py:133
  59.9 13.3 %route.1 = (bf16[8192,128]{1,0:T(8,128)(2,1)}, s32[1,2048]{1,0:T(1,128)S(1)}) custom-call(s32[1]{0:T(128)} %bitcast.2.own_ref, s32[4,2048]{1,0:T(4,128)S(1)} %reshape.46.dest_ref, bf16[2048,128]{1,0:T(8,128)(2,1)S(1)} %bitcast.35), custom_call_target="tpu_custom_call" | custom-call | tf_op jit(solution)/shard_map/route/pallas_call | solution.py:48
  73.2 0.0 copy-start.3
  73.2 13.3 %all-to-all-start.2 = ((bf16[128,64,128]{2,1,0:T(8,128)(2,1)}), bf16[128,64,128]{2,1,0:T(8,128)(2,1)}, u32[]{:S(2)}, u32[]{:S(2)}) async-start(bf16[128,64,128]{2,1,0:T(8,128)(2,1)} %bitcast.10), calls=%async_computation.2 | async-start | bytes 4194304 | tf_op jit(solution)/shard_map/all_to_all | solution.py:138
  86.6 0.0 copy-done.3
  86.6 7.9 %all-gather = s32[4,4,12]{2,1,0:T(4,128)S(1)} all-gather(s32[1,4,12]{2,1,0:T(4,128)S(1)} %bitcast.42), channel_id=1, replica_groups=mesh['y'=8,'xl'=2,'z'=8,'xh'=2,'k'=2] {'xh','k'}, dimensions={0}, use_global_device_ids=true | all-gather | bytes 960 | tf_op jit(solution)/shard_map/all_gather | solution.py:127
  94.5 0.1 copy.30
  94.6 0.4 select_reduce_fusion
  95.0 0.1 copy.34
  95.1 0.1 reshape.51.slot_ref
  95.2 40.8 %all-to-all-done.2 = bf16[128,64,128]{2,1,0:T(8,128)(2,1)} async-done(((bf16[128,64,128]{2,1,0:T(8,128)(2,1)}), bf16[128,64,128]{2,1,0:T(8,128)(2,1)}, u32[]{:S(2)}, u32[]{:S(2)}) %all-to-all-start.2) | async-done | bytes 2097184 | tf_op jit(solution)/shard_map/all_to_all | solution.py:138
  135.9 3.2 %copy.35 = bf16[64,4,8,4,128]{4,3,2,1,0:T(4,128)(2,1)S(1)} copy(bf16[64,4,8,4,128]{4,0,3,1,2:T(8,128)(2,1)} %bitcast.12) | data formatting | bytes 4194304 | tf_op jit(solution)/shard_map/transpose | solution.py:140
  139.1 0.0 all-gather.3.cloned.1.call-done.w_ref
  139.2 13.7 %ladder.1 = f32[16,128,128]{2,1,0:T(8,128)S(1)} custom-call(s32[192]{0:T(256)S(1)} %reshape.51.slot_ref, f32[16,12,128,128]{3,2,1,0:T(8,128)} %all-gather.3.cloned.1.call-done.w_ref, bf16[64,128,128]{2,1,0:T(8,128)(2,1)S(1)} %bitcast.33), custom_call_target="tpu_custom_call" | custom-call | tf_op jit(solution)/shard_map/ladder/pallas_call | solution.py:95
  152.9 0.0 copy-start.1
  152.9 0.0 copy-start.4
  152.9 0.0 copy-start.5
  153.0 21.2 %all_to_all.21 = f32[4,512,128]{2,1,0:T(8,128)S(1)} all-to-all(f32[4,512,128]{2,1,0:T(8,128)S(1)} %bitcast.34), channel_id=1, replica_groups=mesh['y'=8,'xl'=2,'z'=8,'xh'=2,'k'=2] {'xh','k'}, dimensions={0} | all-to-all | bytes 2097152 | tf_op jit(solution)/shard_map/all_to_all | solution.py:151
  174.2 0.0 copy-done.1
  174.2 0.0 copy-done.4
  174.2 0.0 copy-done.5
  174.2 1.0 fusion.1
  (1 shorter events, 0.0 us)
Async XLA Ops:
  6.5 1.0 copy-start
  6.5 132.6 %all-gather.3.cloned.1.call-start = ((), (), s32[]{:S(2)}) async-start(), calls=%async_computation.4 | async-start | bytes 15728640 | tf_op jit(solution)/shard_map/all_gather | solution.py:126
  7.7 39.3 %copy-start.2 = (s32[2048,4]{0,1:T(4,128)S(1)}, s32[2048,4]{0,1:T(4,128)}, u32[]{:S(2)}) copy-start(s32[2048,4]{0,1:T(4,128)} %param.10) | copy-start | bytes 98308
  36.8 23.1 %all-to-all-start.1 = ((bf16[16,8,16,128]{3,2,1,0:T(8,128)(2,1)}), bf16[16,8,16,128]{3,2,1,0:T(8,128)(2,1)S(1)}, u32[]{:S(2)}, u32[]{:S(2)}) async-start(bf16[16,8,16,128]{3,2,1,0:T(8,128)(2,1)} %copy.33), calls=%async_computation.1 | async-start | bytes 1048576 | tf_op jit(solution)/shard_map/all_to_all | solution.py:133
  73.2 13.3 %copy-start.3 = (s32[4,12]{1,0:T(4,128)S(1)}, s32[4,12]{1,0:T(4,128)}, u32[]{:S(2)}) copy-start(s32[4,12]{1,0:T(4,128)} %param.9) | copy-start | bytes 580
  73.2 62.7 %all-to-all-start.2 = ((bf16[128,64,128]{2,1,0:T(8,128)(2,1)}), bf16[128,64,128]{2,1,0:T(8,128)(2,1)}, u32[]{:S(2)}, u32[]{:S(2)}) async-start(bf16[128,64,128]{2,1,0:T(8,128)(2,1)} %bitcast.10), calls=%async_computation.2 | async-start | bytes 4194304 | tf_op jit(solution)/shard_map/all_to_all | solution.py:138
  152.9 21.3 %copy-start.1 = (bf16[512,512]{1,0:T(8,128)(2,1)S(1)}, bf16[512,512]{1,0:T(8,128)(2,1)}, u32[]{:S(2)}) copy-start(bf16[512,512]{1,0:T(8,128)(2,1)} %param.11) | copy-start | bytes 1572868
  152.9 21.3 %copy-start.4 = (f32[512]{0:T(512)S(1)}, f32[512]{0:T(512)}, u32[]{:S(2)}) copy-start(f32[512]{0:T(512)} %param.12) | copy-start | bytes 6148
  152.9 21.2 %copy-start.5 = (f32[512]{0:T(512)S(1)}, f32[512]{0:T(512)}, u32[]{:S(2)}) copy-start(f32[512]{0:T(512)} %param.13) | copy-start | bytes 6148
Sparse Core Ops, SparseCore 0:
  9.4 122.9 all-gather.2

commit v2 on v1

v2 whole, which is shorter than its diff:
```python
import jax
import jax.numpy as jnp
from jax import lax
from jax.experimental import pallas as pl
from jax.experimental.pallas import tpu as pltpu
from jax.sharding import Mesh, PartitionSpec as P

GRP = ("y", "xl", "z")
BLK = ("xh", "k")
LINE = ("xl", "xh", "k")
PLANE = ("y", "z")
BF = jnp.bfloat16
F32 = jnp.float32
PARAMS = pltpu.CompilerParams(vmem_limit_bytes=48 * 1024 * 1024)


def rank_call(own, dest, groups):
    named_by, tiles = dest.shape
    lanes = 128
    half = tiles // 2 // lanes

    def body(own_ref, dest_ref, slot_ref, early_ref, mine_ref):
        ids = lax.broadcasted_iota(jnp.int32, (groups, lanes), 0)
        before = lax.broadcasted_iota(jnp.int32, (lanes, lanes), 0)
        after = lax.broadcasted_iota(jnp.int32, (lanes, lanes), 1)
        tri = (before < after).astype(F32).astype(BF)
        carry = jnp.zeros((groups, 1), F32)
        for i in range(tiles // lanes):
            if i == half:
                early_ref[...] = jnp.broadcast_to(carry, (groups, lanes))
            named = dest_ref[0:1, pl.ds(i * lanes, lanes)] == ids
            for l in range(1, named_by):
                named = named | (dest_ref[l : l + 1, pl.ds(i * lanes, lanes)] == ids)
            ones = named.astype(F32)
            earlier = jnp.dot(ones.astype(BF), tri, preferred_element_type=F32) + carry
            slot_ref[:, pl.ds(i * lanes, lanes)] = jnp.where(named, earlier, -1.0)
            carry = carry + jnp.sum(ones, axis=1, keepdims=True)
        mine_ref[...] = slot_ref[pl.ds(own_ref[0], 1), :].astype(jnp.int32)

    return pl.pallas_call(
        body,
        grid_spec=pltpu.PrefetchScalarGridSpec(
            num_scalar_prefetch=1,
            grid=(1,),
            in_specs=[pl.BlockSpec(dest.shape, lambda i, s: (0, 0))],
            out_specs=[
                pl.BlockSpec((groups, tiles), lambda i, s: (0, 0)),
                pl.BlockSpec((groups, lanes), lambda i, s: (0, 0)),
                pl.BlockSpec((1, tiles), lambda i, s: (0, 0)),
            ],
        ),
        out_shape=[
            jax.ShapeDtypeStruct((groups, tiles), F32),
            jax.ShapeDtypeStruct((groups, lanes), F32),
            jax.ShapeDtypeStruct((1, tiles), jnp.int32),
        ],
        compiler_params=PARAMS,
        name="rank",
    )(own, dest)


def route_call(slot, early, table, slots):
    groups, tiles = slot.shape
    width = table.shape[1]
    half = tiles // 2
    step = 32
    deep = 16

    def body(slot_ref, early_ref, table_ref, out_ref):
        one = jnp.asarray(1, BF)
        zero = jnp.asarray(0, BF)
        place = lax.broadcasted_iota(jnp.int32, (deep, half), 0)
        places = [(place + deep * q).astype(F32).astype(BF) for q in range(slots // deep)]
        rows = slot_ref[...]
        parts = []
        for d in range(step):
            lo = jnp.broadcast_to(rows[d : d + 1, :half], (deep, half)).astype(BF)
            hi = jnp.broadcast_to(rows[d : d + 1, half:], (deep, half)).astype(BF)
            for at in places:
                parts.append(jnp.where((lo == at) | (hi == at), one, zero))
        pick = jnp.concatenate(parts, axis=0)
        both = jnp.concatenate([table_ref[:half, :], table_ref[half:, :]], axis=1)
        got = jnp.dot(pick, both, preferred_element_type=F32)
        j = lax.broadcasted_iota(jnp.int32, (slots, width), 0).astype(F32)
        for d in range(step):
            late = j >= early_ref[d : d + 1, :]
            g = got[d * slots : (d + 1) * slots]
            out_ref[d * slots : (d + 1) * slots, :] = jnp.where(late, g[:, width:], g[:, :width]).astype(BF)

    return pl.pallas_call(
        body,
        grid=(groups // step,),
        in_specs=[
            pl.BlockSpec((step, tiles), lambda i: (i, 0)),
            pl.BlockSpec((step, width), lambda i: (i, 0)),
            pl.BlockSpec((tiles, width), lambda i: (0, 0)),
        ],
        out_specs=pl.BlockSpec((step * slots, width), lambda i: (i, 0)),
        out_shape=jax.ShapeDtypeStruct((groups * slots, width), BF),
        compiler_params=PARAMS,
        name="route",
    )(slot, early, table)


def turn_call(tiles):
    slots, depth, width = tiles.shape
    step = 8

    def body(t_ref, out_ref):
        for i in range(step):
            out_ref[i] = t_ref[i].T

    return pl.pallas_call(
        body,
        grid=(slots // step,),
        in_specs=[pl.BlockSpec((step, depth, width), lambda i: (i, 0, 0))],
        out_specs=pl.BlockSpec((step, width, depth), lambda i: (i, 0, 0)),
        out_shape=jax.ShapeDtypeStruct((slots, width, depth), BF),
        compiler_params=PARAMS,
        name="turn",
    )(tiles)


def ladder_call(slot, base, weights, turned):
    columns, listed, depth, size = weights.shape
    width = turned.shape[1]

    def body(slot_ref, base_ref, w_ref, t_ref, out_ref):
        for n in range(columns):
            right, left = [], []
            for r in range(listed):
                s = slot_ref[base_ref[0] + n * listed + r]
                w = w_ref[n, r]
                hi = w.astype(BF)
                lo = (w - hi.astype(F32)).astype(BF)
                right.append(jnp.concatenate([hi, lo], axis=1))
                t = t_ref[jnp.maximum(s, 0)]
                left.append(jnp.where(s >= 0, t, jnp.zeros_like(t)))
            right = jnp.concatenate(right, axis=0)
            left = jnp.concatenate(left, axis=1)
            acc = jnp.dot(left, right, preferred_element_type=F32)
            out_ref[n * size : (n + 1) * size, :] = (acc[:, :size] + acc[:, size:]).T

    return pl.pallas_call(
        body,
        grid_spec=pltpu.PrefetchScalarGridSpec(
            num_scalar_prefetch=2,
            grid=(1,),
            in_specs=[
                pl.BlockSpec(weights.shape, lambda i, s, b: (0, 0, 0, 0)),
                pl.BlockSpec(turned.shape, lambda i, s, b: (0, 0, 0)),
            ],
            out_specs=pl.BlockSpec((columns * size, width), lambda i, s, b: (0, 0)),
        ),
        out_shape=jax.ShapeDtypeStruct((columns * size, width), F32),
        compiler_params=PARAMS,
        name="ladder",
    )(slot, base, weights, turned)


def finish_call(blk, pieces, source, occ, virt):
    rows, width = pieces[0].shape
    count = len(pieces)
    tall, size = virt.shape

    def body(blk_ref, *refs):
        piece_refs = refs[:count]
        s_ref, o_ref, v_ref, out_ref = refs[count:]
        i = pl.program_id(0)
        for j in range(count):

            @pl.when(i == j)
            def _(j=j):
                for n in range(tall):
                    at = slice(n * size, (n + 1) * size)
                    v = jnp.broadcast_to(v_ref[n : n + 1, :], (size, size)).T
                    total = s_ref[at, :].astype(F32) + piece_refs[j][at, :]
                    out_ref[at, :] = (total / (v + o_ref[...])).astype(BF)

    whole = pl.BlockSpec((rows, width), lambda i, b: (0, 0))
    part = pl.BlockSpec((rows, width), lambda i, b: (0, b[0] ^ i))
    return pl.pallas_call(
        body,
        grid_spec=pltpu.PrefetchScalarGridSpec(
            num_scalar_prefetch=1,
            grid=(count,),
            in_specs=[whole] * count
            + [part, pl.BlockSpec((1, width), lambda i, b: (0, b[0] ^ i)), pl.BlockSpec(virt.shape, lambda i, b: (0, 0))],
            out_specs=part,
        ),
        out_shape=jax.ShapeDtypeStruct(source.shape, BF),
        compiler_params=PARAMS,
        name="finish",
    )(blk, *pieces, source, occ, virt)


def swap(x, flip, n):
    return lax.ppermute(x, BLK, [(b, b ^ flip) for b in range(n)])


def per_device(amplitudes, integrals, tile_rows, destinations, source_terms, occ_energy, virt_energy):
    ny, nx, nz = (lax.axis_size(a) for a in GRP)
    nblk = lax.axis_size("xh") * lax.axis_size("k")
    groups = ny * nx * nz
    own = lax.axis_index(GRP).astype(jnp.int32)
    blk = lax.axis_index(BLK).astype(jnp.int32)
    owned, rows, full_width = amplitudes.shape
    all_tiles, dest = destinations.shape
    width = full_width // nblk
    sub = rows // nx
    slots = all_tiles * dest // groups
    columns, listed, _, size = integrals.shape

    x = amplitudes.reshape(owned, nx, sub, nblk, width).transpose(1, 3, 2, 0, 4)
    x = lax.all_to_all(x.reshape(nx * nblk, sub, owned, width), LINE, 0, 0, tiled=True)
    held, x = lax.optimization_barrier((integrals, x))
    across = swap(held, 2, nblk)
    x = x.reshape(nx, nblk, sub, owned, width).transpose(1, 2, 0, 3, 4)
    x = lax.all_to_all(x.reshape(ny * nz, nx * owned, width), PLANE, 0, 0, tiled=True)
    table = x.reshape(all_tiles, width)

    dest_t = destinations.reshape(ny, nx, nz, owned, dest).transpose(4, 0, 2, 1, 3)
    slot_of, early, mine = rank_call(own.reshape(1), dest_t.reshape(dest, all_tiles), groups)
    outgoing = route_call(slot_of, early, table, slots)
    incoming = lax.all_to_all(outgoing.reshape(groups, slots, width), GRP, 0, 0, tiled=True)

    beside = swap(held, 1, nblk)
    named_tiles = lax.all_gather(tile_rows, BLK, axis=0, tiled=True)
    y_of = named_tiles // (nx * nz * owned)
    x_of = (named_tiles // (nz * owned)) % nx
    z_of = (named_tiles // owned) % nz
    at = ((y_of * nz + z_of) * nx + x_of) * owned + named_tiles % owned
    where = jnp.arange(all_tiles, dtype=jnp.int32)
    slot = jnp.max(jnp.where(at[:, :, None] == where, mine.reshape(1, 1, all_tiles), -1), axis=2)
    slot = slot.reshape(-1)
    diagonal = swap(across, 1, nblk)

    tiles = incoming.reshape(nblk, ny // nblk, nx, nz, slots, width).transpose(4, 0, 2, 1, 3, 5)
    turned = turn_call(tiles.reshape(slots, rows * nblk, width))

    def partial(flip, weights):
        base = (blk ^ flip) * (columns * listed)
        return ladder_call(slot, base.reshape(1), weights, turned)

    far = swap(partial(2, across), 2, nblk)
    farther = swap(partial(3, diagonal), 3, nblk)
    near = swap(partial(1, beside), 1, nblk)
    home = partial(0, integrals)
    return finish_call(
        blk.reshape(1),
        (home, near, far, farther),
        source_terms,
        occ_energy.reshape(1, full_width),
        virt_energy.reshape(columns, size),
    )


def solution(mesh):
    n_grp = mesh.shape["grp"]
    fine = Mesh(mesh.devices.reshape(8, 2, n_grp // 16, 2, 2), GRP + BLK)
    every = GRP + BLK
    in_specs = (
        P(GRP, BLK, None),
        P(every, None, None, None),
        P(every, None),
        P(),
        P(every, None),
        P(),
        P(every),
    )
    return jax.shard_map(
        per_device, mesh=fine, in_specs=in_specs, out_specs=P(every, None), check_vma=False
    )
```

time: 183 us -> 157 us (0.86)
  blocking collectives: 56.9 us -> 25 us
  starting transfers between devices: 23.5 us -> 43.1 us
  between operations: 13.5 us -> 0.27 us
  waiting for transfers between devices: 54 us -> 58.9 us
  Pallas kernels: 27.1 us -> 22.8 us
    ppermute x0 -> x6, waiting for transfers between devices: none -> 44.2 us  [swap(): return lax.ppermute(x, BLK, [(b, b ^ flip) for b in range(n)])]
    all_to_all x1, waiting for transfers between devices: 40.8 us -> 0.01 us  [per_device(): lax.all_to_all(outgoing.reshape(groups, slots, width), GRP, 0, 0, tiled=T...]
    all_to_all x2 -> x1, blocking collectives: 49.1 us -> 18.4 us  [per_device(): lax.all_to_all(x.reshape(nx * nblk, sub, owned, width), LINE, 0, 0, tiled...]
    ppermute x0 -> x6, starting transfers between devices: none -> 20.7 us  [swap(): return lax.ppermute(x, BLK, [(b, b ^ flip) for b in range(n)])]
    pallas_call x1 -> x4, Pallas kernels: 13.3 us -> 9.53 us  [the longest x1 5.88 us: route_call(): pl.pallas_call(body, grid=(groups // step,), in_specs=[pl.BlockSpec((step...]
    all_to_all x1, starting transfers between devices: 13.3 us -> 9.74 us  [per_device(): lax.all_to_all(outgoing.reshape(groups, slots, width), GRP, 0, 0, tiled=T...]
    all_to_all x1, starting transfers between devices: 10.2 us -> 12.6 us  [per_device(): lax.all_to_all(x.reshape(ny * nz, nx * owned, width), PLANE, 0, 0, tiled=...]
    all_to_all x1, waiting for transfers between devices: 12.5 us -> 14.7 us  [per_device(): lax.all_to_all(x.reshape(ny * nz, nx * owned, width), PLANE, 0, 0, tiled=...]
  transfers between devices with their start and end apart: 3 -> 8, of which waited for: 2 -> 3; matrix products, arithmetic and copies ran while one was open for 3% -> 3% of each run, Pallas kernels for 7% -> 13%
where the time goes in v2:
time: 157 us
  waiting for transfers between devices  58.9 us (38%)
  starting transfers between devices  43.1 us (27%)
  blocking collectives  25 us (16%)
  Pallas kernels  22.8 us (15%)
  local copies, waits for them, and re-layouts  6.18 us (4%)
    ppermute x6, waiting for transfers between devices, swap(): return lax.ppermute(x, BLK, [(b, b ^ flip) for b in range(n)])  44.2 us
    ppermute x6, starting transfers between devices, swap(): return lax.ppermute(x, BLK, [(b, b ^ flip) for b in range(n)])  20.7 us
    all_to_all x1, blocking collectives, per_device(): lax.all_to_all(x.reshape(nx * nblk, sub, owned, width), LINE, 0, 0, tiled...  18.4 us
    all_to_all x1, waiting for transfers between devices, per_device(): lax.all_to_all(x.reshape(ny * nz, nx * owned, width), PLANE, 0, 0, tiled=...  14.7 us
    pallas_call x4, Pallas kernels, ladder_call(): pl.pallas_call(body, grid_spec=pltpu.PrefetchScalarGridSpec(num_scalar_pr...  13.3 us
    all_to_all x1, starting transfers between devices, per_device(): lax.all_to_all(x.reshape(ny * nz, nx * owned, width), PLANE, 0, 0, tiled=...  12.6 us
    all_to_all x1, starting transfers between devices, per_device(): lax.all_to_all(outgoing.reshape(groups, slots, width), GRP, 0, 0, tiled=T...  9.74 us
    all_gather x1, blocking collectives, per_device(): named_tiles = lax.all_gather(tile_rows, BLK, axis=0, tiled=True)  6.65 us
  transfers between devices with their start and end apart: 8, of which 3 were waited for; matrix products, arithmetic and copies ran while one was open for 3% of the time, Pallas kernels for 13%

profile of v2, /device:TPU:1, one launch (start us, length us, event | category | flops | bytes accessed | tf_op | source)
XLA Modules:
  0.0 156.7 jit_solution(15497116642651624644)
XLA Ops:
  0.0 1.2 reshape.66
  1.2 0.0 copy-start.3
  1.2 0.3 copy.27
  1.5 18.4 %all_to_all.15 = bf16[8,16,16,128]{3,2,1,0:T(8,128)(2,1)S(1)} all-to-all(bf16[8,16,16,128]{3,2,1,0:T(8,128)(2,1)S(1)} %bitcast.34), channel_id=1, replica_groups=mesh['y'=8,'xl'=2,'z'=8,'xh'=2,'k'=2] {'xl','xh','k'}, dimensions={0} | all-to-all | bytes 1048576 | tf_op jit(solution)/shard_map/all_to_all | solution.py:215
  19.9 3.0 %collective-permute-start.2 = (f32[4,12,128,128]{3,2,1,0:T(8,128)}, f32[4,12,128,128]{3,2,1,0:T(8,128)}, u32[]{:S(2)}, u32[]{:S(2)}) collective-permute-start(f32[4,12,128,128]{3,2,1,0:T(8,128)} %w_ref.1), channel_id=1, source_target_pairs={{0,2},{1,3},{2,0},{3,1},{4,6},{5,7},{6,4},{7,5},{8,10},{9,11},{10,... | collective-permute-start | bytes 9437192 | tf_op jit(solution)/shard_map/ppermute | solution.py:198
  22.9 0.8 copy.28
  23.8 12.6 %all-to-all-start.1 = ((bf16[64,32,128]{2,1,0:T(8,128)(2,1)}), bf16[64,32,128]{2,1,0:T(8,128)(2,1)S(1)}, u32[]{:S(2)}, u32[]{:S(2)}) async-start(bf16[64,32,128]{2,1,0:T(8,128)(2,1)} %bitcast.11), calls=%async_computation.1 | async-start | bytes 1048576 | tf_op jit(solution)/shard_map/all_to_all | solution.py:219
  36.4 0.0 copy-done.3
  36.5 0.1 reshape.62
  36.6 0.1 copy.31
  36.7 0.3 reshape.63.dest_ref
  37.1 0.7 rank.1
  37.7 14.7 %all-to-all-done.1 = bf16[64,32,128]{2,1,0:T(8,128)(2,1)S(1)} async-done(((bf16[64,32,128]{2,1,0:T(8,128)(2,1)}), bf16[64,32,128]{2,1,0:T(8,128)(2,1)S(1)}, u32[]{:S(2)}, u32[]{:S(2)}) %all-to-all-start.1) | async-done | bytes 524320 | tf_op jit(solution)/shard_map/all_to_all | solution.py:219
  52.5 5.9 %route.1 = bf16[8192,128]{1,0:T(8,128)(2,1)} custom-call(f32[128,2048]{1,0:T(8,128)S(1)} %get-tuple-element.11.slot_ref, f32[128,128]{1,0:T(8,128)S(1)} %get-tuple-element.12.early_ref, bf16[2048,128]{1,0:T(8,128)(2,1)S(1)} %bitcast.29), custom_call_target="tpu_custom_call" | custom-call | tf_op jit(solution)/shard_map/route/pallas_call | solution.py:90
  58.3 0.0 copy-start.4
  58.3 9.7 %all-to-all-start.2 = ((bf16[128,64,128]{2,1,0:T(8,128)(2,1)}), bf16[128,64,128]{2,1,0:T(8,128)(2,1)}, u32[]{:S(2)}, u32[]{:S(2)}) async-start(bf16[128,64,128]{2,1,0:T(8,128)(2,1)} %bitcast.13), calls=%async_computation.2 | async-start | bytes 4194304 | tf_op jit(solution)/shard_map/all_to_all | solution.py:225
  68.1 3.8 %collective-permute-start = (f32[4,12,128,128]{3,2,1,0:T(8,128)}, f32[4,12,128,128]{3,2,1,0:T(8,128)}, u32[]{:S(2)}, u32[]{:S(2)}) collective-permute-start(f32[4,12,128,128]{3,2,1,0:T(8,128)} %w_ref.1), channel_id=1, source_target_pairs={{0,1},{1,0},{2,3},{3,2},{4,5},{5,4},{6,7},{7,6},{8,9},{9,8},{10,11... | collective-permute-start | bytes 9437192 | tf_op jit(solution)/shard_map/ppermute | solution.py:198
  71.9 39.5 %collective-permute-done.2.w_ref = f32[4,12,128,128]{3,2,1,0:T(8,128)} collective-permute-done((f32[4,12,128,128]{3,2,1,0:T(8,128)}, f32[4,12,128,128]{3,2,1,0:T(8,128)}, u32[]{:S(2)}, u32[]{:S(2)}) %collective-permute-start.2) | collective-permute-done | bytes 3145760 | tf_op jit(solution)/shard_map/ppermute | solution.py:198
  111.4 4.8 %collective-permute-start.4 = (f32[4,12,128,128]{3,2,1,0:T(8,128)}, f32[4,12,128,128]{3,2,1,0:T(8,128)}, u32[]{:S(2)}, u32[]{:S(2)}) collective-permute-start(f32[4,12,128,128]{3,2,1,0:T(8,128)} %collective-permute-done.2.w_ref), channel_id=1, source_target_pairs={{0,1},{1,0},{2,3},{3,2},{4,5},{5,4},{6,7},{7,6},{8,9},{9,8},{10,11... | collective-permute-start | bytes 9437192 | tf_op jit(solution)/shard_map/ppermute | solution.py:198
  116.2 0.0 copy-done.4
  116.3 6.7 %all-gather = s32[4,4,12]{2,1,0:T(4,128)S(1)} all-gather(s32[1,4,12]{2,1,0:T(4,128)S(1)} %bitcast.38), channel_id=1, replica_groups=mesh['y'=8,'xl'=2,'z'=8,'xh'=2,'k'=2] {'xh','k'}, dimensions={0}, use_global_device_ids=true | all-gather | bytes 960 | tf_op jit(solution)/shard_map/all_gather | solution.py:228
  122.9 0.1 copy.24
  123.0 0.4 select_reduce_fusion
  123.4 0.1 copy.26
  123.5 0.1 reshape.64.slot_ref
  123.6 0.0 all-to-all-done.2
  123.6 2.9 %copy.29 = bf16[64,4,2,2,8,128]{5,4,3,2,1,0:T(8,128)(2,1)S(1)} copy(bf16[64,4,2,2,8,128]{5,0,4,2,3,1:T(8,128)(2,1)} %bitcast.15) | data formatting | bytes 4194304 | tf_op jit(solution)/shard_map/transpose | solution.py:238
  126.6 1.1 turn.1.t_ref
  127.6 3.1 %ladder.6 = f32[512,128]{1,0:T(8,128)S(1)} custom-call(s32[192]{0:T(256)S(1)} %reshape.64.slot_ref, s32[1]{0:T(128)} %bitcast.18.base_ref, f32[4,12,128,128]{3,2,1,0:T(8,128)} %collective-permute-done.2.w_ref, bf16[64,128,128]{2,1,0:T(8,128)(2,1)S(1)} %turn.1.t_ref), custom_call_target="tpu_custom_call" | custom-call | tf_op jit(solution)/shard_map/ladder/pallas_call | solution.py:144
  130.8 3.0 %collective-permute-start.3 = (f32[512,128]{1,0:T(8,128)S(1)}, f32[512,128]{1,0:T(8,128)S(1)}, u32[]{:S(2)}, u32[]{:S(2)}) collective-permute-start(f32[512,128]{1,0:T(8,128)S(1)} %ladder.6), channel_id=1, source_target_pairs={{0,2},{1,3},{2,0},{3,1},{4,6},{5,7},{6,4},{7,5},{8,10},{9,11},{10,... | collective-permute-start | bytes 786440 | tf_op jit(solution)/shard_map/ppermute | solution.py:198
  133.8 0.0 collective-permute-done.w_ref
  133.8 3.1 %ladder.5 = f32[512,128]{1,0:T(8,128)S(1)} custom-call(s32[192]{0:T(256)S(1)} %reshape.64.slot_ref, s32[1]{0:T(128)} %bitcast.17.base_ref, f32[4,12,128,128]{3,2,1,0:T(8,128)} %collective-permute-done.w_ref, bf16[64,128,128]{2,1,0:T(8,128)(2,1)S(1)} %turn.1.t_ref), custom_call_target="tpu_custom_call" | custom-call | tf_op jit(solution)/shard_map/ladder/pallas_call | solution.py:144
  137.0 2.4 %collective-permute-start.1 = (f32[512,128]{1,0:T(8,128)S(1)}, f32[512,128]{1,0:T(8,128)S(1)}, u32[]{:S(2)}, u32[]{:S(2)}) collective-permute-start(f32[512,128]{1,0:T(8,128)S(1)} %ladder.5), channel_id=1, source_target_pairs={{0,1},{1,0},{2,3},{3,2},{4,5},{5,4},{6,7},{7,6},{8,9},{9,8},{10,11... | collective-permute-start | bytes 786440 | tf_op jit(solution)/shard_map/ppermute | solution.py:198
  139.3 0.0 collective-permute-done.4.w_ref
  139.3 3.9 %ladder.7 = f32[512,128]{1,0:T(8,128)} custom-call(s32[192]{0:T(256)S(1)} %reshape.64.slot_ref, s32[1]{0:T(128)} %bitcast.19.base_ref, f32[4,12,128,128]{3,2,1,0:T(8,128)} %collective-permute-done.4.w_ref, bf16[64,128,128]{2,1,0:T(8,128)(2,1)S(1)} %turn.1.t_ref), custom_call_target="tpu_custom_call" | custom-call | tf_op jit(solution)/shard_map/ladder/pallas_call | solution.py:144
  143.2 3.7 %collective-permute-start.5 = (f32[512,128]{1,0:T(8,128)}, f32[512,128]{1,0:T(8,128)S(1)}, u32[]{:S(2)}, u32[]{:S(2)}) collective-permute-start(f32[512,128]{1,0:T(8,128)} %ladder.7), channel_id=1, source_target_pairs={{0,3},{1,2},{2,1},{3,0},{4,7},{5,6},{6,5},{7,4},{8,11},{9,10},{10,... | collective-permute-start | bytes 786440 | tf_op jit(solution)/shard_map/ppermute | solution.py:198
  146.9 0.0 copy-start
  146.9 0.0 copy-start.1
  146.9 0.0 copy-start.2
  147.0 3.1 %ladder.4.refs_0_ = f32[512,128]{1,0:T(8,128)S(1)} custom-call(s32[192]{0:T(256)S(1)} %reshape.64.slot_ref, s32[1]{0:T(128)} %bitcast.6.base_ref, f32[4,12,128,128]{3,2,1,0:T(8,128)} %w_ref.1, bf16[64,128,128]{2,1,0:T(8,128)(2,1)S(1)} %turn.1.t_ref), custom_call_target="tpu_custom_call" | custom-call | tf_op jit(solution)/shard_map/ladder/pallas_call | solution.py:144
  150.1 0.0 collective-permute-done.3.refs_2_
  150.1 0.0 collective-permute-done.1.refs_1_
  150.1 4.6 %collective-permute-done.5.refs_3_ = f32[512,128]{1,0:T(8,128)S(1)} collective-permute-done((f32[512,128]{1,0:T(8,128)}, f32[512,128]{1,0:T(8,128)S(1)}, u32[]{:S(2)}, u32[]{:S(2)}) %collective-permute-start.5) | collective-permute-done | bytes 262176 | tf_op jit(solution)/shard_map/ppermute | solution.py:198
  154.8 0.0 copy-done
  154.8 0.0 copy-done.1
  154.8 0.0 copy-done.2
  154.8 1.9 %finish.1 = bf16[512,512]{1,0:T(8,128)(2,1)} custom-call(s32[1]{0:T(128)} %bitcast.blk_ref, f32[512,128]{1,0:T(8,128)S(1)} %ladder.4.refs_0_, f32[512,128]{1,0:T(8,128)S(1)} %collective-permute-done.1.refs_1_, f32[512,128]{1,0:T(8,128)S(1)} %collective-permute-done.3.refs_2_, f32[512,128]{1,0:T(8,128)S(1)} %collective-permute-done.5.refs_3_, ...), custom_call_target="tpu_custom_call" | custom-call | tf_op jit(solution)/shard_map/finish/pallas_call | solution.py:182
  (1 shorter events, 0.0 us)
Async XLA Ops:
  1.2 35.3 %copy-start.3 = (s32[2048,4]{0,1:T(4,128)S(1)}, s32[2048,4]{0,1:T(4,128)}, u32[]{:S(2)}) copy-start(s32[2048,4]{0,1:T(4,128)} %param.10) | copy-start | bytes 98308
  19.9 91.5 %collective-permute-start.2 = (f32[4,12,128,128]{3,2,1,0:T(8,128)}, f32[4,12,128,128]{3,2,1,0:T(8,128)}, u32[]{:S(2)}, u32[]{:S(2)}) collective-permute-start(f32[4,12,128,128]{3,2,1,0:T(8,128)} %w_ref.1), channel_id=1, source_target_pairs={{0,2},{1,3},{2,0},{3,1},{4,6},{5,7},{6,4},{7,5},{8,10},{9,11},{10,... | collective-permute-start | bytes 9437192 | tf_op jit(solution)/shard_map/ppermute | solution.py:198
  23.8 28.7 %all-to-all-start.1 = ((bf16[64,32,128]{2,1,0:T(8,128)(2,1)}), bf16[64,32,128]{2,1,0:T(8,128)(2,1)S(1)}, u32[]{:S(2)}, u32[]{:S(2)}) async-start(bf16[64,32,128]{2,1,0:T(8,128)(2,1)} %bitcast.11), calls=%async_computation.1 | async-start | bytes 1048576 | tf_op jit(solution)/shard_map/all_to_all | solution.py:219
  58.3 57.9 %copy-start.4 = (s32[4,12]{1,0:T(4,128)S(1)}, s32[4,12]{1,0:T(4,128)}, u32[]{:S(2)}) copy-start(s32[4,12]{1,0:T(4,128)} %param.9) | copy-start | bytes 580
  58.3 65.3 %all-to-all-start.2 = ((bf16[128,64,128]{2,1,0:T(8,128)(2,1)}), bf16[128,64,128]{2,1,0:T(8,128)(2,1)}, u32[]{:S(2)}, u32[]{:S(2)}) async-start(bf16[128,64,128]{2,1,0:T(8,128)(2,1)} %bitcast.13), calls=%async_computation.2 | async-start | bytes 4194304 | tf_op jit(solution)/shard_map/all_to_all | solution.py:225
  68.1 65.7 %collective-permute-start = (f32[4,12,128,128]{3,2,1,0:T(8,128)}, f32[4,12,128,128]{3,2,1,0:T(8,128)}, u32[]{:S(2)}, u32[]{:S(2)}) collective-permute-start(f32[4,12,128,128]{3,2,1,0:T(8,128)} %w_ref.1), channel_id=1, source_target_pairs={{0,1},{1,0},{2,3},{3,2},{4,5},{5,4},{6,7},{7,6},{8,9},{9,8},{10,11... | collective-permute-start | bytes 9437192 | tf_op jit(solution)/shard_map/ppermute | solution.py:198
  111.4 27.9 %collective-permute-start.4 = (f32[4,12,128,128]{3,2,1,0:T(8,128)}, f32[4,12,128,128]{3,2,1,0:T(8,128)}, u32[]{:S(2)}, u32[]{:S(2)}) collective-permute-start(f32[4,12,128,128]{3,2,1,0:T(8,128)} %collective-permute-done.2.w_ref), channel_id=1, source_target_pairs={{0,1},{1,0},{2,3},{3,2},{4,5},{5,4},{6,7},{7,6},{8,9},{9,8},{10,11... | collective-permute-start | bytes 9437192 | tf_op jit(solution)/shard_map/ppermute | solution.py:198
  130.8 19.3 %collective-permute-start.3 = (f32[512,128]{1,0:T(8,128)S(1)}, f32[512,128]{1,0:T(8,128)S(1)}, u32[]{:S(2)}, u32[]{:S(2)}) collective-permute-start(f32[512,128]{1,0:T(8,128)S(1)} %ladder.6), channel_id=1, source_target_pairs={{0,2},{1,3},{2,0},{3,1},{4,6},{5,7},{6,4},{7,5},{8,10},{9,11},{10,... | collective-permute-start | bytes 786440 | tf_op jit(solution)/shard_map/ppermute | solution.py:198
  137.0 13.2 %collective-permute-start.1 = (f32[512,128]{1,0:T(8,128)S(1)}, f32[512,128]{1,0:T(8,128)S(1)}, u32[]{:S(2)}, u32[]{:S(2)}) collective-permute-start(f32[512,128]{1,0:T(8,128)S(1)} %ladder.5), channel_id=1, source_target_pairs={{0,1},{1,0},{2,3},{3,2},{4,5},{5,4},{6,7},{7,6},{8,9},{9,8},{10,11... | collective-permute-start | bytes 786440 | tf_op jit(solution)/shard_map/ppermute | solution.py:198
  143.2 11.6 %collective-permute-start.5 = (f32[512,128]{1,0:T(8,128)}, f32[512,128]{1,0:T(8,128)S(1)}, u32[]{:S(2)}, u32[]{:S(2)}) collective-permute-start(f32[512,128]{1,0:T(8,128)} %ladder.7), channel_id=1, source_target_pairs={{0,3},{1,2},{2,1},{3,0},{4,7},{5,6},{6,5},{7,4},{8,11},{9,10},{10,... | collective-permute-start | bytes 786440 | tf_op jit(solution)/shard_map/ppermute | solution.py:198
  146.9 7.8 %copy-start = (bf16[512,512]{1,0:T(8,128)(2,1)S(1)}, bf16[512,512]{1,0:T(8,128)(2,1)}, u32[]{:S(2)}) copy-start(bf16[512,512]{1,0:T(8,128)(2,1)} %refs_4_.1) | copy-start | bytes 1572868
  146.9 7.8 %copy-start.1 = (f32[512]{0:T(512)S(1)}, f32[512]{0:T(512)}, u32[]{:S(2)}) copy-start(f32[512]{0:T(512)} %param.12) | copy-start | bytes 6148
  146.9 7.8 %copy-start.2 = (f32[512]{0:T(512)S(1)}, f32[512]{0:T(512)}, u32[]{:S(2)}) copy-start(f32[512]{0:T(512)} %param.13) | copy-start | bytes 6148

commit v3 on v2

--- a/solution.py
+++ b/solution.py
@@ -4,6 +4,7 @@
 from jax.experimental import pallas as pl
 from jax.experimental.pallas import tpu as pltpu
 from jax.sharding import Mesh, PartitionSpec as P
+
 
 GRP = ("y", "xl", "z")
 BLK = ("xh", "k")
@@ -124,12 +125,14 @@
 def ladder_call(slot, base, weights, turned):
     columns, listed, depth, size = weights.shape
     width = turned.shape[1]
-
-    def body(slot_ref, base_ref, w_ref, t_ref, out_ref):
-        for n in range(columns):
+    some = columns // 2
+
+    def body(slot_ref, w_ref, t_ref, out_ref):
+        first = pl.program_id(0) * some
+        for n in range(some):
             right, left = [], []
             for r in range(listed):
-                s = slot_ref[base_ref[0] + n * listed + r]
+                s = slot_ref[base + (first + n) * listed + r]
                 w = w_ref[n, r]
                 hi = w.astype(BF)
                 lo = (w - hi.astype(F32)).astype(BF)
@@ -144,18 +147,18 @@
     return pl.pallas_call(
         body,
         grid_spec=pltpu.PrefetchScalarGridSpec(
-            num_scalar_prefetch=2,
-            grid=(1,),
+            num_scalar_prefetch=1,
+            grid=(2,),
             in_specs=[
-                pl.BlockSpec(weights.shape, lambda i, s, b: (0, 0, 0, 0)),
-                pl.BlockSpec(turned.shape, lambda i, s, b: (0, 0, 0)),
+                pl.BlockSpec((some, listed, depth, size), lambda i, s: (i, 0, 0, 0)),
+                pl.BlockSpec(turned.shape, lambda i, s: (0, 0, 0)),
             ],
-            out_specs=pl.BlockSpec((columns * size, width), lambda i, s, b: (0, 0)),
+            out_specs=pl.BlockSpec((some * size, width), lambda i, s: (i, 0)),
         ),
         out_shape=jax.ShapeDtypeStruct((columns * size, width), F32),
         compiler_params=PARAMS,
         name="ladder",
-    )(slot, base, weights, turned)
+    )(slot, weights, turned)
 
 
 def finish_call(blk, pieces, source, occ, virt):
@@ -213,8 +216,8 @@
 
     x = amplitudes.reshape(owned, nx, sub, nblk, width).transpose(1, 3, 2, 0, 4)
     x = lax.all_to_all(x.reshape(nx * nblk, sub, owned, width), LINE, 0, 0, tiled=True)
-    held, x = lax.optimization_barrier((integrals, x))
-    across = swap(held, 2, nblk)
+    rows_across = swap(tile_rows, 2, nblk)
+    across = swap(integrals, 2, nblk)
     x = x.reshape(nx, nblk, sub, owned, width).transpose(1, 2, 0, 3, 4)
     x = lax.all_to_all(x.reshape(ny * nz, nx * owned, width), PLANE, 0, 0, tiled=True)
     table = x.reshape(all_tiles, width)
@@ -224,8 +227,10 @@
     outgoing = route_call(slot_of, early, table, slots)
     incoming = lax.all_to_all(outgoing.reshape(groups, slots, width), GRP, 0, 0, tiled=True)
 
-    beside = swap(held, 1, nblk)
-    named_tiles = lax.all_gather(tile_rows, BLK, axis=0, tiled=True)
+    beside = swap(integrals, 1, nblk)
+    near_rows = jnp.concatenate([tile_rows, rows_across], axis=0)
+    far_rows = swap(near_rows, 1, nblk)
+    named_tiles = jnp.concatenate([near_rows, far_rows], axis=0)
     y_of = named_tiles // (nx * nz * owned)
     x_of = (named_tiles // (nz * owned)) % nx
     z_of = (named_tiles // owned) % nz
@@ -238,13 +243,12 @@
     tiles = incoming.reshape(nblk, ny // nblk, nx, nz, slots, width).transpose(4, 0, 2, 1, 3, 5)
     turned = turn_call(tiles.reshape(slots, rows * nblk, width))
 
-    def partial(flip, weights):
-        base = (blk ^ flip) * (columns * listed)
-        return ladder_call(slot, base.reshape(1), weights, turned)
-
-    far = swap(partial(2, across), 2, nblk)
+    def partial(place, weights):
+        return ladder_call(slot, place * columns * listed, weights, turned)
+
+    far = swap(partial(1, across), 2, nblk)
     farther = swap(partial(3, diagonal), 3, nblk)
-    near = swap(partial(1, beside), 1, nblk)
+    near = swap(partial(2, beside), 1, nblk)
     home = partial(0, integrals)
     return finish_call(
         blk.reshape(1),

time: 157 us -> 216 us (1.38)
  blocking collectives: 25 us -> 72.9 us
  starting transfers between devices: 43.1 us -> 57 us
  waiting for transfers between devices: 58.9 us -> 56 us
    all_to_all x1, blocking collectives: 18.4 us -> 72.9 us  [per_device(): lax.all_to_all(x.reshape(nx * nblk, sub, owned, width), LINE, 0, 0, tiled...]
    ppermute x6 -> x8, waiting for transfers between devices: 44.2 us -> 8.27 us  [swap(): return lax.ppermute(x, BLK, [(b, b ^ flip) for b in range(n)])]
    all_to_all x1, waiting for transfers between devices: 0.01 us -> 32.6 us  [per_device(): lax.all_to_all(outgoing.reshape(groups, slots, width), GRP, 0, 0, tiled=T...]
    ppermute x6 -> x8, starting transfers between devices: 20.7 us -> 30.2 us  [swap(): return lax.ppermute(x, BLK, [(b, b ^ flip) for b in range(n)])]
    all_gather x1 -> x0, blocking collectives: 6.65 us -> none  [per_device(): named_tiles = lax.all_gather(tile_rows, BLK, axis=0, tiled=True)]
    all_to_all x1, starting transfers between devices: 12.6 us -> 16.3 us  [per_device(): lax.all_to_all(x.reshape(ny * nz, nx * owned, width), PLANE, 0, 0, tiled=...]
  transfers between devices with their start and end apart: 8 -> 10, of which waited for: 3 -> 5; matrix products, arithmetic and copies ran while one was open for 3% -> 3% of each run, Pallas kernels for 13% -> 9%
where the time goes in v3:
time: 216 us; the launch traced here: 215 us
  blocking collectives  72.9 us (34%)
  starting transfers between devices  57 us (26%)
  waiting for transfers between devices  56 us (26%)
  Pallas kernels  21.9 us (10%)
  local copies, waits for them, and re-layouts  6.18 us (3%)
    all_to_all x1, blocking collectives, per_device(): lax.all_to_all(x.reshape(nx * nblk, sub, owned, width), LINE, 0, 0, tiled...  72.9 us
    all_to_all x1, waiting for transfers between devices, per_device(): lax.all_to_all(outgoing.reshape(groups, slots, width), GRP, 0, 0, tiled=T...  32.6 us
    ppermute x8, starting transfers between devices, swap(): return lax.ppermute(x, BLK, [(b, b ^ flip) for b in range(n)])  30.2 us
    all_to_all x1, starting transfers between devices, per_device(): lax.all_to_all(x.reshape(ny * nz, nx * owned, width), PLANE, 0, 0, tiled=...  16.3 us
    all_to_all x1, waiting for transfers between devices, per_device(): lax.all_to_all(x.reshape(ny * nz, nx * owned, width), PLANE, 0, 0, tiled=...  15.1 us
    pallas_call x4, Pallas kernels, ladder_call(): pl.pallas_call(body, grid_spec=pltpu.PrefetchScalarGridSpec(num_scalar_pr...  12.4 us
    all_to_all x1, starting transfers between devices, per_device(): lax.all_to_all(outgoing.reshape(groups, slots, width), GRP, 0, 0, tiled=T...  10.5 us
    ppermute x8, waiting for transfers between devices, swap(): return lax.ppermute(x, BLK, [(b, b ^ flip) for b in range(n)])  8.27 us
  transfers between devices with their start and end apart: 10, of which 5 were waited for; matrix products, arithmetic and copies ran while one was open for 3% of the time, Pallas kernels for 9%

profile of v3, /device:TPU:1, one launch (start us, length us, event | category | flops | bytes accessed | tf_op | source)
XLA Modules:
  0.0 214.8 jit_solution(6863764993121755856)
XLA Ops:
  0.0 5.5 %collective-permute-start.4 = (f32[4,12,128,128]{3,2,1,0:T(8,128)}, f32[4,12,128,128]{3,2,1,0:T(8,128)}, u32[]{:S(2)}, u32[]{:S(2)}) collective-permute-start(f32[4,12,128,128]{3,2,1,0:T(8,128)} %w_ref.1), channel_id=1, source_target_pairs={{0,2},{1,3},{2,0},{3,1},{4,6},{5,7},{6,4},{7,5},{8,10},{9,11},{10,... | collective-permute-start | bytes 9437192 | tf_op jit(solution)/shard_map/ppermute | solution.py:201
  5.5 1.2 reshape.255
  6.6 0.0 copy-start.3
  6.7 0.3 copy.23
  7.0 72.9 %all_to_all.15 = bf16[8,16,16,128]{3,2,1,0:T(8,128)(2,1)S(1)} all-to-all(bf16[8,16,16,128]{3,2,1,0:T(8,128)(2,1)S(1)} %bitcast.27), channel_id=1, replica_groups=mesh['y'=8,'xl'=2,'z'=8,'xh'=2,'k'=2] {'xl','xh','k'}, dimensions={0} | all-to-all | bytes 1048576 | tf_op jit(solution)/shard_map/all_to_all | solution.py:218
  79.9 0.8 copy.24
  80.8 16.3 %all-to-all-start.1 = ((bf16[64,32,128]{2,1,0:T(8,128)(2,1)}), bf16[64,32,128]{2,1,0:T(8,128)(2,1)S(1)}, u32[]{:S(2)}, u32[]{:S(2)}) async-start(bf16[64,32,128]{2,1,0:T(8,128)(2,1)} %bitcast.8), calls=%async_computation.1 | async-start | bytes 1048576 | tf_op jit(solution)/shard_map/all_to_all | solution.py:222
  97.1 0.0 copy-done.3
  97.1 0.1 reshape.252
  97.2 0.1 copy.27
  97.4 0.3 reshape.253.dest_ref
  97.7 0.7 rank.1
  98.4 15.1 %all-to-all-done.1 = bf16[64,32,128]{2,1,0:T(8,128)(2,1)S(1)} async-done(((bf16[64,32,128]{2,1,0:T(8,128)(2,1)}), bf16[64,32,128]{2,1,0:T(8,128)(2,1)S(1)}, u32[]{:S(2)}, u32[]{:S(2)}) %all-to-all-start.1) | async-done | bytes 524320 | tf_op jit(solution)/shard_map/all_to_all | solution.py:222
  113.5 5.9 %route.1 = bf16[8192,128]{1,0:T(8,128)(2,1)} custom-call(f32[128,2048]{1,0:T(8,128)S(1)} %get-tuple-element.9.slot_ref, f32[128,128]{1,0:T(8,128)S(1)} %get-tuple-element.10.early_ref, bf16[2048,128]{1,0:T(8,128)(2,1)S(1)} %bitcast.23), custom_call_target="tpu_custom_call" | custom-call | tf_op jit(solution)/shard_map/route/pallas_call | solution.py:91
  119.4 0.0 copy-start.4
  119.4 10.5 %all-to-all-start.2 = ((bf16[128,64,128]{2,1,0:T(8,128)(2,1)}), bf16[128,64,128]{2,1,0:T(8,128)(2,1)}, u32[]{:S(2)}, u32[]{:S(2)}) async-start(bf16[128,64,128]{2,1,0:T(8,128)(2,1)} %bitcast.10), calls=%async_computation.2 | async-start | bytes 4194304 | tf_op jit(solution)/shard_map/all_to_all | solution.py:228
  129.9 3.2 %collective-permute-start.2 = (f32[4,12,128,128]{3,2,1,0:T(8,128)}, f32[4,12,128,128]{3,2,1,0:T(8,128)}, u32[]{:S(2)}, u32[]{:S(2)}) collective-permute-start(f32[4,12,128,128]{3,2,1,0:T(8,128)} %w_ref.1), channel_id=1, source_target_pairs={{0,1},{1,0},{2,3},{3,2},{4,5},{5,4},{6,7},{7,6},{8,9},{9,8},{10,11... | collective-permute-start | bytes 9437192 | tf_op jit(solution)/shard_map/ppermute | solution.py:201
  133.2 0.0 collective-permute-done.4.w_ref
  133.2 1.9 collective-permute-start.6
  135.1 0.0 copy-done.4
  135.1 3.6 %collective-permute-start = (s32[4,12]{1,0:T(4,128)S(1)}, s32[4,12]{1,0:T(4,128)S(1)}, u32[]{:S(2)}, u32[]{:S(2)}) collective-permute-start(s32[4,12]{1,0:T(4,128)S(1)} %copy-done.4), channel_id=1, source_target_pairs={{0,2},{1,3},{2,0},{3,1},{4,6},{5,7},{6,4},{7,5},{8,10},{9,11},{10,... | collective-permute-start | bytes 584 | tf_op jit(solution)/shard_map/ppermute | solution.py:201
  138.8 2.6 %collective-permute-done = s32[4,12]{1,0:T(4,128)S(1)} collective-permute-done((s32[4,12]{1,0:T(4,128)S(1)}, s32[4,12]{1,0:T(4,128)S(1)}, u32[]{:S(2)}, u32[]{:S(2)}) %collective-permute-start) | collective-permute-done | bytes 224 | tf_op jit(solution)/shard_map/ppermute | solution.py:201
  141.4 3.2 %collective-permute-start.1 = (s32[8,12]{1,0:T(8,128)S(1)}, s32[8,12]{1,0:T(8,128)S(1)}, u32[]{:S(2)}, u32[]{:S(2)}) collective-permute-start(s32[8,12]{1,0:T(8,128)S(1)} %pad_add_fusion.1), channel_id=1, source_target_pairs={{0,1},{1,0},{2,3},{3,2},{4,5},{5,4},{6,7},{7,6},{8,9},{9,8},{10,11... | collective-permute-start | bytes 1160 | tf_op jit(solution)/shard_map/ppermute | solution.py:201
  144.6 0.8 collective-permute-done.1
  145.4 0.1 copy.20
  145.5 0.4 select_reduce_fusion
  145.9 0.1 copy.22
  146.0 0.1 reshape.254.slot_ref
  146.1 32.6 %all-to-all-done.2 = bf16[128,64,128]{2,1,0:T(8,128)(2,1)} async-done(((bf16[128,64,128]{2,1,0:T(8,128)(2,1)}), bf16[128,64,128]{2,1,0:T(8,128)(2,1)}, u32[]{:S(2)}, u32[]{:S(2)}) %all-to-all-start.2) | async-done | bytes 2097184 | tf_op jit(solution)/shard_map/all_to_all | solution.py:228
  178.7 2.9 %copy.25 = bf16[64,4,2,2,8,128]{5,4,3,2,1,0:T(8,128)(2,1)S(1)} copy(bf16[64,4,2,2,8,128]{5,0,4,2,3,1:T(8,128)(2,1)} %bitcast.12) | data formatting | bytes 4194304 | tf_op jit(solution)/shard_map/transpose | solution.py:243
  181.6 1.1 turn.1.t_ref
  182.7 2.9 %ladder.6 = f32[512,128]{1,0:T(8,128)S(1)} custom-call(s32[192]{0:T(256)S(1)} %reshape.254.slot_ref, f32[4,12,128,128]{3,2,1,0:T(8,128)} %collective-permute-done.4.w_ref, bf16[64,128,128]{2,1,0:T(8,128)(2,1)S(1)} %turn.1.t_ref), custom_call_target="tpu_custom_call" | custom-call | tf_op jit(solution)/shard_map/ladder/pallas_call | solution.py:147
  185.6 2.2 %collective-permute-start.5 = (f32[512,128]{1,0:T(8,128)S(1)}, f32[512,128]{1,0:T(8,128)S(1)}, u32[]{:S(2)}, u32[]{:S(2)}) collective-permute-start(f32[512,128]{1,0:T(8,128)S(1)} %ladder.6), channel_id=1, source_target_pairs={{0,2},{1,3},{2,0},{3,1},{4,6},{5,7},{6,4},{7,5},{8,10},{9,11},{10,... | collective-permute-start | bytes 786440 | tf_op jit(solution)/shard_map/ppermute | solution.py:201
  187.9 0.0 collective-permute-done.2.w_ref
  187.9 2.9 %ladder.5 = f32[512,128]{1,0:T(8,128)S(1)} custom-call(s32[192]{0:T(256)S(1)} %reshape.254.slot_ref, f32[4,12,128,128]{3,2,1,0:T(8,128)} %collective-permute-done.2.w_ref, bf16[64,128,128]{2,1,0:T(8,128)(2,1)S(1)} %turn.1.t_ref), custom_call_target="tpu_custom_call" | custom-call | tf_op jit(solution)/shard_map/ladder/pallas_call | solution.py:147
  190.8 6.9 %collective-permute-start.3 = (f32[512,128]{1,0:T(8,128)S(1)}, f32[512,128]{1,0:T(8,128)S(1)}, u32[]{:S(2)}, u32[]{:S(2)}) collective-permute-start(f32[512,128]{1,0:T(8,128)S(1)} %ladder.5), channel_id=1, source_target_pairs={{0,1},{1,0},{2,3},{3,2},{4,5},{5,4},{6,7},{7,6},{8,9},{9,8},{10,11... | collective-permute-start | bytes 786440 | tf_op jit(solution)/shard_map/ppermute | solution.py:201
  197.7 0.0 collective-permute-done.6.w_ref
  197.7 3.6 %ladder.7 = f32[512,128]{1,0:T(8,128)} custom-call(s32[192]{0:T(256)S(1)} %reshape.254.slot_ref, f32[4,12,128,128]{3,2,1,0:T(8,128)} %collective-permute-done.6.w_ref, bf16[64,128,128]{2,1,0:T(8,128)(2,1)S(1)} %turn.1.t_ref), custom_call_target="tpu_custom_call" | custom-call | tf_op jit(solution)/shard_map/ladder/pallas_call | solution.py:147
  201.3 3.6 %collective-permute-start.7 = (f32[512,128]{1,0:T(8,128)}, f32[512,128]{1,0:T(8,128)S(1)}, u32[]{:S(2)}, u32[]{:S(2)}) collective-permute-start(f32[512,128]{1,0:T(8,128)} %ladder.7), channel_id=1, source_target_pairs={{0,3},{1,2},{2,1},{3,0},{4,7},{5,6},{6,5},{7,4},{8,11},{9,10},{10,... | collective-permute-start | bytes 786440 | tf_op jit(solution)/shard_map/ppermute | solution.py:201
  205.0 0.0 copy-start
  205.0 0.0 copy-start.1
  205.0 0.0 copy-start.2
  205.0 2.9 %ladder.4.refs_0_ = f32[512,128]{1,0:T(8,128)S(1)} custom-call(s32[192]{0:T(256)S(1)} %reshape.254.slot_ref, f32[4,12,128,128]{3,2,1,0:T(8,128)} %w_ref.1, bf16[64,128,128]{2,1,0:T(8,128)(2,1)S(1)} %turn.1.t_ref), custom_call_target="tpu_custom_call" | custom-call | tf_op jit(solution)/shard_map/ladder/pallas_call | solution.py:147
  207.9 0.0 collective-permute-done.5.refs_2_
  208.0 0.0 collective-permute-done.3.refs_1_
  208.0 4.9 %collective-permute-done.7.refs_3_ = f32[512,128]{1,0:T(8,128)S(1)} collective-permute-done((f32[512,128]{1,0:T(8,128)}, f32[512,128]{1,0:T(8,128)S(1)}, u32[]{:S(2)}, u32[]{:S(2)}) %collective-permute-start.7) | collective-permute-done | bytes 262176 | tf_op jit(solution)/shard_map/ppermute | solution.py:201
  212.8 0.0 copy-done
  212.8 0.0 copy-done.1
  212.9 0.0 copy-done.2
  212.9 1.9 finish.1
  (2 shorter events, 0.0 us)
Async XLA Ops:
  0.0 133.2 %collective-permute-start.4 = (f32[4,12,128,128]{3,2,1,0:T(8,128)}, f32[4,12,128,128]{3,2,1,0:T(8,128)}, u32[]{:S(2)}, u32[]{:S(2)}) collective-permute-start(f32[4,12,128,128]{3,2,1,0:T(8,128)} %w_ref.1), channel_id=1, source_target_pairs={{0,2},{1,3},{2,0},{3,1},{4,6},{5,7},{6,4},{7,5},{8,10},{9,11},{10,... | collective-permute-start | bytes 9437192 | tf_op jit(solution)/shard_map/ppermute | solution.py:201
  6.6 90.5 %copy-start.3 = (s32[2048,4]{0,1:T(4,128)S(1)}, s32[2048,4]{0,1:T(4,128)}, u32[]{:S(2)}) copy-start(s32[2048,4]{0,1:T(4,128)} %param.10) | copy-start | bytes 98308
  80.8 32.8 %all-to-all-start.1 = ((bf16[64,32,128]{2,1,0:T(8,128)(2,1)}), bf16[64,32,128]{2,1,0:T(8,128)(2,1)S(1)}, u32[]{:S(2)}, u32[]{:S(2)}) async-start(bf16[64,32,128]{2,1,0:T(8,128)(2,1)} %bitcast.8), calls=%async_computation.1 | async-start | bytes 1048576 | tf_op jit(solution)/shard_map/all_to_all | solution.py:222
  119.4 15.7 %copy-start.4 = (s32[4,12]{1,0:T(4,128)S(1)}, s32[4,12]{1,0:T(4,128)}, u32[]{:S(2)}) copy-start(s32[4,12]{1,0:T(4,128)} %param.9) | copy-start | bytes 580
  119.4 59.3 %all-to-all-start.2 = ((bf16[128,64,128]{2,1,0:T(8,128)(2,1)}), bf16[128,64,128]{2,1,0:T(8,128)(2,1)}, u32[]{:S(2)}, u32[]{:S(2)}) async-start(bf16[128,64,128]{2,1,0:T(8,128)(2,1)} %bitcast.10), calls=%async_computation.2 | async-start | bytes 4194304 | tf_op jit(solution)/shard_map/all_to_all | solution.py:228
  129.9 57.9 %collective-permute-start.2 = (f32[4,12,128,128]{3,2,1,0:T(8,128)}, f32[4,12,128,128]{3,2,1,0:T(8,128)}, u32[]{:S(2)}, u32[]{:S(2)}) collective-permute-start(f32[4,12,128,128]{3,2,1,0:T(8,128)} %w_ref.1), channel_id=1, source_target_pairs={{0,1},{1,0},{2,3},{3,2},{4,5},{5,4},{6,7},{7,6},{8,9},{9,8},{10,11... | collective-permute-start | bytes 9437192 | tf_op jit(solution)/shard_map/ppermute | solution.py:201
  133.2 64.5 %collective-permute-start.6 = (f32[4,12,128,128]{3,2,1,0:T(8,128)}, f32[4,12,128,128]{3,2,1,0:T(8,128)}, u32[]{:S(2)}, u32[]{:S(2)}) collective-permute-start(f32[4,12,128,128]{3,2,1,0:T(8,128)} %collective-permute-done.4.w_ref), channel_id=1, source_target_pairs={{0,1},{1,0},{2,3},{3,2},{4,5},{5,4},{6,7},{7,6},{8,9},{9,8},{10,11... | collective-permute-start | bytes 9437192 | tf_op jit(solution)/shard_map/ppermute | solution.py:201
  135.1 6.2 %collective-permute-start = (s32[4,12]{1,0:T(4,128)S(1)}, s32[4,12]{1,0:T(4,128)S(1)}, u32[]{:S(2)}, u32[]{:S(2)}) collective-permute-start(s32[4,12]{1,0:T(4,128)S(1)} %copy-done.4), channel_id=1, source_target_pairs={{0,2},{1,3},{2,0},{3,1},{4,6},{5,7},{6,4},{7,5},{8,10},{9,11},{10,... | collective-permute-start | bytes 584 | tf_op jit(solution)/shard_map/ppermute | solution.py:201
  141.4 4.0 %collective-permute-start.1 = (s32[8,12]{1,0:T(8,128)S(1)}, s32[8,12]{1,0:T(8,128)S(1)}, u32[]{:S(2)}, u32[]{:S(2)}) collective-permute-start(s32[8,12]{1,0:T(8,128)S(1)} %pad_add_fusion.1), channel_id=1, source_target_pairs={{0,1},{1,0},{2,3},{3,2},{4,5},{5,4},{6,7},{7,6},{8,9},{9,8},{10,11... | collective-permute-start | bytes 1160 | tf_op jit(solution)/shard_map/ppermute | solution.py:201
  185.6 22.3 %collective-permute-start.5 = (f32[512,128]{1,0:T(8,128)S(1)}, f32[512,128]{1,0:T(8,128)S(1)}, u32[]{:S(2)}, u32[]{:S(2)}) collective-permute-start(f32[512,128]{1,0:T(8,128)S(1)} %ladder.6), channel_id=1, source_target_pairs={{0,2},{1,3},{2,0},{3,1},{4,6},{5,7},{6,4},{7,5},{8,10},{9,11},{10,... | collective-permute-start | bytes 786440 | tf_op jit(solution)/shard_map/ppermute | solution.py:201
  190.8 17.2 %collective-permute-start.3 = (f32[512,128]{1,0:T(8,128)S(1)}, f32[512,128]{1,0:T(8,128)S(1)}, u32[]{:S(2)}, u32[]{:S(2)}) collective-permute-start(f32[512,128]{1,0:T(8,128)S(1)} %ladder.5), channel_id=1, source_target_pairs={{0,1},{1,0},{2,3},{3,2},{4,5},{5,4},{6,7},{7,6},{8,9},{9,8},{10,11... | collective-permute-start | bytes 786440 | tf_op jit(solution)/shard_map/ppermute | solution.py:201
  201.3 11.5 %collective-permute-start.7 = (f32[512,128]{1,0:T(8,128)}, f32[512,128]{1,0:T(8,128)S(1)}, u32[]{:S(2)}, u32[]{:S(2)}) collective-permute-start(f32[512,128]{1,0:T(8,128)} %ladder.7), channel_id=1, source_target_pairs={{0,3},{1,2},{2,1},{3,0},{4,7},{5,6},{6,5},{7,4},{8,11},{9,10},{10,... | collective-permute-start | bytes 786440 | tf_op jit(solution)/shard_map/ppermute | solution.py:201
  205.0 7.9 %copy-start = (bf16[512,512]{1,0:T(8,128)(2,1)S(1)}, bf16[512,512]{1,0:T(8,128)(2,1)}, u32[]{:S(2)}) copy-start(bf16[512,512]{1,0:T(8,128)(2,1)} %refs_4_.1) | copy-start | bytes 1572868
  205.0 7.9 %copy-start.1 = (f32[512]{0:T(512)S(1)}, f32[512]{0:T(512)}, u32[]{:S(2)}) copy-start(f32[512]{0:T(512)} %param.12) | copy-start | bytes 6148
  205.0 7.9 %copy-start.2 = (f32[512]{0:T(512)S(1)}, f32[512]{0:T(512)}, u32[]{:S(2)}) copy-start(f32[512]{0:T(512)} %param.13) | copy-start | bytes 6148

commit v4 on v2

--- a/solution.py
+++ b/solution.py
@@ -4,6 +4,7 @@
 from jax.experimental import pallas as pl
 from jax.experimental.pallas import tpu as pltpu
 from jax.sharding import Mesh, PartitionSpec as P
+
 
 GRP = ("y", "xl", "z")
 BLK = ("xh", "k")
@@ -121,77 +122,72 @@
     )(tiles)
 
 
-def ladder_call(slot, base, weights, turned):
-    columns, listed, depth, size = weights.shape
+def ladder_call(slot, blk, flips, weights, turned, sources, occ, virt):
+    columns, listed, depth, size = weights[0].shape
     width = turned.shape[1]
-
-    def body(slot_ref, base_ref, w_ref, t_ref, out_ref):
-        for n in range(columns):
-            right, left = [], []
-            for r in range(listed):
-                s = slot_ref[base_ref[0] + n * listed + r]
-                w = w_ref[n, r]
-                hi = w.astype(BF)
-                lo = (w - hi.astype(F32)).astype(BF)
-                right.append(jnp.concatenate([hi, lo], axis=1))
-                t = t_ref[jnp.maximum(s, 0)]
-                left.append(jnp.where(s >= 0, t, jnp.zeros_like(t)))
-            right = jnp.concatenate(right, axis=0)
-            left = jnp.concatenate(left, axis=1)
-            acc = jnp.dot(left, right, preferred_element_type=F32)
-            out_ref[n * size : (n + 1) * size, :] = (acc[:, :size] + acc[:, size:]).T
+    owners = len(weights)
+    some = 2
+
+    def body(slot_ref, blk_ref, *refs):
+        w_refs = refs[:owners]
+        t_ref = refs[owners]
+        s_refs = refs[owners + 1 : 2 * owners + 1]
+        o_ref, v_ref, out_ref, held_ref, sems = refs[2 * owners + 1 :]
+        for m in range(owners):
+            for n in range(columns):
+                at = m * columns + n
+                pltpu.make_async_copy(w_refs[m].at[n], held_ref.at[at], sems.at[at]).start()
+        for m in range(owners):
+            to = blk_ref[0] ^ flips[m]
+
+            def some_columns(i, _, m=m, to=to):
+                for u in range(some):
+                    n = i * some + u
+                    at = m * columns + n
+                    pltpu.make_async_copy(w_refs[m].at[n], held_ref.at[at], sems.at[at]).wait()
+                    right, left = [], []
+                    for r in range(listed):
+                        s = slot_ref[at * listed + r]
+                        w = held_ref[at, r]
+                        hi = w.astype(BF)
+                        lo = (w - hi.astype(F32)).astype(BF)
+                        right.append(jnp.concatenate([hi, lo], axis=1))
+                        t = t_ref[jnp.maximum(s, 0)]
+                        left.append(jnp.where(s >= 0, t, jnp.zeros_like(t)))
+                    right = jnp.concatenate(right, axis=0)
+                    left = jnp.concatenate(left, axis=1)
+                    acc = jnp.dot(left, right, preferred_element_type=F32)
+                    part = (acc[:, :size] + acc[:, size:]).T
+                    rows = pl.ds(n * size, size)
+                    total = s_refs[m][rows, :].astype(F32) + part
+                    v = jnp.broadcast_to(v_ref[pl.ds(at, 1), :], (size, size)).T
+                    out_ref[to, rows, :] = (total / (v + o_ref[...])).astype(BF)
+                return 0
+
+            lax.fori_loop(0, columns // some, some_columns, 0)
+
+    def whole(x):
+        return pl.BlockSpec(x.shape, lambda i, s, b: (0,) * x.ndim)
 
     return pl.pallas_call(
         body,
         grid_spec=pltpu.PrefetchScalarGridSpec(
             num_scalar_prefetch=2,
             grid=(1,),
-            in_specs=[
-                pl.BlockSpec(weights.shape, lambda i, s, b: (0, 0, 0, 0)),
-                pl.BlockSpec(turned.shape, lambda i, s, b: (0, 0, 0)),
+            in_specs=[pl.BlockSpec(memory_space=pl.ANY)] * owners
+            + [whole(turned)]
+            + [whole(x) for x in sources]
+            + [pl.BlockSpec((1, width), lambda i, s, b: (0, b[0])), whole(virt)],
+            out_specs=pl.BlockSpec((owners, columns * size, width), lambda i, s, b: (0, 0, 0)),
+            scratch_shapes=[
+                pltpu.VMEM((owners * columns, listed, depth, size), F32),
+                pltpu.SemaphoreType.DMA((owners * columns,)),
             ],
-            out_specs=pl.BlockSpec((columns * size, width), lambda i, s, b: (0, 0)),
         ),
-        out_shape=jax.ShapeDtypeStruct((columns * size, width), F32),
-        compiler_params=PARAMS,
+        out_shape=jax.ShapeDtypeStruct((owners, columns * size, width), BF),
+        compiler_params=pltpu.CompilerParams(vmem_limit_bytes=48 * 1024 * 1024),
         name="ladder",
-    )(slot, base, weights, turned)
-
-
-def finish_call(blk, pieces, source, occ, virt):
-    rows, width = pieces[0].shape
-    count = len(pieces)
-    tall, size = virt.shape
-
-    def body(blk_ref, *refs):
-        piece_refs = refs[:count]
-        s_ref, o_ref, v_ref, out_ref = refs[count:]
-        i = pl.program_id(0)
-        for j in range(count):
-
-            @pl.when(i == j)
-            def _(j=j):
-                for n in range(tall):
-                    at = slice(n * size, (n + 1) * size)
-                    v = jnp.broadcast_to(v_ref[n : n + 1, :], (size, size)).T
-                    total = s_ref[at, :].astype(F32) + piece_refs[j][at, :]
-                    out_ref[at, :] = (total / (v + o_ref[...])).astype(BF)
-
-    whole = pl.BlockSpec((rows, width), lambda i, b: (0, 0))
-    part = pl.BlockSpec((rows, width), lambda i, b: (0, b[0] ^ i))
-    return pl.pallas_call(
-        body,
-        grid_spec=pltpu.PrefetchScalarGridSpec(
-            num_scalar_prefetch=1,
-            grid=(count,),
-            in_specs=[whole] * count
-            + [part, pl.BlockSpec((1, width), lambda i, b: (0, b[0] ^ i)), pl.BlockSpec(virt.shape, lambda i, b: (0, 0))],
-            out_specs=part,
-        ),
-        out_shape=jax.ShapeDtypeStruct(source.shape, BF),
-        compiler_params=PARAMS,
-        name="finish",
-    )(blk, *pieces, source, occ, virt)
+    )(slot, blk, *weights, turned, *sources, occ, virt)
 
 
 def swap(x, flip, n):
@@ -213,8 +209,11 @@
 
     x = amplitudes.reshape(owned, nx, sub, nblk, width).transpose(1, 3, 2, 0, 4)
     x = lax.all_to_all(x.reshape(nx * nblk, sub, owned, width), LINE, 0, 0, tiled=True)
-    held, x = lax.optimization_barrier((integrals, x))
-    across = swap(held, 2, nblk)
+    facts = [virt_energy.reshape(columns, size), tile_rows.astype(F32)]
+    facts.append(jnp.zeros((columns, size - listed), F32))
+    facts = jnp.concatenate(facts, axis=1)
+    facts_across = swap(facts, 2, nblk)
+    across = swap(integrals, 2, nblk)
     x = x.reshape(nx, nblk, sub, owned, width).transpose(1, 2, 0, 3, 4)
     x = lax.all_to_all(x.reshape(ny * nz, nx * owned, width), PLANE, 0, 0, tiled=True)
     table = x.reshape(all_tiles, width)
@@ -224,8 +223,10 @@
     outgoing = route_call(slot_of, early, table, slots)
     incoming = lax.all_to_all(outgoing.reshape(groups, slots, width), GRP, 0, 0, tiled=True)
 
-    beside = swap(held, 1, nblk)
-    named_tiles = lax.all_gather(tile_rows, BLK, axis=0, tiled=True)
+    beside = swap(integrals, 1, nblk)
+    facts = jnp.concatenate([facts, facts_across], axis=0)
+    facts = jnp.concatenate([facts, swap(facts, 1, nblk)], axis=0)
+    named_tiles = facts[:, size : size + listed].astype(jnp.int32)
     y_of = named_tiles // (nx * nz * owned)
     x_of = (named_tiles // (nz * owned)) % nx
     z_of = (named_tiles // owned) % nz
@@ -238,21 +239,25 @@
     tiles = incoming.reshape(nblk, ny // nblk, nx, nz, slots, width).transpose(4, 0, 2, 1, 3, 5)
     turned = turn_call(tiles.reshape(slots, rows * nblk, width))
 
-    def partial(flip, weights):
-        base = (blk ^ flip) * (columns * listed)
-        return ladder_call(slot, base.reshape(1), weights, turned)
-
-    far = swap(partial(2, across), 2, nblk)
-    farther = swap(partial(3, diagonal), 3, nblk)
-    near = swap(partial(1, beside), 1, nblk)
-    home = partial(0, integrals)
-    return finish_call(
+    def quarter(flip):
+        return lax.dynamic_slice_in_dim(source_terms, (blk ^ flip) * width, width, 1)
+
+    source_far = swap(quarter(2), 2, nblk)
+    source_near = swap(quarter(1), 1, nblk)
+    source_diagonal = swap(quarter(3), 3, nblk)
+
+    done = ladder_call(
+        slot,
         blk.reshape(1),
-        (home, near, far, farther),
-        source_terms,
+        (0, 2, 1, 3),
+        (integrals, across, beside, diagonal),
+        turned,
+        (quarter(0), source_far, source_near, source_diagonal),
         occ_energy.reshape(1, full_width),
-        virt_energy.reshape(columns, size),
+        facts[:, :size],
     )
+    done = lax.all_to_all(done, BLK, 0, 0, tiled=True)
+    return done.transpose(1, 0, 2).reshape(columns * size, full_width)
 
 
 def solution(mesh):

time: 157 us -> 210 us (1.34)
  blocking collectives: 25 us -> 88.6 us
  waiting for transfers between devices: 58.9 us -> 41.3 us
  starting transfers between devices: 43.1 us -> 53.6 us
  Pallas kernels: 22.8 us -> 16.4 us
    all_to_all x1, blocking collectives: 18.4 us -> 72.9 us  [per_device(): lax.all_to_all(x.reshape(nx * nblk, sub, owned, width), LINE, 0, 0, tiled...]
    ppermute x6 -> x8, waiting for transfers between devices: 44.2 us -> 2.64 us  [swap(): return lax.ppermute(x, BLK, [(b, b ^ flip) for b in range(n)])]
    all_to_all x1, waiting for transfers between devices: 0.01 us -> 23.6 us  [per_device(): lax.all_to_all(outgoing.reshape(groups, slots, width), GRP, 0, 0, tiled=T...]
    all_to_all x0 -> x1, blocking collectives: none -> 15.7 us  [per_device(): done = lax.all_to_all(done, BLK, 0, 0, tiled=True)]
    all_gather x1 -> x0, blocking collectives: 6.65 us -> none  [per_device(): named_tiles = lax.all_gather(tile_rows, BLK, axis=0, tiled=True)]
    ppermute x6 -> x8, starting transfers between devices: 20.7 us -> 26.8 us  [swap(): return lax.ppermute(x, BLK, [(b, b ^ flip) for b in range(n)])]
    pallas_call x4 -> x1, Pallas kernels: 13.3 us -> 8.7 us  [ladder_call(): pl.pallas_call(body, grid_spec=pltpu.PrefetchScalarGridSpec(num_scalar_pr...]
    all_to_all x1, starting transfers between devices: 12.6 us -> 16.3 us  [per_device(): lax.all_to_all(x.reshape(ny * nz, nx * owned, width), PLANE, 0, 0, tiled=...]
  transfers between devices with their start and end apart: 8 -> 10, of which waited for: 3 -> 3; matrix products, arithmetic and copies ran while one was open for 3% -> 3% of each run, Pallas kernels for 13% -> 4%
where the time goes in v4:
time: 210 us; the launch traced here: 208 us
  blocking collectives  88.6 us (42%)
  starting transfers between devices  53.6 us (26%)
  waiting for transfers between devices  41.3 us (20%)
  Pallas kernels  16.4 us (8%)
  local copies, waits for them, and re-layouts  7.5 us (4%)
    all_to_all x1, blocking collectives, per_device(): lax.all_to_all(x.reshape(nx * nblk, sub, owned, width), LINE, 0, 0, tiled...  72.9 us
    ppermute x8, starting transfers between devices, swap(): return lax.ppermute(x, BLK, [(b, b ^ flip) for b in range(n)])  26.8 us
    all_to_all x1, waiting for transfers between devices, per_device(): lax.all_to_all(outgoing.reshape(groups, slots, width), GRP, 0, 0, tiled=T...  23.6 us
    all_to_all x1, starting transfers between devices, per_device(): lax.all_to_all(x.reshape(ny * nz, nx * owned, width), PLANE, 0, 0, tiled=...  16.3 us
    all_to_all x1, blocking collectives, per_device(): done = lax.all_to_all(done, BLK, 0, 0, tiled=True)  15.7 us
    all_to_all x1, waiting for transfers between devices, per_device(): lax.all_to_all(x.reshape(ny * nz, nx * owned, width), PLANE, 0, 0, tiled=...  15.1 us
    all_to_all x1, starting transfers between devices, per_device(): lax.all_to_all(outgoing.reshape(groups, slots, width), GRP, 0, 0, tiled=T...  10.5 us
    pallas_call x1, Pallas kernels, ladder_call(): pl.pallas_call(body, grid_spec=pltpu.PrefetchScalarGridSpec(num_scalar_pr...  8.7 us
  transfers between devices with their start and end apart: 10, of which 3 were waited for; matrix products, arithmetic and copies ran while one was open for 3% of the time, Pallas kernels for 4%

profile of v4, /device:TPU:1, one launch (start us, length us, event | category | flops | bytes accessed | tf_op | source)
XLA Modules:
  0.0 208.4 jit_solution(15239253454348534070)
XLA Ops:
  0.0 5.5 %collective-permute-start.2 = (f32[4,12,128,128]{3,2,1,0:T(8,128)}, f32[4,12,128,128]{3,2,1,0:T(8,128)}, u32[]{:S(2)}, u32[]{:S(2)}) collective-permute-start(f32[4,12,128,128]{3,2,1,0:T(8,128)} %refs_0_.1), channel_id=1, source_target_pairs={{0,2},{1,3},{2,0},{3,1},{4,6},{5,7},{6,4},{7,5},{8,10},{9,11},{10,... | collective-permute-start | bytes 9437192 | tf_op jit(solution)/shard_map/ppermute | solution.py:194
  5.5 1.2 reshape.57
  6.6 0.0 copy-start.2
  6.7 0.3 copy.29
  7.0 72.9 %all_to_all.20 = bf16[8,16,16,128]{3,2,1,0:T(8,128)(2,1)S(1)} all-to-all(bf16[8,16,16,128]{3,2,1,0:T(8,128)(2,1)S(1)} %bitcast.28), channel_id=1, replica_groups=mesh['y'=8,'xl'=2,'z'=8,'xh'=2,'k'=2] {'xl','xh','k'}, dimensions={0} | all-to-all | bytes 1048576 | tf_op jit(solution)/shard_map/all_to_all | solution.py:211
  79.9 0.8 copy.30
  80.8 16.3 %all-to-all-start.1 = ((bf16[64,32,128]{2,1,0:T(8,128)(2,1)}), bf16[64,32,128]{2,1,0:T(8,128)(2,1)S(1)}, u32[]{:S(2)}, u32[]{:S(2)}) async-start(bf16[64,32,128]{2,1,0:T(8,128)(2,1)} %bitcast.9), calls=%async_computation.1 | async-start | bytes 1048576 | tf_op jit(solution)/shard_map/all_to_all | solution.py:218
  97.1 0.0 copy-done.2
  97.1 0.1 reshape.53
  97.2 0.1 copy.35
  97.4 0.3 reshape.54.dest_ref
  97.7 0.7 rank.1
  98.4 15.1 %all-to-all-done.1 = bf16[64,32,128]{2,1,0:T(8,128)(2,1)S(1)} async-done(((bf16[64,32,128]{2,1,0:T(8,128)(2,1)}), bf16[64,32,128]{2,1,0:T(8,128)(2,1)S(1)}, u32[]{:S(2)}, u32[]{:S(2)}) %all-to-all-start.1) | async-done | bytes 524320 | tf_op jit(solution)/shard_map/all_to_all | solution.py:218
  113.5 5.9 %route.1 = bf16[8192,128]{1,0:T(8,128)(2,1)} custom-call(f32[128,2048]{1,0:T(8,128)S(1)} %get-tuple-element.9.slot_ref, f32[128,128]{1,0:T(8,128)S(1)} %get-tuple-element.10.early_ref, bf16[2048,128]{1,0:T(8,128)(2,1)S(1)} %bitcast.25), custom_call_target="tpu_custom_call" | custom-call | tf_op jit(solution)/shard_map/route/pallas_call | solution.py:91
  119.5 0.0 copy-start.4
  119.5 0.0 copy-start.3
  119.5 0.0 copy-start.1
  119.5 10.5 %all-to-all-start.2 = ((bf16[128,64,128]{2,1,0:T(8,128)(2,1)}), bf16[128,64,128]{2,1,0:T(8,128)(2,1)}, u32[]{:S(2)}, u32[]{:S(2)}) async-start(bf16[128,64,128]{2,1,0:T(8,128)(2,1)} %bitcast.11), calls=%async_computation.2 | async-start | bytes 4194304 | tf_op jit(solution)/shard_map/all_to_all | solution.py:224
  130.0 3.2 %collective-permute-start.3 = (f32[4,12,128,128]{3,2,1,0:T(8,128)}, f32[4,12,128,128]{3,2,1,0:T(8,128)}, u32[]{:S(2)}, u32[]{:S(2)}) collective-permute-start(f32[4,12,128,128]{3,2,1,0:T(8,128)} %refs_0_.1), channel_id=1, source_target_pairs={{0,1},{1,0},{2,3},{3,2},{4,5},{5,4},{6,7},{7,6},{8,9},{9,8},{10,11... | collective-permute-start | bytes 9437192 | tf_op jit(solution)/shard_map/ppermute | solution.py:194
  133.3 0.0 collective-permute-done.2.refs_1_
  133.3 1.9 collective-permute-start.4
  135.2 0.0 copy-done.4
  135.2 0.0 copy-done.3
  135.2 0.1 pad_maximum_fusion.2
  135.3 3.6 %collective-permute-start = (f32[4,256]{1,0:T(4,128)S(1)}, f32[4,256]{1,0:T(4,128)S(1)}, u32[]{:S(2)}, u32[]{:S(2)}) collective-permute-start(f32[4,256]{1,0:T(4,128)S(1)} %pad_maximum_fusion.2), channel_id=1, source_target_pairs={{0,2},{1,3},{2,0},{3,1},{4,6},{5,7},{6,4},{7,5},{8,10},{9,11},{10,... | collective-permute-start | bytes 12296 | tf_op jit(solution)/shard_map/ppermute | solution.py:194
  139.0 2.6 %collective-permute-done = f32[4,256]{1,0:T(4,128)S(1)} collective-permute-done((f32[4,256]{1,0:T(4,128)S(1)}, f32[4,256]{1,0:T(4,128)S(1)}, u32[]{:S(2)}, u32[]{:S(2)}) %collective-permute-start) | collective-permute-done | bytes 4128 | tf_op jit(solution)/shard_map/ppermute | solution.py:194
  141.6 0.1 pad_maximum_fusion.1
  141.7 3.2 %collective-permute-start.1 = (f32[8,256]{1,0:T(8,128)S(1)}, f32[8,256]{1,0:T(8,128)S(1)}, u32[]{:S(2)}, u32[]{:S(2)}) collective-permute-start(f32[8,256]{1,0:T(8,128)S(1)} %pad_maximum_fusion.1), channel_id=1, source_target_pairs={{0,1},{1,0},{2,3},{3,2},{4,5},{5,4},{6,7},{7,6},{8,9},{9,8},{10,11... | collective-permute-start | bytes 24584 | tf_op jit(solution)/shard_map/ppermute | solution.py:194
  144.9 0.0 copy-done.1
  144.9 0.1 constant_dynamic-slice_fusion
  145.0 3.4 %collective-permute-start.7 = (bf16[512,128]{1,0:T(8,128)(2,1)S(1)}, bf16[512,128]{1,0:T(8,128)(2,1)S(1)}, u32[]{:S(2)}, u32[]{:S(2)}) collective-permute-start(bf16[512,128]{1,0:T(8,128)(2,1)S(1)} %get-tuple-element.11), channel_id=1, source_target_pairs={{0,3},{1,2},{2,1},{3,0},{4,7},{5,6},{6,5},{7,4},{8,11},{9,10},{10,... | collective-permute-start | bytes 393224 | tf_op jit(solution)/shard_map/ppermute | solution.py:194
  148.5 3.2 %collective-permute-start.5 = (bf16[512,128]{1,0:T(8,128)(2,1)S(1)}, bf16[512,128]{1,0:T(8,128)(2,1)S(1)}, u32[]{:S(2)}, u32[]{:S(2)}) collective-permute-start(bf16[512,128]{1,0:T(8,128)(2,1)S(1)} %get-tuple-element.12), channel_id=1, source_target_pairs={{0,2},{1,3},{2,0},{3,1},{4,6},{5,7},{6,4},{7,5},{8,10},{9,11},{10,... | collective-permute-start | bytes 393224 | tf_op jit(solution)/shard_map/ppermute | solution.py:194
  151.7 0.0 collective-permute-done.1
  151.7 2.7 %collective-permute-start.6 = (bf16[512,128]{1,0:T(8,128)(2,1)S(1)}, bf16[512,128]{1,0:T(8,128)(2,1)S(1)}, u32[]{:S(2)}, u32[]{:S(2)}) collective-permute-start(bf16[512,128]{1,0:T(8,128)(2,1)S(1)} %get-tuple-element.14), channel_id=1, source_target_pairs={{0,1},{1,0},{2,3},{3,2},{4,5},{5,4},{6,7},{7,6},{8,9},{9,8},{10,11... | collective-permute-start | bytes 393224 | tf_op jit(solution)/shard_map/ppermute | solution.py:194
  154.4 0.1 pad_maximum_fusion
  154.5 0.1 copy.26
  154.6 0.4 select_reduce_fusion
  155.0 0.1 copy.28
  155.1 0.1 reshape.55.slot_ref
  155.2 23.6 %all-to-all-done.2 = bf16[128,64,128]{2,1,0:T(8,128)(2,1)} async-done(((bf16[128,64,128]{2,1,0:T(8,128)(2,1)}), bf16[128,64,128]{2,1,0:T(8,128)(2,1)}, u32[]{:S(2)}, u32[]{:S(2)}) %all-to-all-start.2) | async-done | bytes 2097184 | tf_op jit(solution)/shard_map/all_to_all | solution.py:224
  178.8 2.9 %copy.31 = bf16[64,4,2,2,8,128]{5,4,3,2,1,0:T(8,128)(2,1)S(1)} copy(bf16[64,4,2,2,8,128]{5,0,4,2,3,1:T(8,128)(2,1)} %bitcast.13) | data formatting | bytes 4194304 | tf_op jit(solution)/shard_map/transpose | solution.py:239
  181.7 0.0 copy-start
  181.7 1.1 turn.1.refs_4_
  182.8 0.0 collective-permute-done.7.refs_8_
  182.8 0.0 collective-permute-done.5.refs_6_
  182.8 0.0 collective-permute-done.6.refs_7_
  182.8 0.0 collective-permute-done.3.refs_2_
  182.8 0.0 collective-permute-done.4.refs_3_
  182.8 0.0 copy-done
  182.8 8.7 %ladder.1 = bf16[4,512,128]{2,1,0:T(8,128)(2,1)S(1)} custom-call(s32[192]{0:T(256)S(1)} %reshape.55.slot_ref, s32[1]{0:T(128)} %bitcast.4.blk_ref, f32[4,12,128,128]{3,2,1,0:T(8,128)} %refs_0_.1, f32[4,12,128,128]{3,2,1,0:T(8,128)} %collective-permute-done.2.refs_1_, f32[4,12,128,128]{3,2,1,0:T(8,128)} %collective-permute-done.3.refs_2_, ...), custom_call_target="tpu_custom_call" | custom-call | tf_op jit(solution)/shard_map/ladder/pallas_call | solution.py:172
  191.6 15.7 %all_to_all.21 = bf16[4,512,128]{2,1,0:T(8,128)(2,1)S(1)} all-to-all(bf16[4,512,128]{2,1,0:T(8,128)(2,1)S(1)} %ladder.1), channel_id=1, replica_groups=mesh['y'=8,'xl'=2,'z'=8,'xh'=2,'k'=2] {'xh','k'}, dimensions={0} | all-to-all | bytes 1048576 | tf_op jit(solution)/shard_map/all_to_all | solution.py:259
  207.2 0.2 copy.32
  207.4 1.0 copy.33
  (4 shorter events, 0.0 us)
Async XLA Ops:
  0.0 133.3 %collective-permute-start.2 = (f32[4,12,128,128]{3,2,1,0:T(8,128)}, f32[4,12,128,128]{3,2,1,0:T(8,128)}, u32[]{:S(2)}, u32[]{:S(2)}) collective-permute-start(f32[4,12,128,128]{3,2,1,0:T(8,128)} %refs_0_.1), channel_id=1, source_target_pairs={{0,2},{1,3},{2,0},{3,1},{4,6},{5,7},{6,4},{7,5},{8,10},{9,11},{10,... | collective-permute-start | bytes 9437192 | tf_op jit(solution)/shard_map/ppermute | solution.py:194
  6.6 90.5 %copy-start.2 = (s32[2048,4]{0,1:T(4,128)S(1)}, s32[2048,4]{0,1:T(4,128)}, u32[]{:S(2)}) copy-start(s32[2048,4]{0,1:T(4,128)} %param.10) | copy-start | bytes 98308
  80.8 32.8 %all-to-all-start.1 = ((bf16[64,32,128]{2,1,0:T(8,128)(2,1)}), bf16[64,32,128]{2,1,0:T(8,128)(2,1)S(1)}, u32[]{:S(2)}, u32[]{:S(2)}) async-start(bf16[64,32,128]{2,1,0:T(8,128)(2,1)} %bitcast.9), calls=%async_computation.1 | async-start | bytes 1048576 | tf_op jit(solution)/shard_map/all_to_all | solution.py:218
  119.5 15.7 %copy-start.4 = (s32[4,12]{1,0:T(4,128)S(1)}, s32[4,12]{1,0:T(4,128)}, u32[]{:S(2)}) copy-start(s32[4,12]{1,0:T(4,128)} %param.9) | copy-start | bytes 580
  119.5 15.7 %copy-start.3 = (f32[512]{0:T(512)S(1)}, f32[512]{0:T(512)}, u32[]{:S(2)}) copy-start(f32[512]{0:T(512)} %param.13) | copy-start | bytes 6148
  119.5 25.4 %copy-start.1 = (bf16[512,512]{1,0:T(8,128)(2,1)S(1)}, bf16[512,512]{1,0:T(8,128)(2,1)}, u32[]{:S(2)}) copy-start(bf16[512,512]{1,0:T(8,128)(2,1)} %param.11) | copy-start | bytes 1572868
  119.5 59.3 %all-to-all-start.2 = ((bf16[128,64,128]{2,1,0:T(8,128)(2,1)}), bf16[128,64,128]{2,1,0:T(8,128)(2,1)}, u32[]{:S(2)}, u32[]{:S(2)}) async-start(bf16[128,64,128]{2,1,0:T(8,128)(2,1)} %bitcast.11), calls=%async_computation.2 | async-start | bytes 4194304 | tf_op jit(solution)/shard_map/all_to_all | solution.py:224
  130.0 52.8 %collective-permute-start.3 = (f32[4,12,128,128]{3,2,1,0:T(8,128)}, f32[4,12,128,128]{3,2,1,0:T(8,128)}, u32[]{:S(2)}, u32[]{:S(2)}) collective-permute-start(f32[4,12,128,128]{3,2,1,0:T(8,128)} %refs_0_.1), channel_id=1, source_target_pairs={{0,1},{1,0},{2,3},{3,2},{4,5},{5,4},{6,7},{7,6},{8,9},{9,8},{10,11... | collective-permute-start | bytes 9437192 | tf_op jit(solution)/shard_map/ppermute | solution.py:194
  133.3 49.6 %collective-permute-start.4 = (f32[4,12,128,128]{3,2,1,0:T(8,128)}, f32[4,12,128,128]{3,2,1,0:T(8,128)}, u32[]{:S(2)}, u32[]{:S(2)}) collective-permute-start(f32[4,12,128,128]{3,2,1,0:T(8,128)} %collective-permute-done.2.refs_1_), channel_id=1, source_target_pairs={{0,1},{1,0},{2,3},{3,2},{4,5},{5,4},{6,7},{7,6},{8,9},{9,8},{10,11... | collective-permute-start | bytes 9437192 | tf_op jit(solution)/shard_map/ppermute | solution.py:194
  135.3 6.3 %collective-permute-start = (f32[4,256]{1,0:T(4,128)S(1)}, f32[4,256]{1,0:T(4,128)S(1)}, u32[]{:S(2)}, u32[]{:S(2)}) collective-permute-start(f32[4,256]{1,0:T(4,128)S(1)} %pad_maximum_fusion.2), channel_id=1, source_target_pairs={{0,2},{1,3},{2,0},{3,1},{4,6},{5,7},{6,4},{7,5},{8,10},{9,11},{10,... | collective-permute-start | bytes 12296 | tf_op jit(solution)/shard_map/ppermute | solution.py:194
  141.7 10.1 %collective-permute-start.1 = (f32[8,256]{1,0:T(8,128)S(1)}, f32[8,256]{1,0:T(8,128)S(1)}, u32[]{:S(2)}, u32[]{:S(2)}) collective-permute-start(f32[8,256]{1,0:T(8,128)S(1)} %pad_maximum_fusion.1), channel_id=1, source_target_pairs={{0,1},{1,0},{2,3},{3,2},{4,5},{5,4},{6,7},{7,6},{8,9},{9,8},{10,11... | collective-permute-start | bytes 24584 | tf_op jit(solution)/shard_map/ppermute | solution.py:194
  145.0 37.8 %collective-permute-start.7 = (bf16[512,128]{1,0:T(8,128)(2,1)S(1)}, bf16[512,128]{1,0:T(8,128)(2,1)S(1)}, u32[]{:S(2)}, u32[]{:S(2)}) collective-permute-start(bf16[512,128]{1,0:T(8,128)(2,1)S(1)} %get-tuple-element.11), channel_id=1, source_target_pairs={{0,3},{1,2},{2,1},{3,0},{4,7},{5,6},{6,5},{7,4},{8,11},{9,10},{10,... | collective-permute-start | bytes 393224 | tf_op jit(solution)/shard_map/ppermute | solution.py:194
  148.5 34.3 %collective-permute-start.5 = (bf16[512,128]{1,0:T(8,128)(2,1)S(1)}, bf16[512,128]{1,0:T(8,128)(2,1)S(1)}, u32[]{:S(2)}, u32[]{:S(2)}) collective-permute-start(bf16[512,128]{1,0:T(8,128)(2,1)S(1)} %get-tuple-element.12), channel_id=1, source_target_pairs={{0,2},{1,3},{2,0},{3,1},{4,6},{5,7},{6,4},{7,5},{8,10},{9,11},{10,... | collective-permute-start | bytes 393224 | tf_op jit(solution)/shard_map/ppermute | solution.py:194
  151.7 31.1 %collective-permute-start.6 = (bf16[512,128]{1,0:T(8,128)(2,1)S(1)}, bf16[512,128]{1,0:T(8,128)(2,1)S(1)}, u32[]{:S(2)}, u32[]{:S(2)}) collective-permute-start(bf16[512,128]{1,0:T(8,128)(2,1)S(1)} %get-tuple-element.14), channel_id=1, source_target_pairs={{0,1},{1,0},{2,3},{3,2},{4,5},{5,4},{6,7},{7,6},{8,9},{9,8},{10,11... | collective-permute-start | bytes 393224 | tf_op jit(solution)/shard_map/ppermute | solution.py:194
  181.7 1.1 copy-start

commit v5 on v4

--- a/solution.py
+++ b/solution.py
@@ -103,23 +103,50 @@
     )(slot, early, table)
 
 
-def turn_call(tiles):
-    slots, depth, width = tiles.shape
-    step = 8
+def cut_call(amplitudes, nx, nblk):
+    owned, rows, full_width = amplitudes.shape
+    sub = rows // nx
+    width = full_width // nblk
+
+    def body(a_ref, out_ref):
+        for h in range(nx):
+            for q in range(nblk):
+                part = a_ref[:, h * sub : (h + 1) * sub, q * width : (q + 1) * width]
+                out_ref[h * nblk + q] = jnp.swapaxes(part, 0, 1)
+
+    return pl.pallas_call(
+        body,
+        grid=(1,),
+        in_specs=[pl.BlockSpec(amplitudes.shape, lambda i: (0, 0, 0))],
+        out_specs=pl.BlockSpec((nx * nblk, sub, owned, width), lambda i: (0, 0, 0, 0)),
+        out_shape=jax.ShapeDtypeStruct((nx * nblk, sub, owned, width), BF),
+        compiler_params=PARAMS,
+        name="cut",
+    )(amplitudes)
+
+
+def turn_call(incoming, nblk, ny, nx, nz):
+    depth, slots, width = incoming.shape
+    step = 16
+    low = ny // nblk
 
     def body(t_ref, out_ref):
-        for i in range(step):
-            out_ref[i] = t_ref[i].T
+        x = t_ref[...].reshape(nblk, low, nx, nz, step, width)
+        order = [(b, y, h) for b in range(nblk) for h in range(nx) for y in range(low)]
+        x = jnp.concatenate([x[b, y, h] for b, y, h in order], axis=0)
+        x = jnp.swapaxes(x, 0, 1)
+        for j in range(step):
+            out_ref[j] = x[j].T
 
     return pl.pallas_call(
         body,
         grid=(slots // step,),
-        in_specs=[pl.BlockSpec((step, depth, width), lambda i: (i, 0, 0))],
+        in_specs=[pl.BlockSpec((depth, step, width), lambda i: (0, i, 0))],
         out_specs=pl.BlockSpec((step, width, depth), lambda i: (i, 0, 0)),
         out_shape=jax.ShapeDtypeStruct((slots, width, depth), BF),
         compiler_params=PARAMS,
         name="turn",
-    )(tiles)
+    )(incoming)
 
 
 def ladder_call(slot, blk, flips, weights, turned, sources, occ, virt):
@@ -207,8 +234,8 @@
     slots = all_tiles * dest // groups
     columns, listed, _, size = integrals.shape
 
-    x = amplitudes.reshape(owned, nx, sub, nblk, width).transpose(1, 3, 2, 0, 4)
-    x = lax.all_to_all(x.reshape(nx * nblk, sub, owned, width), LINE, 0, 0, tiled=True)
+    x = cut_call(amplitudes, nx, nblk)
+    x = lax.all_to_all(x, LINE, 0, 0, tiled=True)
     facts = [virt_energy.reshape(columns, size), tile_rows.astype(F32)]
     facts.append(jnp.zeros((columns, size - listed), F32))
     facts = jnp.concatenate(facts, axis=1)
@@ -236,8 +263,7 @@
     slot = slot.reshape(-1)
     diagonal = swap(across, 1, nblk)
 
-    tiles = incoming.reshape(nblk, ny // nblk, nx, nz, slots, width).transpose(4, 0, 2, 1, 3, 5)
-    turned = turn_call(tiles.reshape(slots, rows * nblk, width))
+    turned = turn_call(incoming, nblk, ny, nx, nz)
 
     def quarter(flip):
         return lax.dynamic_slice_in_dim(source_terms, (blk ^ flip) * width, width, 1)

time: 210 us -> 207 us (0.986)
  local copies, waits for them, and re-layouts: 7.5 us -> 4.09 us
    transpose x2 -> x0, local copies, waits for them, and re-layouts: 3.29 us -> none  [the longest x1 2.94 us: per_device(): incoming.reshape(nblk, ny // nblk, nx, nz, slots, width)]
  transfers between devices with their start and end apart: 10 -> 10, of which waited for: 3 -> 3; matrix products, arithmetic and copies ran while one was open for 3% -> 1% of each run, Pallas kernels for 4% -> 4%
where the time goes in v5:
time: 207 us; the launch traced here: 206 us
  blocking collectives  88.9 us (43%)
  starting transfers between devices  52.7 us (25%)
  waiting for transfers between devices  42.2 us (20%)
  Pallas kernels  16.8 us (8%)
  local copies, waits for them, and re-layouts  4.09 us (2%)
    all_to_all x1, blocking collectives, per_device(): x = lax.all_to_all(x, LINE, 0, 0, tiled=True)  73.3 us
    ppermute x8, starting transfers between devices, swap(): return lax.ppermute(x, BLK, [(b, b ^ flip) for b in range(n)])  26.4 us
    all_to_all x1, waiting for transfers between devices, per_device(): lax.all_to_all(outgoing.reshape(groups, slots, width), GRP, 0, 0, tiled=T...  24.1 us
    all_to_all x1, starting transfers between devices, per_device(): lax.all_to_all(x.reshape(ny * nz, nx * owned, width), PLANE, 0, 0, tiled=...  16.3 us
    all_to_all x1, blocking collectives, per_device(): done = lax.all_to_all(done, BLK, 0, 0, tiled=True)  15.7 us
    all_to_all x1, waiting for transfers between devices, per_device(): lax.all_to_all(x.reshape(ny * nz, nx * owned, width), PLANE, 0, 0, tiled=...  15.1 us
    all_to_all x1, starting transfers between devices, per_device(): lax.all_to_all(outgoing.reshape(groups, slots, width), GRP, 0, 0, tiled=T...  9.97 us
    pallas_call x1, Pallas kernels, ladder_call(): pl.pallas_call(body, grid_spec=pltpu.PrefetchScalarGridSpec(num_scalar_pr...  8.7 us
  transfers between devices with their start and end apart: 10, of which 3 were waited for; matrix products, arithmetic and copies ran while one was open for 1% of the time, Pallas kernels for 4%

profile of v5, /device:TPU:1, one launch (start us, length us, event | category | flops | bytes accessed | tf_op | source)
XLA Modules:
  0.0 205.7 jit_solution(3790051200378805608)
XLA Ops:
  0.0 5.5 %collective-permute-start.2 = (f32[4,12,128,128]{3,2,1,0:T(8,128)}, f32[4,12,128,128]{3,2,1,0:T(8,128)}, u32[]{:S(2)}, u32[]{:S(2)}) collective-permute-start(f32[4,12,128,128]{3,2,1,0:T(8,128)} %refs_0_.1), channel_id=1, source_target_pairs={{0,2},{1,3},{2,0},{3,1},{4,6},{5,7},{6,4},{7,5},{8,10},{9,11},{10,... | collective-permute-start | bytes 9437192 | tf_op jit(solution)/shard_map/ppermute | solution.py:221
  5.5 0.0 copy-start
  5.5 1.0 copy-done
  6.5 0.0 copy-start.3
  6.5 0.2 cut.1
  6.7 73.3 %all_to_all.20 = bf16[8,16,16,128]{3,2,1,0:T(8,128)(2,1)S(1)} all-to-all(bf16[8,16,16,128]{3,2,1,0:T(8,128)(2,1)S(1)} %cut.1), channel_id=1, replica_groups=mesh['y'=8,'xl'=2,'z'=8,'xh'=2,'k'=2] {'xl','xh','k'}, dimensions={0} | all-to-all | bytes 1048576 | tf_op jit(solution)/shard_map/all_to_all | solution.py:238
  79.9 0.8 copy.22
  80.8 16.3 %all-to-all-start.1 = ((bf16[64,32,128]{2,1,0:T(8,128)(2,1)}), bf16[64,32,128]{2,1,0:T(8,128)(2,1)S(1)}, u32[]{:S(2)}, u32[]{:S(2)}) async-start(bf16[64,32,128]{2,1,0:T(8,128)(2,1)} %bitcast.7), calls=%async_computation.1 | async-start | bytes 1048576 | tf_op jit(solution)/shard_map/all_to_all | solution.py:245
  97.1 0.0 copy-done.3
  97.1 0.1 reshape.41
  97.2 0.1 copy.26
  97.4 0.3 reshape.42.dest_ref
  97.7 0.7 rank.1
  98.4 15.1 %all-to-all-done.1 = bf16[64,32,128]{2,1,0:T(8,128)(2,1)S(1)} async-done(((bf16[64,32,128]{2,1,0:T(8,128)(2,1)}), bf16[64,32,128]{2,1,0:T(8,128)(2,1)S(1)}, u32[]{:S(2)}, u32[]{:S(2)}) %all-to-all-start.1) | async-done | bytes 524320 | tf_op jit(solution)/shard_map/all_to_all | solution.py:245
  113.5 5.9 %route.1 = bf16[8192,128]{1,0:T(8,128)(2,1)} custom-call(f32[128,2048]{1,0:T(8,128)S(1)} %get-tuple-element.9.slot_ref, f32[128,128]{1,0:T(8,128)S(1)} %get-tuple-element.10.early_ref, bf16[2048,128]{1,0:T(8,128)(2,1)S(1)} %bitcast.18), custom_call_target="tpu_custom_call" | custom-call | tf_op jit(solution)/shard_map/route/pallas_call | solution.py:91
  119.5 0.0 copy-start.5
  119.5 0.0 copy-start.4
  119.5 0.0 copy-start.2
  119.5 10.0 %all-to-all-start.2 = ((bf16[128,64,128]{2,1,0:T(8,128)(2,1)}), bf16[128,64,128]{2,1,0:T(8,128)(2,1)S(1)}, u32[]{:S(2)}, u32[]{:S(2)}) async-start(bf16[128,64,128]{2,1,0:T(8,128)(2,1)} %bitcast.9), calls=%async_computation.2 | async-start | bytes 4194304 | tf_op jit(solution)/shard_map/all_to_all | solution.py:251
  129.5 3.2 %collective-permute-start.3 = (f32[4,12,128,128]{3,2,1,0:T(8,128)}, f32[4,12,128,128]{3,2,1,0:T(8,128)}, u32[]{:S(2)}, u32[]{:S(2)}) collective-permute-start(f32[4,12,128,128]{3,2,1,0:T(8,128)} %refs_0_.1), channel_id=1, source_target_pairs={{0,1},{1,0},{2,3},{3,2},{4,5},{5,4},{6,7},{7,6},{8,9},{9,8},{10,11... | collective-permute-start | bytes 9437192 | tf_op jit(solution)/shard_map/ppermute | solution.py:221
  132.7 0.0 collective-permute-done.2.refs_1_
  132.7 1.9 collective-permute-start.4
  134.6 0.0 copy-done.5
  134.7 0.0 copy-done.4
  134.7 0.1 pad_maximum_fusion.2
  134.8 3.6 %collective-permute-start = (f32[4,256]{1,0:T(4,128)S(1)}, f32[4,256]{1,0:T(4,128)S(1)}, u32[]{:S(2)}, u32[]{:S(2)}) collective-permute-start(f32[4,256]{1,0:T(4,128)S(1)} %pad_maximum_fusion.2), channel_id=1, source_target_pairs={{0,2},{1,3},{2,0},{3,1},{4,6},{5,7},{6,4},{7,5},{8,10},{9,11},{10,... | collective-permute-start | bytes 12296 | tf_op jit(solution)/shard_map/ppermute | solution.py:221
  138.4 2.9 %collective-permute-done = f32[4,256]{1,0:T(4,128)S(1)} collective-permute-done((f32[4,256]{1,0:T(4,128)S(1)}, f32[4,256]{1,0:T(4,128)S(1)}, u32[]{:S(2)}, u32[]{:S(2)}) %collective-permute-start) | collective-permute-done | bytes 4128 | tf_op jit(solution)/shard_map/ppermute | solution.py:221
  141.3 0.1 pad_maximum_fusion.1
  141.4 2.8 %collective-permute-start.1 = (f32[8,256]{1,0:T(8,128)S(1)}, f32[8,256]{1,0:T(8,128)S(1)}, u32[]{:S(2)}, u32[]{:S(2)}) collective-permute-start(f32[8,256]{1,0:T(8,128)S(1)} %pad_maximum_fusion.1), channel_id=1, source_target_pairs={{0,1},{1,0},{2,3},{3,2},{4,5},{5,4},{6,7},{7,6},{8,9},{9,8},{10,11... | collective-permute-start | bytes 24584 | tf_op jit(solution)/shard_map/ppermute | solution.py:221
  144.2 0.0 copy-done.2
  144.2 0.1 constant_dynamic-slice_fusion
  144.4 3.5 %collective-permute-start.7 = (bf16[512,128]{1,0:T(8,128)(2,1)S(1)}, bf16[512,128]{1,0:T(8,128)(2,1)S(1)}, u32[]{:S(2)}, u32[]{:S(2)}) collective-permute-start(bf16[512,128]{1,0:T(8,128)(2,1)S(1)} %get-tuple-element.11), channel_id=1, source_target_pairs={{0,3},{1,2},{2,1},{3,0},{4,7},{5,6},{6,5},{7,4},{8,11},{9,10},{10,... | collective-permute-start | bytes 393224 | tf_op jit(solution)/shard_map/ppermute | solution.py:221
  147.9 3.2 %collective-permute-start.5 = (bf16[512,128]{1,0:T(8,128)(2,1)S(1)}, bf16[512,128]{1,0:T(8,128)(2,1)S(1)}, u32[]{:S(2)}, u32[]{:S(2)}) collective-permute-start(bf16[512,128]{1,0:T(8,128)(2,1)S(1)} %get-tuple-element.12), channel_id=1, source_target_pairs={{0,2},{1,3},{2,0},{3,1},{4,6},{5,7},{6,4},{7,5},{8,10},{9,11},{10,... | collective-permute-start | bytes 393224 | tf_op jit(solution)/shard_map/ppermute | solution.py:221
  151.1 0.0 collective-permute-done.1
  151.1 2.7 %collective-permute-start.6 = (bf16[512,128]{1,0:T(8,128)(2,1)S(1)}, bf16[512,128]{1,0:T(8,128)(2,1)S(1)}, u32[]{:S(2)}, u32[]{:S(2)}) collective-permute-start(bf16[512,128]{1,0:T(8,128)(2,1)S(1)} %get-tuple-element.14), channel_id=1, source_target_pairs={{0,1},{1,0},{2,3},{3,2},{4,5},{5,4},{6,7},{7,6},{8,9},{9,8},{10,11... | collective-permute-start | bytes 393224 | tf_op jit(solution)/shard_map/ppermute | solution.py:221
  153.8 0.1 pad_maximum_fusion
  153.9 0.1 copy.19
  154.0 0.4 select_reduce_fusion
  154.4 0.1 copy.21
  154.5 0.1 reshape.43.slot_ref
  154.5 0.0 copy-start.1
  154.6 24.1 %all-to-all-done.2.t_ref = bf16[128,64,128]{2,1,0:T(8,128)(2,1)S(1)} async-done(((bf16[128,64,128]{2,1,0:T(8,128)(2,1)}), bf16[128,64,128]{2,1,0:T(8,128)(2,1)S(1)}, u32[]{:S(2)}, u32[]{:S(2)}) %all-to-all-start.2) | async-done | bytes 2097184 | tf_op jit(solution)/shard_map/all_to_all | solution.py:251
  178.6 1.4 turn.1.refs_4_
  180.0 0.0 collective-permute-done.7.refs_8_
  180.0 0.0 collective-permute-done.5.refs_6_
  180.0 0.0 collective-permute-done.6.refs_7_
  180.1 0.0 collective-permute-done.3.refs_2_
  180.1 0.0 collective-permute-done.4.refs_3_
  180.1 0.0 copy-done.1
  180.1 8.7 %ladder.1 = bf16[4,512,128]{2,1,0:T(8,128)(2,1)S(1)} custom-call(s32[192]{0:T(256)S(1)} %reshape.43.slot_ref, s32[1]{0:T(128)} %bitcast.4.blk_ref, f32[4,12,128,128]{3,2,1,0:T(8,128)} %refs_0_.1, f32[4,12,128,128]{3,2,1,0:T(8,128)} %collective-permute-done.2.refs_1_, f32[4,12,128,128]{3,2,1,0:T(8,128)} %collective-permute-done.3.refs_2_, ...), custom_call_target="tpu_custom_call" | custom-call | tf_op jit(solution)/shard_map/ladder/pallas_call | solution.py:199
  188.8 15.7 %all_to_all.21 = bf16[4,512,128]{2,1,0:T(8,128)(2,1)S(1)} all-to-all(bf16[4,512,128]{2,1,0:T(8,128)(2,1)S(1)} %ladder.1), channel_id=1, replica_groups=mesh['y'=8,'xl'=2,'z'=8,'xh'=2,'k'=2] {'xh','k'}, dimensions={0} | all-to-all | bytes 1048576 | tf_op jit(solution)/shard_map/all_to_all | solution.py:285
  204.4 0.2 copy.23
  204.7 1.0 copy.24
  (4 shorter events, 0.0 us)
Async XLA Ops:
  0.0 132.7 %collective-permute-start.2 = (f32[4,12,128,128]{3,2,1,0:T(8,128)}, f32[4,12,128,128]{3,2,1,0:T(8,128)}, u32[]{:S(2)}, u32[]{:S(2)}) collective-permute-start(f32[4,12,128,128]{3,2,1,0:T(8,128)} %refs_0_.1), channel_id=1, source_target_pairs={{0,2},{1,3},{2,0},{3,1},{4,6},{5,7},{6,4},{7,5},{8,10},{9,11},{10,... | collective-permute-start | bytes 9437192 | tf_op jit(solution)/shard_map/ppermute | solution.py:221
  5.5 1.0 copy-start
  6.5 90.6 %copy-start.3 = (s32[2048,4]{0,1:T(4,128)S(1)}, s32[2048,4]{0,1:T(4,128)}, u32[]{:S(2)}) copy-start(s32[2048,4]{0,1:T(4,128)} %param.10) | copy-start | bytes 98308
  80.8 32.8 %all-to-all-start.1 = ((bf16[64,32,128]{2,1,0:T(8,128)(2,1)}), bf16[64,32,128]{2,1,0:T(8,128)(2,1)S(1)}, u32[]{:S(2)}, u32[]{:S(2)}) async-start(bf16[64,32,128]{2,1,0:T(8,128)(2,1)} %bitcast.7), calls=%async_computation.1 | async-start | bytes 1048576 | tf_op jit(solution)/shard_map/all_to_all | solution.py:245
  119.5 15.2 %copy-start.5 = (s32[4,12]{1,0:T(4,128)S(1)}, s32[4,12]{1,0:T(4,128)}, u32[]{:S(2)}) copy-start(s32[4,12]{1,0:T(4,128)} %param.9) | copy-start | bytes 580
  119.5 15.2 %copy-start.4 = (f32[512]{0:T(512)S(1)}, f32[512]{0:T(512)}, u32[]{:S(2)}) copy-start(f32[512]{0:T(512)} %param.13) | copy-start | bytes 6148
  119.5 24.8 %copy-start.2 = (bf16[512,512]{1,0:T(8,128)(2,1)S(1)}, bf16[512,512]{1,0:T(8,128)(2,1)}, u32[]{:S(2)}) copy-start(bf16[512,512]{1,0:T(8,128)(2,1)} %param.11) | copy-start | bytes 1572868
  119.5 59.2 %all-to-all-start.2 = ((bf16[128,64,128]{2,1,0:T(8,128)(2,1)}), bf16[128,64,128]{2,1,0:T(8,128)(2,1)S(1)}, u32[]{:S(2)}, u32[]{:S(2)}) async-start(bf16[128,64,128]{2,1,0:T(8,128)(2,1)} %bitcast.9), calls=%async_computation.2 | async-start | bytes 4194304 | tf_op jit(solution)/shard_map/all_to_all | solution.py:251
  129.5 50.6 %collective-permute-start.3 = (f32[4,12,128,128]{3,2,1,0:T(8,128)}, f32[4,12,128,128]{3,2,1,0:T(8,128)}, u32[]{:S(2)}, u32[]{:S(2)}) collective-permute-start(f32[4,12,128,128]{3,2,1,0:T(8,128)} %refs_0_.1), channel_id=1, source_target_pairs={{0,1},{1,0},{2,3},{3,2},{4,5},{5,4},{6,7},{7,6},{8,9},{9,8},{10,11... | collective-permute-start | bytes 9437192 | tf_op jit(solution)/shard_map/ppermute | solution.py:221
  132.7 47.4 %collective-permute-start.4 = (f32[4,12,128,128]{3,2,1,0:T(8,128)}, f32[4,12,128,128]{3,2,1,0:T(8,128)}, u32[]{:S(2)}, u32[]{:S(2)}) collective-permute-start(f32[4,12,128,128]{3,2,1,0:T(8,128)} %collective-permute-done.2.refs_1_), channel_id=1, source_target_pairs={{0,1},{1,0},{2,3},{3,2},{4,5},{5,4},{6,7},{7,6},{8,9},{9,8},{10,11... | collective-permute-start | bytes 9437192 | tf_op jit(solution)/shard_map/ppermute | solution.py:221
  134.8 6.5 %collective-permute-start = (f32[4,256]{1,0:T(4,128)S(1)}, f32[4,256]{1,0:T(4,128)S(1)}, u32[]{:S(2)}, u32[]{:S(2)}) collective-permute-start(f32[4,256]{1,0:T(4,128)S(1)} %pad_maximum_fusion.2), channel_id=1, source_target_pairs={{0,2},{1,3},{2,0},{3,1},{4,6},{5,7},{6,4},{7,5},{8,10},{9,11},{10,... | collective-permute-start | bytes 12296 | tf_op jit(solution)/shard_map/ppermute | solution.py:221
  141.4 9.7 %collective-permute-start.1 = (f32[8,256]{1,0:T(8,128)S(1)}, f32[8,256]{1,0:T(8,128)S(1)}, u32[]{:S(2)}, u32[]{:S(2)}) collective-permute-start(f32[8,256]{1,0:T(8,128)S(1)} %pad_maximum_fusion.1), channel_id=1, source_target_pairs={{0,1},{1,0},{2,3},{3,2},{4,5},{5,4},{6,7},{7,6},{8,9},{9,8},{10,11... | collective-permute-start | bytes 24584 | tf_op jit(solution)/shard_map/ppermute | solution.py:221
  144.4 35.7 %collective-permute-start.7 = (bf16[512,128]{1,0:T(8,128)(2,1)S(1)}, bf16[512,128]{1,0:T(8,128)(2,1)S(1)}, u32[]{:S(2)}, u32[]{:S(2)}) collective-permute-start(bf16[512,128]{1,0:T(8,128)(2,1)S(1)} %get-tuple-element.11), channel_id=1, source_target_pairs={{0,3},{1,2},{2,1},{3,0},{4,7},{5,6},{6,5},{7,4},{8,11},{9,10},{10,... | collective-permute-start | bytes 393224 | tf_op jit(solution)/shard_map/ppermute | solution.py:221
  147.9 32.2 %collective-permute-start.5 = (bf16[512,128]{1,0:T(8,128)(2,1)S(1)}, bf16[512,128]{1,0:T(8,128)(2,1)S(1)}, u32[]{:S(2)}, u32[]{:S(2)}) collective-permute-start(bf16[512,128]{1,0:T(8,128)(2,1)S(1)} %get-tuple-element.12), channel_id=1, source_target_pairs={{0,2},{1,3},{2,0},{3,1},{4,6},{5,7},{6,4},{7,5},{8,10},{9,11},{10,... | collective-permute-start | bytes 393224 | tf_op jit(solution)/shard_map/ppermute | solution.py:221
  151.1 29.0 %collective-permute-start.6 = (bf16[512,128]{1,0:T(8,128)(2,1)S(1)}, bf16[512,128]{1,0:T(8,128)(2,1)S(1)}, u32[]{:S(2)}, u32[]{:S(2)}) collective-permute-start(bf16[512,128]{1,0:T(8,128)(2,1)S(1)} %get-tuple-element.14), channel_id=1, source_target_pairs={{0,1},{1,0},{2,3},{3,2},{4,5},{5,4},{6,7},{7,6},{8,9},{9,8},{10,11... | collective-permute-start | bytes 393224 | tf_op jit(solution)/shard_map/ppermute | solution.py:221
  154.5 25.5 %copy-start.1 = (f32[512]{0:T(512)S(1)}, f32[512]{0:T(512)}, u32[]{:S(2)}) copy-start(f32[512]{0:T(512)} %param.12) | copy-start | bytes 6148

commit v6 on v5

--- a/solution.py
+++ b/solution.py
@@ -13,6 +13,8 @@
 BF = jnp.bfloat16
 F32 = jnp.float32
 PARAMS = pltpu.CompilerParams(vmem_limit_bytes=48 * 1024 * 1024)
+WIDE = pltpu.CompilerParams(vmem_limit_bytes=46 * 1024 * 1024)
+FULL = pltpu.CompilerParams(vmem_limit_bytes=67043328)
 
 
 def rank_call(own, dest, groups):
@@ -108,19 +110,29 @@
     sub = rows // nx
     width = full_width // nblk
 
-    def body(a_ref, out_ref):
-        for h in range(nx):
-            for q in range(nblk):
-                part = a_ref[:, h * sub : (h + 1) * sub, q * width : (q + 1) * width]
-                out_ref[h * nblk + q] = jnp.swapaxes(part, 0, 1)
+    def body(a_ref, out_ref, held_ref, sems):
+        def load(q):
+            part = a_ref.at[:, :, pl.ds(q * width, width)]
+            return pltpu.make_async_copy(part, held_ref.at[q], sems.at[q])
+
+        for q in range(nblk):
+            load(q).start()
+        for q in range(nblk):
+            load(q).wait()
+            for h in range(nx):
+                out_ref[h * nblk + q] = jnp.swapaxes(held_ref[q, :, h * sub : (h + 1) * sub, :], 0, 1)
 
     return pl.pallas_call(
         body,
         grid=(1,),
-        in_specs=[pl.BlockSpec(amplitudes.shape, lambda i: (0, 0, 0))],
+        in_specs=[pl.BlockSpec(memory_space=pl.ANY)],
         out_specs=pl.BlockSpec((nx * nblk, sub, owned, width), lambda i: (0, 0, 0, 0)),
         out_shape=jax.ShapeDtypeStruct((nx * nblk, sub, owned, width), BF),
-        compiler_params=PARAMS,
+        scratch_shapes=[
+            pltpu.VMEM((nblk, owned, rows, width), BF),
+            pltpu.SemaphoreType.DMA((nblk,)),
+        ],
+        compiler_params=FULL,
         name="cut",
     )(amplitudes)
 
@@ -149,32 +161,38 @@
     )(incoming)
 
 
-def ladder_call(slot, blk, flips, weights, turned, sources, occ, virt):
+def ladder_call(slot, blk, first, weights, turned, sources, occ, virt, ready=None, places=None):
     columns, listed, depth, size = weights[0].shape
     width = turned.shape[1]
     owners = len(weights)
     some = 2
+    total = owners if places is None else len(places)
 
     def body(slot_ref, blk_ref, *refs):
         w_refs = refs[:owners]
         t_ref = refs[owners]
         s_refs = refs[owners + 1 : 2 * owners + 1]
-        o_ref, v_ref, out_ref, held_ref, sems = refs[2 * owners + 1 :]
+        o_ref, v_ref = refs[2 * owners + 1 : 2 * owners + 3]
+        out_ref, held_ref, sems = refs[-3:]
         for m in range(owners):
             for n in range(columns):
                 at = m * columns + n
                 pltpu.make_async_copy(w_refs[m].at[n], held_ref.at[at], sems.at[at]).start()
+        if places is not None:
+            for m in range(first):
+                out_ref[blk_ref[0] ^ places[m]] = refs[-4][m]
         for m in range(owners):
-            to = blk_ref[0] ^ flips[m]
+            to = m if places is None else blk_ref[0] ^ places[first + m]
 
             def some_columns(i, _, m=m, to=to):
                 for u in range(some):
                     n = i * some + u
                     at = m * columns + n
+                    named = first * columns + at
                     pltpu.make_async_copy(w_refs[m].at[n], held_ref.at[at], sems.at[at]).wait()
                     right, left = [], []
                     for r in range(listed):
-                        s = slot_ref[at * listed + r]
+                        s = slot_ref[named * listed + r]
                         w = held_ref[at, r]
                         hi = w.astype(BF)
                         lo = (w - hi.astype(F32)).astype(BF)
@@ -186,9 +204,9 @@
                     acc = jnp.dot(left, right, preferred_element_type=F32)
                     part = (acc[:, :size] + acc[:, size:]).T
                     rows = pl.ds(n * size, size)
-                    total = s_refs[m][rows, :].astype(F32) + part
-                    v = jnp.broadcast_to(v_ref[pl.ds(at, 1), :], (size, size)).T
-                    out_ref[to, rows, :] = (total / (v + o_ref[...])).astype(BF)
+                    summed = s_refs[m][rows, :].astype(F32) + part
+                    v = jnp.broadcast_to(v_ref[pl.ds(named, 1), :], (size, size)).T
+                    out_ref[to, rows, :] = (summed / (v + o_ref[...])).astype(BF)
                 return 0
 
             lax.fori_loop(0, columns // some, some_columns, 0)
@@ -196,6 +214,7 @@
     def whole(x):
         return pl.BlockSpec(x.shape, lambda i, s, b: (0,) * x.ndim)
 
+    extra = () if ready is None else (ready,)
     return pl.pallas_call(
         body,
         grid_spec=pltpu.PrefetchScalarGridSpec(
@@ -204,17 +223,18 @@
             in_specs=[pl.BlockSpec(memory_space=pl.ANY)] * owners
             + [whole(turned)]
             + [whole(x) for x in sources]
-            + [pl.BlockSpec((1, width), lambda i, s, b: (0, b[0])), whole(virt)],
-            out_specs=pl.BlockSpec((owners, columns * size, width), lambda i, s, b: (0, 0, 0)),
+            + [pl.BlockSpec((1, width), lambda i, s, b: (0, b[0])), whole(virt)]
+            + [whole(x) for x in extra],
+            out_specs=pl.BlockSpec((total, columns * size, width), lambda i, s, b: (0, 0, 0)),
             scratch_shapes=[
                 pltpu.VMEM((owners * columns, listed, depth, size), F32),
                 pltpu.SemaphoreType.DMA((owners * columns,)),
             ],
         ),
-        out_shape=jax.ShapeDtypeStruct((owners, columns * size, width), BF),
-        compiler_params=pltpu.CompilerParams(vmem_limit_bytes=48 * 1024 * 1024),
+        out_shape=jax.ShapeDtypeStruct((total, columns * size, width), BF),
+        compiler_params=WIDE,
         name="ladder",
-    )(slot, blk, *weights, turned, *sources, occ, virt)
+    )(slot, blk, *weights, turned, *sources, occ, virt, *extra)
 
 
 def swap(x, flip, n):
@@ -251,8 +271,9 @@
     incoming = lax.all_to_all(outgoing.reshape(groups, slots, width), GRP, 0, 0, tiled=True)
 
     beside = swap(integrals, 1, nblk)
-    facts = jnp.concatenate([facts, facts_across], axis=0)
-    facts = jnp.concatenate([facts, swap(facts, 1, nblk)], axis=0)
+    pair = jnp.concatenate([facts, facts_across], axis=0)
+    other = swap(pair, 1, nblk)
+    facts = jnp.concatenate([facts, other[:columns], facts_across, other[columns:]], axis=0)
     named_tiles = facts[:, size : size + listed].astype(jnp.int32)
     y_of = named_tiles // (nx * nz * owned)
     x_of = (named_tiles // (nz * owned)) % nx
@@ -272,15 +293,23 @@
     source_near = swap(quarter(1), 1, nblk)
     source_diagonal = swap(quarter(3), 3, nblk)
 
+    occ = occ_energy.reshape(1, full_width)
+    virt = facts[:, :size]
+    mine = blk.reshape(1)
+    local = ladder_call(
+        slot, mine, 0, (integrals, beside), turned, (quarter(0), source_near), occ, virt
+    )
     done = ladder_call(
         slot,
-        blk.reshape(1),
-        (0, 2, 1, 3),
-        (integrals, across, beside, diagonal),
+        mine,
+        2,
+        (across, diagonal),
         turned,
-        (quarter(0), source_far, source_near, source_diagonal),
-        occ_energy.reshape(1, full_width),
-        facts[:, :size],
+        (source_far, source_diagonal),
+        occ,
+        virt,
+        ready=local,
+        places=(0, 1, 2, 3),
     )
     done = lax.all_to_all(done, BLK, 0, 0, tiled=True)
     return done.transpose(1, 0, 2).reshape(columns * size, full_width)
@@ -299,6 +328,4 @@
         P(),
         P(every),
     )
-    return jax.shard_map(
-        per_device, mesh=fine, in_specs=in_specs, out_specs=P(every, None), check_vma=False
-    )
+    return jax.shard_map(per_device, mesh=fine, in_specs=in_specs, out_specs=P(every, None), check_vma=False)

time: 207 us -> 208 us (level)
  Pallas kernels: 16.8 us -> 19.4 us
    pallas_call x1 -> x2, Pallas kernels: 8.7 us -> 9.47 us  [ladder_call(): pl.pallas_call(body, grid_spec=pltpu.PrefetchScalarGridSpec(num_scalar_pr...]
  transfers between devices with their start and end apart: 10 -> 10, of which waited for: 3 -> 3; matrix products, arithmetic and copies ran while one was open for 1% -> 1% of each run, Pallas kernels for 4% -> 7%
where the time goes in v6:
time: 208 us; the launch traced here: 207 us
  blocking collectives  88.1 us (42%)
  starting transfers between devices  52.7 us (25%)
  waiting for transfers between devices  42.1 us (20%)
  Pallas kernels  19.4 us (9%)
  local copies, waits for them, and re-layouts  3.54 us (2%)
    all_to_all x1, blocking collectives, per_device(): x = lax.all_to_all(x, LINE, 0, 0, tiled=True)  72.5 us
    ppermute x8, starting transfers between devices, swap(): return lax.ppermute(x, BLK, [(b, b ^ flip) for b in range(n)])  26.4 us
    all_to_all x1, waiting for transfers between devices, per_device(): lax.all_to_all(outgoing.reshape(groups, slots, width), GRP, 0, 0, tiled=T...  24.1 us
    all_to_all x1, starting transfers between devices, per_device(): lax.all_to_all(x.reshape(ny * nz, nx * owned, width), PLANE, 0, 0, tiled=...  16.3 us
    all_to_all x1, blocking collectives, per_device(): done = lax.all_to_all(done, BLK, 0, 0, tiled=True)  15.6 us
    all_to_all x1, waiting for transfers between devices, per_device(): lax.all_to_all(x.reshape(ny * nz, nx * owned, width), PLANE, 0, 0, tiled=...  15.1 us
    all_to_all x1, starting transfers between devices, per_device(): lax.all_to_all(outgoing.reshape(groups, slots, width), GRP, 0, 0, tiled=T...  9.97 us
    pallas_call x2, Pallas kernels, ladder_call(): pl.pallas_call(body, grid_spec=pltpu.PrefetchScalarGridSpec(num_scalar_pr...  9.47 us
  transfers between devices with their start and end apart: 10, of which 3 were waited for; matrix products, arithmetic and copies ran while one was open for 1% of the time, Pallas kernels for 7%

profile of v6, /device:TPU:1, one launch (start us, length us, event | category | flops | bytes accessed | tf_op | source)
XLA Modules:
  0.0 206.9 jit_solution(8682585439414814406)
XLA Ops:
  0.0 5.5 %collective-permute-start.2 = (f32[4,12,128,128]{3,2,1,0:T(8,128)}, f32[4,12,128,128]{3,2,1,0:T(8,128)}, u32[]{:S(2)}, u32[]{:S(2)}) collective-permute-start(f32[4,12,128,128]{3,2,1,0:T(8,128)} %refs_0_.1), channel_id=1, source_target_pairs={{0,2},{1,3},{2,0},{3,1},{4,6},{5,7},{6,4},{7,5},{8,10},{9,11},{10,... | collective-permute-start | bytes 9437192 | tf_op jit(solution)/shard_map/ppermute | solution.py:241
  5.5 2.0 cut.1
  7.5 0.0 copy-start.3
  7.5 72.5 %all_to_all.20 = bf16[8,16,16,128]{3,2,1,0:T(8,128)(2,1)S(1)} all-to-all(bf16[8,16,16,128]{3,2,1,0:T(8,128)(2,1)} %cut.1), channel_id=1, replica_groups=mesh['y'=8,'xl'=2,'z'=8,'xh'=2,'k'=2] {'xl','xh','k'}, dimensions={0} | all-to-all | bytes 1048576 | tf_op jit(solution)/shard_map/all_to_all | solution.py:258
  79.9 0.8 copy.22
  80.8 16.3 %all-to-all-start.1 = ((bf16[64,32,128]{2,1,0:T(8,128)(2,1)}), bf16[64,32,128]{2,1,0:T(8,128)(2,1)S(1)}, u32[]{:S(2)}, u32[]{:S(2)}) async-start(bf16[64,32,128]{2,1,0:T(8,128)(2,1)} %bitcast.7), calls=%async_computation.1 | async-start | bytes 1048576 | tf_op jit(solution)/shard_map/all_to_all | solution.py:265
  97.1 0.0 copy-done.3
  97.1 0.1 reshape.41
  97.2 0.1 copy.26
  97.4 0.3 reshape.42.dest_ref
  97.7 0.7 rank.1
  98.4 15.1 %all-to-all-done.1 = bf16[64,32,128]{2,1,0:T(8,128)(2,1)S(1)} async-done(((bf16[64,32,128]{2,1,0:T(8,128)(2,1)}), bf16[64,32,128]{2,1,0:T(8,128)(2,1)S(1)}, u32[]{:S(2)}, u32[]{:S(2)}) %all-to-all-start.1) | async-done | bytes 524320 | tf_op jit(solution)/shard_map/all_to_all | solution.py:265
  113.5 5.9 %route.1 = bf16[8192,128]{1,0:T(8,128)(2,1)} custom-call(f32[128,2048]{1,0:T(8,128)S(1)} %get-tuple-element.9.slot_ref, f32[128,128]{1,0:T(8,128)S(1)} %get-tuple-element.10.early_ref, bf16[2048,128]{1,0:T(8,128)(2,1)S(1)} %bitcast.18), custom_call_target="tpu_custom_call" | custom-call | tf_op jit(solution)/shard_map/route/pallas_call | solution.py:93
  119.5 0.0 copy-start.5
  119.5 0.0 copy-start.4
  119.5 0.0 copy-start.2
  119.5 10.0 %all-to-all-start.2 = ((bf16[128,64,128]{2,1,0:T(8,128)(2,1)}), bf16[128,64,128]{2,1,0:T(8,128)(2,1)S(1)}, u32[]{:S(2)}, u32[]{:S(2)}) async-start(bf16[128,64,128]{2,1,0:T(8,128)(2,1)} %bitcast.9), calls=%async_computation.2 | async-start | bytes 4194304 | tf_op jit(solution)/shard_map/all_to_all | solution.py:271
  129.5 3.2 %collective-permute-start.6 = (f32[4,12,128,128]{3,2,1,0:T(8,128)}, f32[4,12,128,128]{3,2,1,0:T(8,128)}, u32[]{:S(2)}, u32[]{:S(2)}) collective-permute-start(f32[4,12,128,128]{3,2,1,0:T(8,128)} %refs_0_.1), channel_id=1, source_target_pairs={{0,1},{1,0},{2,3},{3,2},{4,5},{5,4},{6,7},{7,6},{8,9},{9,8},{10,11... | collective-permute-start | bytes 9437192 | tf_op jit(solution)/shard_map/ppermute | solution.py:241
  132.7 0.0 collective-permute-done.2.refs_0_
  132.7 1.9 collective-permute-start.3
  134.6 0.0 copy-done.5
  134.7 0.0 copy-done.4
  134.7 0.1 pad_maximum_fusion.2
  134.8 3.6 %collective-permute-start = (f32[4,256]{1,0:T(4,128)S(1)}, f32[4,256]{1,0:T(4,128)S(1)}, u32[]{:S(2)}, u32[]{:S(2)}) collective-permute-start(f32[4,256]{1,0:T(4,128)S(1)} %pad_maximum_fusion.2), channel_id=1, source_target_pairs={{0,2},{1,3},{2,0},{3,1},{4,6},{5,7},{6,4},{7,5},{8,10},{9,11},{10,... | collective-permute-start | bytes 12296 | tf_op jit(solution)/shard_map/ppermute | solution.py:241
  138.4 2.9 %collective-permute-done = f32[4,256]{1,0:T(4,128)S(1)} collective-permute-done((f32[4,256]{1,0:T(4,128)S(1)}, f32[4,256]{1,0:T(4,128)S(1)}, u32[]{:S(2)}, u32[]{:S(2)}) %collective-permute-start) | collective-permute-done | bytes 4128 | tf_op jit(solution)/shard_map/ppermute | solution.py:241
  141.3 0.1 pad_maximum_fusion.1
  141.4 2.8 %collective-permute-start.1 = (f32[8,256]{1,0:T(8,128)S(1)}, f32[8,256]{1,0:T(8,128)S(1)}, u32[]{:S(2)}, u32[]{:S(2)}) collective-permute-start(f32[8,256]{1,0:T(8,128)S(1)} %pad_maximum_fusion.1), channel_id=1, source_target_pairs={{0,1},{1,0},{2,3},{3,2},{4,5},{5,4},{6,7},{7,6},{8,9},{9,8},{10,11... | collective-permute-start | bytes 24584 | tf_op jit(solution)/shard_map/ppermute | solution.py:241
  144.2 0.0 copy-done.2
  144.2 0.1 constant_dynamic-slice_fusion
  144.3 1.9 collective-permute-start.7
  146.3 3.6 %collective-permute-start.4 = (bf16[512,128]{1,0:T(8,128)(2,1)S(1)}, bf16[512,128]{1,0:T(8,128)(2,1)S(1)}, u32[]{:S(2)}, u32[]{:S(2)}) collective-permute-start(bf16[512,128]{1,0:T(8,128)(2,1)S(1)} %get-tuple-element.13), channel_id=1, source_target_pairs={{0,2},{1,3},{2,0},{3,1},{4,6},{5,7},{6,4},{7,5},{8,10},{9,11},{10,... | collective-permute-start | bytes 393224 | tf_op jit(solution)/shard_map/ppermute | solution.py:241
  149.9 0.0 collective-permute-done.1
  149.9 3.8 %collective-permute-start.5 = (bf16[512,128]{1,0:T(8,128)(2,1)S(1)}, bf16[512,128]{1,0:T(8,128)(2,1)S(1)}, u32[]{:S(2)}, u32[]{:S(2)}) collective-permute-start(bf16[512,128]{1,0:T(8,128)(2,1)S(1)} %get-tuple-element.12), channel_id=1, source_target_pairs={{0,3},{1,2},{2,1},{3,0},{4,7},{5,6},{6,5},{7,4},{8,11},{9,10},{10,... | collective-permute-start | bytes 393224 | tf_op jit(solution)/shard_map/ppermute | solution.py:241
  153.8 0.1 pad_maximum_fusion
  153.9 0.1 copy.19
  154.0 0.4 select_reduce_fusion
  154.4 0.1 copy.21
  154.5 0.1 reshape.43.slot_ref
  154.6 0.0 copy-start.1
  154.6 24.1 %all-to-all-done.2.t_ref = bf16[128,64,128]{2,1,0:T(8,128)(2,1)S(1)} async-done(((bf16[128,64,128]{2,1,0:T(8,128)(2,1)}), bf16[128,64,128]{2,1,0:T(8,128)(2,1)S(1)}, u32[]{:S(2)}, u32[]{:S(2)}) %all-to-all-start.2) | async-done | bytes 2097184 | tf_op jit(solution)/shard_map/all_to_all | solution.py:271
  178.7 0.0 copy-start
  178.7 1.4 turn.1.refs_2_
  180.0 0.0 collective-permute-done.7.refs_4_
  180.0 0.0 collective-permute-done.6.refs_1_
  180.1 0.0 copy-done.1
  180.1 0.5 copy-done
  180.5 4.3 %ladder.2.refs_7_ = bf16[2,512,128]{2,1,0:T(8,128)(2,1)S(1)} custom-call(s32[192]{0:T(256)S(1)} %reshape.43.slot_ref, s32[1]{0:T(128)} %bitcast.4.blk_ref, f32[4,12,128,128]{3,2,1,0:T(8,128)S(1)} %copy-done, f32[4,12,128,128]{3,2,1,0:T(8,128)} %collective-permute-done.6.refs_1_, bf16[64,128,128]{2,1,0:T(8,128)(2,1)S(1)} %turn.1.refs_2_, ...), custom_call_target="tpu_custom_call" | custom-call | tf_op jit(solution)/shard_map/ladder/pallas_call | solution.py:218
  184.8 0.0 collective-permute-done.4.refs_3_
  184.8 0.0 collective-permute-done.5.refs_4_
  184.8 0.0 collective-permute-done.3.refs_1_
  184.9 5.2 %ladder.3 = bf16[4,512,128]{2,1,0:T(8,128)(2,1)S(1)} custom-call(s32[192]{0:T(256)S(1)} %reshape.43.slot_ref, s32[1]{0:T(128)} %bitcast.4.blk_ref, f32[4,12,128,128]{3,2,1,0:T(8,128)} %collective-permute-done.2.refs_0_, f32[4,12,128,128]{3,2,1,0:T(8,128)} %collective-permute-done.3.refs_1_, bf16[64,128,128]{2,1,0:T(8,128)(2,1)S(1)} %turn.1.refs_2_, ...), custom_call_target="tpu_custom_call" | custom-call | tf_op jit(solution)/shard_map/ladder/pallas_call | solution.py:218
  190.1 15.6 %all_to_all.21 = bf16[4,512,128]{2,1,0:T(8,128)(2,1)S(1)} all-to-all(bf16[4,512,128]{2,1,0:T(8,128)(2,1)S(1)} %ladder.3), channel_id=1, replica_groups=mesh['y'=8,'xl'=2,'z'=8,'xh'=2,'k'=2] {'xh','k'}, dimensions={0} | all-to-all | bytes 1048576 | tf_op jit(solution)/shard_map/all_to_all | solution.py:314
  205.7 0.2 copy.23
  205.9 1.0 copy.24
  (5 shorter events, 0.0 us)
Async XLA Ops:
  0.0 132.7 %collective-permute-start.2 = (f32[4,12,128,128]{3,2,1,0:T(8,128)}, f32[4,12,128,128]{3,2,1,0:T(8,128)}, u32[]{:S(2)}, u32[]{:S(2)}) collective-permute-start(f32[4,12,128,128]{3,2,1,0:T(8,128)} %refs_0_.1), channel_id=1, source_target_pairs={{0,2},{1,3},{2,0},{3,1},{4,6},{5,7},{6,4},{7,5},{8,10},{9,11},{10,... | collective-permute-start | bytes 9437192 | tf_op jit(solution)/shard_map/ppermute | solution.py:241
  7.5 89.6 %copy-start.3 = (s32[2048,4]{0,1:T(4,128)S(1)}, s32[2048,4]{0,1:T(4,128)}, u32[]{:S(2)}) copy-start(s32[2048,4]{0,1:T(4,128)} %param.10) | copy-start | bytes 98308
  80.8 32.8 %all-to-all-start.1 = ((bf16[64,32,128]{2,1,0:T(8,128)(2,1)}), bf16[64,32,128]{2,1,0:T(8,128)(2,1)S(1)}, u32[]{:S(2)}, u32[]{:S(2)}) async-start(bf16[64,32,128]{2,1,0:T(8,128)(2,1)} %bitcast.7), calls=%async_computation.1 | async-start | bytes 1048576 | tf_op jit(solution)/shard_map/all_to_all | solution.py:265
  119.5 15.2 %copy-start.5 = (s32[4,12]{1,0:T(4,128)S(1)}, s32[4,12]{1,0:T(4,128)}, u32[]{:S(2)}) copy-start(s32[4,12]{1,0:T(4,128)} %param.9) | copy-start | bytes 580
  119.5 15.2 %copy-start.4 = (f32[512]{0:T(512)S(1)}, f32[512]{0:T(512)}, u32[]{:S(2)}) copy-start(f32[512]{0:T(512)} %param.13) | copy-start | bytes 6148
  119.5 24.8 %copy-start.2 = (bf16[512,512]{1,0:T(8,128)(2,1)S(1)}, bf16[512,512]{1,0:T(8,128)(2,1)}, u32[]{:S(2)}) copy-start(bf16[512,512]{1,0:T(8,128)(2,1)} %param.11) | copy-start | bytes 1572868
  119.5 59.2 %all-to-all-start.2 = ((bf16[128,64,128]{2,1,0:T(8,128)(2,1)}), bf16[128,64,128]{2,1,0:T(8,128)(2,1)S(1)}, u32[]{:S(2)}, u32[]{:S(2)}) async-start(bf16[128,64,128]{2,1,0:T(8,128)(2,1)} %bitcast.9), calls=%async_computation.2 | async-start | bytes 4194304 | tf_op jit(solution)/shard_map/all_to_all | solution.py:271
  129.5 50.6 %collective-permute-start.6 = (f32[4,12,128,128]{3,2,1,0:T(8,128)}, f32[4,12,128,128]{3,2,1,0:T(8,128)}, u32[]{:S(2)}, u32[]{:S(2)}) collective-permute-start(f32[4,12,128,128]{3,2,1,0:T(8,128)} %refs_0_.1), channel_id=1, source_target_pairs={{0,1},{1,0},{2,3},{3,2},{4,5},{5,4},{6,7},{7,6},{8,9},{9,8},{10,11... | collective-permute-start | bytes 9437192 | tf_op jit(solution)/shard_map/ppermute | solution.py:241
  132.7 52.1 %collective-permute-start.3 = (f32[4,12,128,128]{3,2,1,0:T(8,128)}, f32[4,12,128,128]{3,2,1,0:T(8,128)}, u32[]{:S(2)}, u32[]{:S(2)}) collective-permute-start(f32[4,12,128,128]{3,2,1,0:T(8,128)} %collective-permute-done.2.refs_0_), channel_id=1, source_target_pairs={{0,1},{1,0},{2,3},{3,2},{4,5},{5,4},{6,7},{7,6},{8,9},{9,8},{10,11... | collective-permute-start | bytes 9437192 | tf_op jit(solution)/shard_map/ppermute | solution.py:241
  134.8 6.5 %collective-permute-start = (f32[4,256]{1,0:T(4,128)S(1)}, f32[4,256]{1,0:T(4,128)S(1)}, u32[]{:S(2)}, u32[]{:S(2)}) collective-permute-start(f32[4,256]{1,0:T(4,128)S(1)} %pad_maximum_fusion.2), channel_id=1, source_target_pairs={{0,2},{1,3},{2,0},{3,1},{4,6},{5,7},{6,4},{7,5},{8,10},{9,11},{10,... | collective-permute-start | bytes 12296 | tf_op jit(solution)/shard_map/ppermute | solution.py:241
  141.4 8.5 %collective-permute-start.1 = (f32[8,256]{1,0:T(8,128)S(1)}, f32[8,256]{1,0:T(8,128)S(1)}, u32[]{:S(2)}, u32[]{:S(2)}) collective-permute-start(f32[8,256]{1,0:T(8,128)S(1)} %pad_maximum_fusion.1), channel_id=1, source_target_pairs={{0,1},{1,0},{2,3},{3,2},{4,5},{5,4},{6,7},{7,6},{8,9},{9,8},{10,11... | collective-permute-start | bytes 24584 | tf_op jit(solution)/shard_map/ppermute | solution.py:241
  144.3 35.7 %collective-permute-start.7 = (bf16[512,128]{1,0:T(8,128)(2,1)S(1)}, bf16[512,128]{1,0:T(8,128)(2,1)S(1)}, u32[]{:S(2)}, u32[]{:S(2)}) collective-permute-start(bf16[512,128]{1,0:T(8,128)(2,1)S(1)} %get-tuple-element.11), channel_id=1, source_target_pairs={{0,1},{1,0},{2,3},{3,2},{4,5},{5,4},{6,7},{7,6},{8,9},{9,8},{10,11... | collective-permute-start | bytes 393224 | tf_op jit(solution)/shard_map/ppermute | solution.py:241
  146.3 38.6 %collective-permute-start.4 = (bf16[512,128]{1,0:T(8,128)(2,1)S(1)}, bf16[512,128]{1,0:T(8,128)(2,1)S(1)}, u32[]{:S(2)}, u32[]{:S(2)}) collective-permute-start(bf16[512,128]{1,0:T(8,128)(2,1)S(1)} %get-tuple-element.13), channel_id=1, source_target_pairs={{0,2},{1,3},{2,0},{3,1},{4,6},{5,7},{6,4},{7,5},{8,10},{9,11},{10,... | collective-permute-start | bytes 393224 | tf_op jit(solution)/shard_map/ppermute | solution.py:241
  149.9 34.9 %collective-permute-start.5 = (bf16[512,128]{1,0:T(8,128)(2,1)S(1)}, bf16[512,128]{1,0:T(8,128)(2,1)S(1)}, u32[]{:S(2)}, u32[]{:S(2)}) collective-permute-start(bf16[512,128]{1,0:T(8,128)(2,1)S(1)} %get-tuple-element.12), channel_id=1, source_target_pairs={{0,3},{1,2},{2,1},{3,0},{4,7},{5,6},{6,5},{7,4},{8,11},{9,10},{10,... | collective-permute-start | bytes 393224 | tf_op jit(solution)/shard_map/ppermute | solution.py:241
  154.6 25.5 %copy-start.1 = (f32[512]{0:T(512)S(1)}, f32[512]{0:T(512)}, u32[]{:S(2)}) copy-start(f32[512]{0:T(512)} %param.12) | copy-start | bytes 6148
  178.7 1.9 copy-start

commit v7 on v6

--- a/solution.py
+++ b/solution.py
@@ -13,7 +13,6 @@
 BF = jnp.bfloat16
 F32 = jnp.float32
 PARAMS = pltpu.CompilerParams(vmem_limit_bytes=48 * 1024 * 1024)
-WIDE = pltpu.CompilerParams(vmem_limit_bytes=46 * 1024 * 1024)
 FULL = pltpu.CompilerParams(vmem_limit_bytes=67043328)
 
 
@@ -105,36 +104,61 @@
     )(slot, early, table)
 
 
-def cut_call(amplitudes, nx, nblk):
+def cut_call(amplitudes, virt, tile_rows, nx, nblk):
     owned, rows, full_width = amplitudes.shape
     sub = rows // nx
     width = full_width // nblk
-
-    def body(a_ref, out_ref, held_ref, sems):
+    columns, listed = tile_rows.shape
+
+    def body(a_ref, v_ref, r_ref, out_ref, held_ref, virt_ref, rows_ref, slab_ref, sems):
+        facts = (
+            pltpu.make_async_copy(v_ref, virt_ref, sems.at[nblk]),
+            pltpu.make_async_copy(r_ref, rows_ref, sems.at[nblk + 1]),
+        )
+
         def load(q):
             part = a_ref.at[:, :, pl.ds(q * width, width)]
             return pltpu.make_async_copy(part, held_ref.at[q], sems.at[q])
 
+        for fact in facts:
+            fact.start()
         for q in range(nblk):
             load(q).start()
+        slab_ref[...] = jnp.zeros((owned, width), F32)
+        for fact in facts:
+            fact.wait()
+        left = virt_ref[...]
+        for i in range(3):
+            part = left.astype(BF).astype(F32)
+            slab_ref[i * columns : (i + 1) * columns, :] = part
+            left = left - part
+        last = slice(3 * columns, 4 * columns)
+        slab_ref[last, 0:listed] = (rows_ref[...] >> 6).astype(F32)
+        slab_ref[last, listed : 2 * listed] = (rows_ref[...] & 63).astype(F32)
+        slab = slab_ref[...].astype(BF)
         for q in range(nblk):
             load(q).wait()
             for h in range(nx):
-                out_ref[h * nblk + q] = jnp.swapaxes(held_ref[q, :, h * sub : (h + 1) * sub, :], 0, 1)
+                part = held_ref[q, :, h * sub : (h + 1) * sub, :]
+                out_ref[h * nblk + q, :sub] = jnp.swapaxes(part, 0, 1)
+                out_ref[h * nblk + q, sub] = slab
 
     return pl.pallas_call(
         body,
         grid=(1,),
-        in_specs=[pl.BlockSpec(memory_space=pl.ANY)],
-        out_specs=pl.BlockSpec((nx * nblk, sub, owned, width), lambda i: (0, 0, 0, 0)),
-        out_shape=jax.ShapeDtypeStruct((nx * nblk, sub, owned, width), BF),
+        in_specs=[pl.BlockSpec(memory_space=pl.ANY)] * 3,
+        out_specs=pl.BlockSpec((nx * nblk, sub + 1, owned, width), lambda i: (0, 0, 0, 0)),
+        out_shape=jax.ShapeDtypeStruct((nx * nblk, sub + 1, owned, width), BF),
         scratch_shapes=[
             pltpu.VMEM((nblk, owned, rows, width), BF),
-            pltpu.SemaphoreType.DMA((nblk,)),
+            pltpu.VMEM(virt.shape, F32),
+            pltpu.VMEM(tile_rows.shape, jnp.int32),
+            pltpu.VMEM((owned, width), F32),
+            pltpu.SemaphoreType.DMA((nblk + 2,)),
         ],
         compiler_params=FULL,
         name="cut",
-    )(amplitudes)
+    )(amplitudes, virt, tile_rows)
 
 
 def turn_call(incoming, nblk, ny, nx, nz):
@@ -161,12 +185,12 @@
     )(incoming)
 
 
-def ladder_call(slot, blk, first, weights, turned, sources, occ, virt, ready=None, places=None):
+def ladder_call(slot, blk, flips, weights, turned, sources, occ, virt, ready=None, before=()):
     columns, listed, depth, size = weights[0].shape
     width = turned.shape[1]
     owners = len(weights)
     some = 2
-    total = owners if places is None else len(places)
+    total = owners + len(before)
 
     def body(slot_ref, blk_ref, *refs):
         w_refs = refs[:owners]
@@ -178,17 +202,17 @@
             for n in range(columns):
                 at = m * columns + n
                 pltpu.make_async_copy(w_refs[m].at[n], held_ref.at[at], sems.at[at]).start()
-        if places is not None:
-            for m in range(first):
-                out_ref[blk_ref[0] ^ places[m]] = refs[-4][m]
+        for m, flip in enumerate(before):
+            out_ref[blk_ref[0] ^ flip] = refs[-4][m]
         for m in range(owners):
-            to = m if places is None else blk_ref[0] ^ places[first + m]
-
-            def some_columns(i, _, m=m, to=to):
+            owner = blk_ref[0] ^ flips[m]
+            to = owner if before else m
+
+            def some_columns(i, _, m=m, to=to, owner=owner):
                 for u in range(some):
                     n = i * some + u
                     at = m * columns + n
-                    named = first * columns + at
+                    named = owner * columns + n
                     pltpu.make_async_copy(w_refs[m].at[n], held_ref.at[at], sems.at[at]).wait()
                     right, left = [], []
                     for r in range(listed):
@@ -232,7 +256,7 @@
             ],
         ),
         out_shape=jax.ShapeDtypeStruct((total, columns * size, width), BF),
-        compiler_params=WIDE,
+        compiler_params=PARAMS,
         name="ladder",
     )(slot, blk, *weights, turned, *sources, occ, virt, *extra)
 
@@ -254,14 +278,11 @@
     slots = all_tiles * dest // groups
     columns, listed, _, size = integrals.shape
 
-    x = cut_call(amplitudes, nx, nblk)
+    x = cut_call(amplitudes, virt_energy.reshape(columns, size), tile_rows, nx, nblk)
     x = lax.all_to_all(x, LINE, 0, 0, tiled=True)
-    facts = [virt_energy.reshape(columns, size), tile_rows.astype(F32)]
-    facts.append(jnp.zeros((columns, size - listed), F32))
-    facts = jnp.concatenate(facts, axis=1)
-    facts_across = swap(facts, 2, nblk)
     across = swap(integrals, 2, nblk)
-    x = x.reshape(nx, nblk, sub, owned, width).transpose(1, 2, 0, 3, 4)
+    slabs = x[:, sub].reshape(nx, nblk, owned, width)
+    x = x[:, :sub].reshape(nx, nblk, sub, owned, width).transpose(1, 2, 0, 3, 4)
     x = lax.all_to_all(x.reshape(ny * nz, nx * owned, width), PLANE, 0, 0, tiled=True)
     table = x.reshape(all_tiles, width)
 
@@ -271,10 +292,11 @@
     incoming = lax.all_to_all(outgoing.reshape(groups, slots, width), GRP, 0, 0, tiled=True)
 
     beside = swap(integrals, 1, nblk)
-    pair = jnp.concatenate([facts, facts_across], axis=0)
-    other = swap(pair, 1, nblk)
-    facts = jnp.concatenate([facts, other[:columns], facts_across, other[columns:]], axis=0)
-    named_tiles = facts[:, size : size + listed].astype(jnp.int32)
+    slab = lax.dynamic_index_in_dim(slabs, lax.axis_index("xl"), 0, keepdims=False)
+    slab = slab.astype(F32).reshape(nblk, 4, columns, width)
+    virt = (slab[:, 0] + slab[:, 1] + slab[:, 2]).reshape(nblk * columns, size)
+    named_tiles = slab[:, 3, :, :listed] * 64 + slab[:, 3, :, listed : 2 * listed]
+    named_tiles = named_tiles.astype(jnp.int32).reshape(nblk * columns, listed)
     y_of = named_tiles // (nx * nz * owned)
     x_of = (named_tiles // (nz * owned)) % nx
     z_of = (named_tiles // owned) % nz
@@ -294,22 +316,21 @@
     source_diagonal = swap(quarter(3), 3, nblk)
 
     occ = occ_energy.reshape(1, full_width)
-    virt = facts[:, :size]
     mine = blk.reshape(1)
     local = ladder_call(
-        slot, mine, 0, (integrals, beside), turned, (quarter(0), source_near), occ, virt
+        slot, mine, (0, 1), (integrals, beside), turned, (quarter(0), source_near), occ, virt
     )
     done = ladder_call(
         slot,
         mine,
-        2,
+        (2, 3),
         (across, diagonal),
         turned,
         (source_far, source_diagonal),
         occ,
         virt,
         ready=local,
-        places=(0, 1, 2, 3),
+        before=(0, 1),
     )
     done = lax.all_to_all(done, BLK, 0, 0, tiled=True)
     return done.transpose(1, 0, 2).reshape(columns * size, full_width)
@@ -328,4 +349,6 @@
         P(),
         P(every),
     )
-    return jax.shard_map(per_device, mesh=fine, in_specs=in_specs, out_specs=P(every, None), check_vma=False)
+    return jax.shard_map(
+        per_device, mesh=fine, in_specs=in_specs, out_specs=P(every, None), check_vma=False
+    )

time: 208 us -> 210 us (level)
  starting transfers between devices: 52.7 us -> 46.2 us
  waiting for transfers between devices: 42.1 us -> 47.3 us
    all_to_all x1, waiting for transfers between devices: 24.1 us -> 32 us  [per_device(): lax.all_to_all(outgoing.reshape(groups, slots, width), GRP, 0, 0, tiled=T...]
    ppermute x8 -> x6, starting transfers between devices: 26.4 us -> 19.9 us  [swap(): return lax.ppermute(x, BLK, [(b, b ^ flip) for b in range(n)])]
    ppermute x8 -> x6, waiting for transfers between devices: 2.93 us -> 0.02 us  [swap(): return lax.ppermute(x, BLK, [(b, b ^ flip) for b in range(n)])]
  transfers between devices with their start and end apart: 10 -> 8, of which waited for: 3 -> 2; matrix products, arithmetic and copies ran while one was open for 1% -> 2% of each run, Pallas kernels for 7% -> 7%
where the time goes in v7:
time: 210 us; the launch traced here: 209 us
  blocking collectives  89.7 us (43%)
  waiting for transfers between devices  47.3 us (23%)
  starting transfers between devices  46.2 us (22%)
  Pallas kernels  19.4 us (9%)
  local copies, waits for them, and re-layouts  5.26 us (3%)
    all_to_all x1, blocking collectives, per_device(): x = lax.all_to_all(x, LINE, 0, 0, tiled=True)  72.9 us
    all_to_all x1, waiting for transfers between devices, per_device(): lax.all_to_all(outgoing.reshape(groups, slots, width), GRP, 0, 0, tiled=T...  32 us
    ppermute x6, starting transfers between devices, swap(): return lax.ppermute(x, BLK, [(b, b ^ flip) for b in range(n)])  19.9 us
    all_to_all x1, blocking collectives, per_device(): done = lax.all_to_all(done, BLK, 0, 0, tiled=True)  16.8 us
    all_to_all x1, starting transfers between devices, per_device(): lax.all_to_all(x.reshape(ny * nz, nx * owned, width), PLANE, 0, 0, tiled=...  16.4 us
    all_to_all x1, waiting for transfers between devices, per_device(): lax.all_to_all(x.reshape(ny * nz, nx * owned, width), PLANE, 0, 0, tiled=...  15.2 us
    all_to_all x1, starting transfers between devices, per_device(): lax.all_to_all(outgoing.reshape(groups, slots, width), GRP, 0, 0, tiled=T...  9.88 us
    pallas_call x2, Pallas kernels, ladder_call(): pl.pallas_call(body, grid_spec=pltpu.PrefetchScalarGridSpec(num_scalar_pr...  9.47 us
  transfers between devices with their start and end apart: 8, of which 2 were waited for; matrix products, arithmetic and copies ran while one was open for 2% of the time, Pallas kernels for 7%

profile of v7, /device:TPU:1, one launch (start us, length us, event | category | flops | bytes accessed | tf_op | source)
XLA Modules:
  0.0 208.7 jit_solution(14976565587195920608)
XLA Ops:
  0.0 5.5 %collective-permute-start = (f32[4,12,128,128]{3,2,1,0:T(8,128)}, f32[4,12,128,128]{3,2,1,0:T(8,128)}, u32[]{:S(2)}, u32[]{:S(2)}) collective-permute-start(f32[4,12,128,128]{3,2,1,0:T(8,128)} %refs_0_.1), channel_id=1, source_target_pairs={{0,2},{1,3},{2,0},{3,1},{4,6},{5,7},{6,4},{7,5},{8,10},{9,11},{10,... | collective-permute-start | bytes 9437192 | tf_op jit(solution)/shard_map/ppermute | solution.py:265
  5.5 2.1 cut.1
  7.5 0.0 copy-start.2
  7.5 72.9 %all_to_all.20 = bf16[8,17,16,128]{3,2,1,0:T(8,128)(2,1)S(1)} all-to-all(bf16[8,17,16,128]{3,2,1,0:T(8,128)(2,1)} %cut.1), channel_id=1, replica_groups=mesh['y'=8,'xl'=2,'z'=8,'xh'=2,'k'=2] {'xl','xh','k'}, dimensions={0} | all-to-all | bytes 1114112 | tf_op jit(solution)/shard_map/all_to_all | solution.py:282
  80.5 0.8 copy.22
  81.3 16.4 %all-to-all-start.1 = ((bf16[64,32,128]{2,1,0:T(8,128)(2,1)}), bf16[64,32,128]{2,1,0:T(8,128)(2,1)S(1)}, u32[]{:S(2)}, u32[]{:S(2)}) async-start(bf16[64,32,128]{2,1,0:T(8,128)(2,1)} %bitcast.11), calls=%async_computation.1 | async-start | bytes 1048576 | tf_op jit(solution)/shard_map/all_to_all | solution.py:286
  97.7 0.0 copy-done.2
  97.7 0.1 reshape.142
  97.9 0.1 copy.26
  98.0 0.3 reshape.143.dest_ref
  98.3 0.7 rank.1
  99.0 15.2 %all-to-all-done.1 = bf16[64,32,128]{2,1,0:T(8,128)(2,1)S(1)} async-done(((bf16[64,32,128]{2,1,0:T(8,128)(2,1)}), bf16[64,32,128]{2,1,0:T(8,128)(2,1)S(1)}, u32[]{:S(2)}, u32[]{:S(2)}) %all-to-all-start.1) | async-done | bytes 524320 | tf_op jit(solution)/shard_map/all_to_all | solution.py:286
  114.2 5.9 %route.1 = bf16[8192,128]{1,0:T(8,128)(2,1)} custom-call(f32[128,2048]{1,0:T(8,128)S(1)} %get-tuple-element.9.slot_ref, f32[128,128]{1,0:T(8,128)S(1)} %get-tuple-element.10.early_ref, bf16[2048,128]{1,0:T(8,128)(2,1)S(1)} %bitcast.23), custom_call_target="tpu_custom_call" | custom-call | tf_op jit(solution)/shard_map/route/pallas_call | solution.py:92
  120.1 9.9 %all-to-all-start.2 = ((bf16[128,64,128]{2,1,0:T(8,128)(2,1)}), bf16[128,64,128]{2,1,0:T(8,128)(2,1)S(1)}, u32[]{:S(2)}, u32[]{:S(2)}) async-start(bf16[128,64,128]{2,1,0:T(8,128)(2,1)} %bitcast.13), calls=%async_computation.2 | async-start | bytes 4194304 | tf_op jit(solution)/shard_map/all_to_all | solution.py:292
  130.0 3.2 %collective-permute-start.4 = (f32[4,12,128,128]{3,2,1,0:T(8,128)}, f32[4,12,128,128]{3,2,1,0:T(8,128)}, u32[]{:S(2)}, u32[]{:S(2)}) collective-permute-start(f32[4,12,128,128]{3,2,1,0:T(8,128)} %refs_0_.1), channel_id=1, source_target_pairs={{0,1},{1,0},{2,3},{3,2},{4,5},{5,4},{6,7},{7,6},{8,9},{9,8},{10,11... | collective-permute-start | bytes 9437192 | tf_op jit(solution)/shard_map/ppermute | solution.py:265
  133.2 0.0 collective-permute-done.refs_0_
  133.2 1.9 collective-permute-start.1
  135.1 1.8 constant_dynamic-slice_fusion
  136.9 2.4 %collective-permute-start.5 = (bf16[512,128]{1,0:T(8,128)(2,1)}, bf16[512,128]{1,0:T(8,128)(2,1)S(1)}, u32[]{:S(2)}, u32[]{:S(2)}) collective-permute-start(bf16[512,128]{1,0:T(8,128)(2,1)} %get-tuple-element.11), channel_id=1, source_target_pairs={{0,1},{1,0},{2,3},{3,2},{4,5},{5,4},{6,7},{7,6},{8,9},{9,8},{10,11... | collective-permute-start | bytes 393224 | tf_op jit(solution)/shard_map/ppermute | solution.py:265
  139.3 4.3 %collective-permute-start.2 = (bf16[512,128]{1,0:T(8,128)(2,1)S(1)}, bf16[512,128]{1,0:T(8,128)(2,1)S(1)}, u32[]{:S(2)}, u32[]{:S(2)}) collective-permute-start(bf16[512,128]{1,0:T(8,128)(2,1)S(1)} %get-tuple-element.13), channel_id=1, source_target_pairs={{0,2},{1,3},{2,0},{3,1},{4,6},{5,7},{6,4},{7,5},{8,10},{9,11},{10,... | collective-permute-start | bytes 393224 | tf_op jit(solution)/shard_map/ppermute | solution.py:265
  143.6 2.7 %collective-permute-start.3 = (bf16[512,128]{1,0:T(8,128)(2,1)S(1)}, bf16[512,128]{1,0:T(8,128)(2,1)S(1)}, u32[]{:S(2)}, u32[]{:S(2)}) collective-permute-start(bf16[512,128]{1,0:T(8,128)(2,1)S(1)} %get-tuple-element.12), channel_id=1, source_target_pairs={{0,3},{1,2},{2,1},{3,0},{4,7},{5,6},{6,5},{7,4},{8,11},{9,10},{10,... | collective-permute-start | bytes 393224 | tf_op jit(solution)/shard_map/ppermute | solution.py:265
  146.4 0.1 fusion.10
  146.5 0.1 copy.19
  146.6 0.4 select_reduce_fusion
  147.0 0.1 copy.21
  147.1 0.1 reshape.144.slot_ref
  147.2 0.0 copy-start.1
  147.2 32.0 %all-to-all-done.2.t_ref = bf16[128,64,128]{2,1,0:T(8,128)(2,1)S(1)} async-done(((bf16[128,64,128]{2,1,0:T(8,128)(2,1)}), bf16[128,64,128]{2,1,0:T(8,128)(2,1)S(1)}, u32[]{:S(2)}, u32[]{:S(2)}) %all-to-all-start.2) | async-done | bytes 2097184 | tf_op jit(solution)/shard_map/all_to_all | solution.py:292
  179.2 0.0 copy-start
  179.2 1.4 turn.1.refs_2_
  180.6 0.0 collective-permute-done.5.refs_4_
  180.6 0.0 collective-permute-done.4.refs_1_
  180.6 0.0 copy-done.1
  180.6 0.5 copy-done
  181.1 4.3 %ladder.2.refs_7_ = bf16[2,512,128]{2,1,0:T(8,128)(2,1)S(1)} custom-call(s32[192]{0:T(256)S(1)} %reshape.144.slot_ref, s32[1]{0:T(128)} %bitcast.8.blk_ref, f32[4,12,128,128]{3,2,1,0:T(8,128)S(1)} %copy-done, f32[4,12,128,128]{3,2,1,0:T(8,128)} %collective-permute-done.4.refs_1_, bf16[64,128,128]{2,1,0:T(8,128)(2,1)S(1)} %turn.1.refs_2_, ...), custom_call_target="tpu_custom_call" | custom-call | tf_op jit(solution)/shard_map/ladder/pallas_call | solution.py:242
  185.4 0.0 collective-permute-done.2.refs_3_
  185.4 0.0 collective-permute-done.3.refs_4_
  185.4 0.0 collective-permute-done.1.refs_1_
  185.4 5.2 %ladder.3 = bf16[4,512,128]{2,1,0:T(8,128)(2,1)S(1)} custom-call(s32[192]{0:T(256)S(1)} %reshape.144.slot_ref, s32[1]{0:T(128)} %bitcast.8.blk_ref, f32[4,12,128,128]{3,2,1,0:T(8,128)} %collective-permute-done.refs_0_, f32[4,12,128,128]{3,2,1,0:T(8,128)} %collective-permute-done.1.refs_1_, bf16[64,128,128]{2,1,0:T(8,128)(2,1)S(1)} %turn.1.refs_2_, ...), custom_call_target="tpu_custom_call" | custom-call | tf_op jit(solution)/shard_map/ladder/pallas_call | solution.py:242
  190.6 16.8 %all_to_all.21 = bf16[4,512,128]{2,1,0:T(8,128)(2,1)S(1)} all-to-all(bf16[4,512,128]{2,1,0:T(8,128)(2,1)S(1)} %ladder.3), channel_id=1, replica_groups=mesh['y'=8,'xl'=2,'z'=8,'xh'=2,'k'=2] {'xh','k'}, dimensions={0} | all-to-all | bytes 1048576 | tf_op jit(solution)/shard_map/all_to_all | solution.py:335
  207.4 0.2 copy.23
  207.7 1.0 copy.24
  (6 shorter events, 0.1 us)
Async XLA Ops:
  0.0 133.2 %collective-permute-start = (f32[4,12,128,128]{3,2,1,0:T(8,128)}, f32[4,12,128,128]{3,2,1,0:T(8,128)}, u32[]{:S(2)}, u32[]{:S(2)}) collective-permute-start(f32[4,12,128,128]{3,2,1,0:T(8,128)} %refs_0_.1), channel_id=1, source_target_pairs={{0,2},{1,3},{2,0},{3,1},{4,6},{5,7},{6,4},{7,5},{8,10},{9,11},{10,... | collective-permute-start | bytes 9437192 | tf_op jit(solution)/shard_map/ppermute | solution.py:265
  7.5 90.2 %copy-start.2 = (s32[2048,4]{0,1:T(4,128)S(1)}, s32[2048,4]{0,1:T(4,128)}, u32[]{:S(2)}) copy-start(s32[2048,4]{0,1:T(4,128)} %param.10) | copy-start | bytes 98308
  81.3 32.9 %all-to-all-start.1 = ((bf16[64,32,128]{2,1,0:T(8,128)(2,1)}), bf16[64,32,128]{2,1,0:T(8,128)(2,1)S(1)}, u32[]{:S(2)}, u32[]{:S(2)}) async-start(bf16[64,32,128]{2,1,0:T(8,128)(2,1)} %bitcast.11), calls=%async_computation.1 | async-start | bytes 1048576 | tf_op jit(solution)/shard_map/all_to_all | solution.py:286
  120.1 59.1 %all-to-all-start.2 = ((bf16[128,64,128]{2,1,0:T(8,128)(2,1)}), bf16[128,64,128]{2,1,0:T(8,128)(2,1)S(1)}, u32[]{:S(2)}, u32[]{:S(2)}) async-start(bf16[128,64,128]{2,1,0:T(8,128)(2,1)} %bitcast.13), calls=%async_computation.2 | async-start | bytes 4194304 | tf_op jit(solution)/shard_map/all_to_all | solution.py:292
  130.0 50.6 %collective-permute-start.4 = (f32[4,12,128,128]{3,2,1,0:T(8,128)}, f32[4,12,128,128]{3,2,1,0:T(8,128)}, u32[]{:S(2)}, u32[]{:S(2)}) collective-permute-start(f32[4,12,128,128]{3,2,1,0:T(8,128)} %refs_0_.1), channel_id=1, source_target_pairs={{0,1},{1,0},{2,3},{3,2},{4,5},{5,4},{6,7},{7,6},{8,9},{9,8},{10,11... | collective-permute-start | bytes 9437192 | tf_op jit(solution)/shard_map/ppermute | solution.py:265
  133.2 52.2 %collective-permute-start.1 = (f32[4,12,128,128]{3,2,1,0:T(8,128)}, f32[4,12,128,128]{3,2,1,0:T(8,128)}, u32[]{:S(2)}, u32[]{:S(2)}) collective-permute-start(f32[4,12,128,128]{3,2,1,0:T(8,128)} %collective-permute-done.refs_0_), channel_id=1, source_target_pairs={{0,1},{1,0},{2,3},{3,2},{4,5},{5,4},{6,7},{7,6},{8,9},{9,8},{10,11... | collective-permute-start | bytes 9437192 | tf_op jit(solution)/shard_map/ppermute | solution.py:265
  136.9 43.7 %collective-permute-start.5 = (bf16[512,128]{1,0:T(8,128)(2,1)}, bf16[512,128]{1,0:T(8,128)(2,1)S(1)}, u32[]{:S(2)}, u32[]{:S(2)}) collective-permute-start(bf16[512,128]{1,0:T(8,128)(2,1)} %get-tuple-element.11), channel_id=1, source_target_pairs={{0,1},{1,0},{2,3},{3,2},{4,5},{5,4},{6,7},{7,6},{8,9},{9,8},{10,11... | collective-permute-start | bytes 393224 | tf_op jit(solution)/shard_map/ppermute | solution.py:265
  139.3 46.0 %collective-permute-start.2 = (bf16[512,128]{1,0:T(8,128)(2,1)S(1)}, bf16[512,128]{1,0:T(8,128)(2,1)S(1)}, u32[]{:S(2)}, u32[]{:S(2)}) collective-permute-start(bf16[512,128]{1,0:T(8,128)(2,1)S(1)} %get-tuple-element.13), channel_id=1, source_target_pairs={{0,2},{1,3},{2,0},{3,1},{4,6},{5,7},{6,4},{7,5},{8,10},{9,11},{10,... | collective-permute-start | bytes 393224 | tf_op jit(solution)/shard_map/ppermute | solution.py:265
  143.6 41.8 %collective-permute-start.3 = (bf16[512,128]{1,0:T(8,128)(2,1)S(1)}, bf16[512,128]{1,0:T(8,128)(2,1)S(1)}, u32[]{:S(2)}, u32[]{:S(2)}) collective-permute-start(bf16[512,128]{1,0:T(8,128)(2,1)S(1)} %get-tuple-element.12), channel_id=1, source_target_pairs={{0,3},{1,2},{2,1},{3,0},{4,7},{5,6},{6,5},{7,4},{8,11},{9,10},{10,... | collective-permute-start | bytes 393224 | tf_op jit(solution)/shard_map/ppermute | solution.py:265
  147.2 33.4 %copy-start.1 = (f32[512]{0:T(512)S(1)}, f32[512]{0:T(512)}, u32[]{:S(2)}) copy-start(f32[512]{0:T(512)} %param.12) | copy-start | bytes 6148
  179.2 1.9 copy-start

commit v8 on v6

--- a/solution.py
+++ b/solution.py
@@ -13,8 +13,10 @@
 BF = jnp.bfloat16
 F32 = jnp.float32
 PARAMS = pltpu.CompilerParams(vmem_limit_bytes=48 * 1024 * 1024)
-WIDE = pltpu.CompilerParams(vmem_limit_bytes=46 * 1024 * 1024)
-FULL = pltpu.CompilerParams(vmem_limit_bytes=67043328)
+
+
+def quarter_of(x_lo, b):
+    return b ^ ((x_lo & b & 1) << 1)
 
 
 def rank_call(own, dest, groups):
@@ -110,29 +112,19 @@
     sub = rows // nx
     width = full_width // nblk
 
-    def body(a_ref, out_ref, held_ref, sems):
-        def load(q):
-            part = a_ref.at[:, :, pl.ds(q * width, width)]
-            return pltpu.make_async_copy(part, held_ref.at[q], sems.at[q])
-
-        for q in range(nblk):
-            load(q).start()
-        for q in range(nblk):
-            load(q).wait()
-            for h in range(nx):
-                out_ref[h * nblk + q] = jnp.swapaxes(held_ref[q, :, h * sub : (h + 1) * sub, :], 0, 1)
+    def body(a_ref, out_ref):
+        for h in range(nx):
+            for q in range(nblk):
+                part = a_ref[:, h * sub : (h + 1) * sub, q * width : (q + 1) * width]
+                out_ref[h * nblk + quarter_of(h, q)] = jnp.swapaxes(part, 0, 1)
 
     return pl.pallas_call(
         body,
         grid=(1,),
-        in_specs=[pl.BlockSpec(memory_space=pl.ANY)],
+        in_specs=[pl.BlockSpec(amplitudes.shape, lambda i: (0, 0, 0))],
         out_specs=pl.BlockSpec((nx * nblk, sub, owned, width), lambda i: (0, 0, 0, 0)),
         out_shape=jax.ShapeDtypeStruct((nx * nblk, sub, owned, width), BF),
-        scratch_shapes=[
-            pltpu.VMEM((nblk, owned, rows, width), BF),
-            pltpu.SemaphoreType.DMA((nblk,)),
-        ],
-        compiler_params=FULL,
+        compiler_params=PARAMS,
         name="cut",
     )(amplitudes)
 
@@ -223,7 +215,7 @@
             in_specs=[pl.BlockSpec(memory_space=pl.ANY)] * owners
             + [whole(turned)]
             + [whole(x) for x in sources]
-            + [pl.BlockSpec((1, width), lambda i, s, b: (0, b[0])), whole(virt)]
+            + [pl.BlockSpec((1, width), lambda i, s, b: (0, b[1])), whole(virt)]
             + [whole(x) for x in extra],
             out_specs=pl.BlockSpec((total, columns * size, width), lambda i, s, b: (0, 0, 0)),
             scratch_shapes=[
@@ -232,7 +224,7 @@
             ],
         ),
         out_shape=jax.ShapeDtypeStruct((total, columns * size, width), BF),
-        compiler_params=WIDE,
+        compiler_params=PARAMS,
         name="ladder",
     )(slot, blk, *weights, turned, *sources, occ, virt, *extra)
 
@@ -247,6 +239,7 @@
     groups = ny * nx * nz
     own = lax.axis_index(GRP).astype(jnp.int32)
     blk = lax.axis_index(BLK).astype(jnp.int32)
+    x_lo = lax.axis_index("xl").astype(jnp.int32)
     owned, rows, full_width = amplitudes.shape
     all_tiles, dest = destinations.shape
     width = full_width // nblk
@@ -268,7 +261,13 @@
     dest_t = destinations.reshape(ny, nx, nz, owned, dest).transpose(4, 0, 2, 1, 3)
     slot_of, early, mine = rank_call(own.reshape(1), dest_t.reshape(dest, all_tiles), groups)
     outgoing = route_call(slot_of, early, table, slots)
-    incoming = lax.all_to_all(outgoing.reshape(groups, slots, width), GRP, 0, 0, tiled=True)
+    holders = [
+        [g * nblk + quarter_of(g // nz % nx, q) for g in range(groups)] for q in range(nblk)
+    ]
+    outgoing = outgoing.reshape(groups, slots, width)
+    incoming = lax.all_to_all(
+        outgoing, GRP + BLK, 0, 0, axis_index_groups=holders, tiled=True
+    )
 
     beside = swap(integrals, 1, nblk)
     pair = jnp.concatenate([facts, facts_across], axis=0)
@@ -287,7 +286,7 @@
     turned = turn_call(incoming, nblk, ny, nx, nz)
 
     def quarter(flip):
-        return lax.dynamic_slice_in_dim(source_terms, (blk ^ flip) * width, width, 1)
+        return lax.dynamic_slice_in_dim(source_terms, quarter_of(x_lo, blk ^ flip) * width, width, 1)
 
     source_far = swap(quarter(2), 2, nblk)
     source_near = swap(quarter(1), 1, nblk)
@@ -295,7 +294,7 @@
 
     occ = occ_energy.reshape(1, full_width)
     virt = facts[:, :size]
-    mine = blk.reshape(1)
+    mine = jnp.stack([blk, quarter_of(x_lo, blk)])
     local = ladder_call(
         slot, mine, 0, (integrals, beside), turned, (quarter(0), source_near), occ, virt
     )
@@ -312,7 +311,11 @@
         places=(0, 1, 2, 3),
     )
     done = lax.all_to_all(done, BLK, 0, 0, tiled=True)
-    return done.transpose(1, 0, 2).reshape(columns * size, full_width)
+    parts = []
+    for q in range(nblk):
+        usual, other = done[q], done[quarter_of(1, q)]
+        parts.append(usual if quarter_of(1, q) == q else jnp.where(x_lo == 1, other, usual))
+    return jnp.concatenate(parts, axis=1)
 
 
 def solution(mesh):
@@ -328,4 +331,6 @@
         P(),
         P(every),
     )
-    return jax.shard_map(per_device, mesh=fine, in_specs=in_specs, out_specs=P(every, None), check_vma=False)
+    return jax.shard_map(
+        per_device, mesh=fine, in_specs=in_specs, out_specs=P(every, None), check_vma=False
+    )

time: 208 us -> 210 us (level)
  blocking collectives: 88.1 us -> 73.3 us
  waiting for transfers between devices: 42.1 us -> 53.2 us
  starting transfers between devices: 52.7 us -> 58.8 us
    all_to_all x1 -> x0, blocking collectives: 15.6 us -> none  [per_device(): done = lax.all_to_all(done, BLK, 0, 0, tiled=True)]
    all_to_all x1 -> x2, waiting for transfers between devices: 24.1 us -> 37.3 us  [the longest x1 28 us: per_device(): lax.all_to_all(outgoing, GRP + BLK, 0, 0, axis_index_groups=holders, tile...]
    all_to_all x1 -> x2, starting transfers between devices: 9.97 us -> 16.2 us  [the longest x1 9.73 us: per_device(): lax.all_to_all(outgoing, GRP + BLK, 0, 0, axis_index_groups=holders, tile...]
    ppermute x8, waiting for transfers between devices: 2.93 us -> 0.8 us  [swap(): return lax.ppermute(x, BLK, [(b, b ^ flip) for b in range(n)])]
  transfers between devices with their start and end apart: 10 -> 11, of which waited for: 3 -> 4; matrix products, arithmetic and copies ran while one was open for 1% -> 1% of each run, Pallas kernels for 7% -> 6%
where the time goes in v8:
time: 210 us; the launch traced here: 209 us
  blocking collectives  73.3 us (35%)
  starting transfers between devices  58.8 us (28%)
  waiting for transfers between devices  53.2 us (25%)
  Pallas kernels  18.4 us (9%)
  local copies, waits for them, and re-layouts  3.35 us (2%)
    all_to_all x1, blocking collectives, per_device(): x = lax.all_to_all(x, LINE, 0, 0, tiled=True)  73.3 us
    all_to_all x1, waiting for transfers between devices, per_device(): lax.all_to_all(outgoing, GRP + BLK, 0, 0, axis_index_groups=holders, tile...  28 us
    ppermute x8, starting transfers between devices, swap(): return lax.ppermute(x, BLK, [(b, b ^ flip) for b in range(n)])  26.3 us
    all_to_all x1, starting transfers between devices, per_device(): lax.all_to_all(x.reshape(ny * nz, nx * owned, width), PLANE, 0, 0, tiled=...  16.3 us
    all_to_all x1, waiting for transfers between devices, per_device(): lax.all_to_all(x.reshape(ny * nz, nx * owned, width), PLANE, 0, 0, tiled=...  15.1 us
    pallas_call x2, Pallas kernels, ladder_call(): pl.pallas_call(body, grid_spec=pltpu.PrefetchScalarGridSpec(num_scalar_pr...  10.3 us
    all_to_all x1, starting transfers between devices, per_device(): lax.all_to_all(outgoing, GRP + BLK, 0, 0, axis_index_groups=holders, tile...  9.73 us
    all_to_all x1, waiting for transfers between devices, per_device(): done = lax.all_to_all(done, BLK, 0, 0, tiled=True)  9.35 us
  transfers between devices with their start and end apart: 11, of which 4 were waited for; matrix products, arithmetic and copies ran while one was open for 1% of the time, Pallas kernels for 6%

profile of v8, /device:TPU:1, one launch (start us, length us, event | category | flops | bytes accessed | tf_op | source)
XLA Modules:
  0.0 209.0 jit_solution(4395716159447024317)
XLA Ops:
  0.0 5.5 %collective-permute-start.2 = (f32[4,12,128,128]{3,2,1,0:T(8,128)}, f32[4,12,128,128]{3,2,1,0:T(8,128)}, u32[]{:S(2)}, u32[]{:S(2)}) collective-permute-start(f32[4,12,128,128]{3,2,1,0:T(8,128)} %refs_0_.1), channel_id=1, source_target_pairs={{0,2},{1,3},{2,0},{3,1},{4,6},{5,7},{6,4},{7,5},{8,10},{9,11},{10,... | collective-permute-start | bytes 9437192 | tf_op jit(solution)/shard_map/ppermute | solution.py:233
  5.5 0.0 copy-start.1
  5.5 1.0 copy-done.1
  6.5 0.0 copy-start.4
  6.5 0.2 cut.1
  6.7 73.3 %all_to_all.20 = bf16[8,16,16,128]{3,2,1,0:T(8,128)(2,1)S(1)} all-to-all(bf16[8,16,16,128]{3,2,1,0:T(8,128)(2,1)S(1)} %cut.1), channel_id=1, replica_groups=mesh['y'=8,'xl'=2,'z'=8,'xh'=2,'k'=2] {'xl','xh','k'}, dimensions={0} | all-to-all | bytes 1048576 | tf_op jit(solution)/shard_map/all_to_all | solution.py:251
  79.9 0.8 copy.16
  80.8 16.3 %all-to-all-start.1 = ((bf16[64,32,128]{2,1,0:T(8,128)(2,1)}), bf16[64,32,128]{2,1,0:T(8,128)(2,1)S(1)}, u32[]{:S(2)}, u32[]{:S(2)}) async-start(bf16[64,32,128]{2,1,0:T(8,128)(2,1)} %bitcast.8), calls=%async_computation.1 | async-start | bytes 1048576 | tf_op jit(solution)/shard_map/all_to_all | solution.py:258
  97.1 0.0 copy-done.4
  97.1 0.1 reshape.39
  97.2 0.1 copy.18
  97.4 0.3 reshape.40.dest_ref
  97.7 0.7 rank.1
  98.4 15.1 %all-to-all-done.1 = bf16[64,32,128]{2,1,0:T(8,128)(2,1)S(1)} async-done(((bf16[64,32,128]{2,1,0:T(8,128)(2,1)}), bf16[64,32,128]{2,1,0:T(8,128)(2,1)S(1)}, u32[]{:S(2)}, u32[]{:S(2)}) %all-to-all-start.1) | async-done | bytes 524320 | tf_op jit(solution)/shard_map/all_to_all | solution.py:258
  113.5 5.9 %route.1 = bf16[8192,128]{1,0:T(8,128)(2,1)} custom-call(f32[128,2048]{1,0:T(8,128)S(1)} %get-tuple-element.9.slot_ref, f32[128,128]{1,0:T(8,128)S(1)} %get-tuple-element.10.early_ref, bf16[2048,128]{1,0:T(8,128)(2,1)S(1)} %bitcast.25), custom_call_target="tpu_custom_call" | custom-call | tf_op jit(solution)/shard_map/route/pallas_call | solution.py:95
  119.4 0.0 copy-start.6
  119.4 0.0 copy-start.5
  119.4 0.0 copy-start.3
  119.4 9.7 %all-to-all-start.2 = ((bf16[128,64,128]{2,1,0:T(8,128)(2,1)}), bf16[128,64,128]{2,1,0:T(8,128)(2,1)S(1)}, u32[]{:S(2)}, u32[]{:S(2)}) async-start(bf16[128,64,128]{2,1,0:T(8,128)(2,1)} %bitcast.10), calls=%async_computation.2 | async-start | bytes 4194304 | tf_op jit(solution)/shard_map/all_to_all | solution.py:268
  129.2 3.5 %collective-permute-start.6 = (f32[4,12,128,128]{3,2,1,0:T(8,128)}, f32[4,12,128,128]{3,2,1,0:T(8,128)}, u32[]{:S(2)}, u32[]{:S(2)}) collective-permute-start(f32[4,12,128,128]{3,2,1,0:T(8,128)} %refs_0_.1), channel_id=1, source_target_pairs={{0,1},{1,0},{2,3},{3,2},{4,5},{5,4},{6,7},{7,6},{8,9},{9,8},{10,11... | collective-permute-start | bytes 9437192 | tf_op jit(solution)/shard_map/ppermute | solution.py:233
  132.7 0.0 collective-permute-done.2.refs_0_
  132.7 1.9 collective-permute-start.3
  134.6 0.0 copy-done.6
  134.6 0.0 copy-done.5
  134.7 0.1 pad_maximum_fusion.3
  134.7 3.6 %collective-permute-start = (f32[4,256]{1,0:T(4,128)S(1)}, f32[4,256]{1,0:T(4,128)S(1)}, u32[]{:S(2)}, u32[]{:S(2)}) collective-permute-start(f32[4,256]{1,0:T(4,128)S(1)} %pad_maximum_fusion.3), channel_id=1, source_target_pairs={{0,2},{1,3},{2,0},{3,1},{4,6},{5,7},{6,4},{7,5},{8,10},{9,11},{10,... | collective-permute-start | bytes 12296 | tf_op jit(solution)/shard_map/ppermute | solution.py:233
  138.4 0.0 copy-done.3
  138.4 0.1 constant_dynamic-slice_fusion
  138.5 2.7 %collective-permute-start.7 = (bf16[512,128]{1,0:T(8,128)(2,1)S(1)}, bf16[512,128]{1,0:T(8,128)(2,1)S(1)}, u32[]{:S(2)}, u32[]{:S(2)}) collective-permute-start(bf16[512,128]{1,0:T(8,128)(2,1)S(1)} %get-tuple-element.15), channel_id=1, source_target_pairs={{0,1},{1,0},{2,3},{3,2},{4,5},{5,4},{6,7},{7,6},{8,9},{9,8},{10,11... | collective-permute-start | bytes 393224 | tf_op jit(solution)/shard_map/ppermute | solution.py:233
  141.2 3.2 %collective-permute-start.4 = (bf16[512,128]{1,0:T(8,128)(2,1)S(1)}, bf16[512,128]{1,0:T(8,128)(2,1)S(1)}, u32[]{:S(2)}, u32[]{:S(2)}) collective-permute-start(bf16[512,128]{1,0:T(8,128)(2,1)S(1)} %get-tuple-element.17), channel_id=1, source_target_pairs={{0,2},{1,3},{2,0},{3,1},{4,6},{5,7},{6,4},{7,5},{8,10},{9,11},{10,... | collective-permute-start | bytes 393224 | tf_op jit(solution)/shard_map/ppermute | solution.py:233
  144.4 0.0 collective-permute-done
  144.4 0.1 pad_maximum_fusion.2
  144.5 2.2 %collective-permute-start.1 = (f32[8,256]{1,0:T(8,128)S(1)}, f32[8,256]{1,0:T(8,128)S(1)}, u32[]{:S(2)}, u32[]{:S(2)}) collective-permute-start(f32[8,256]{1,0:T(8,128)S(1)} %pad_maximum_fusion.2), channel_id=1, source_target_pairs={{0,1},{1,0},{2,3},{3,2},{4,5},{5,4},{6,7},{7,6},{8,9},{9,8},{10,11... | collective-permute-start | bytes 24584 | tf_op jit(solution)/shard_map/ppermute | solution.py:233
  146.7 0.1 pad_add_fusion.blk_ref
  146.7 0.8 collective-permute-done.1
  147.5 3.8 %collective-permute-start.5 = (bf16[512,128]{1,0:T(8,128)(2,1)S(1)}, bf16[512,128]{1,0:T(8,128)(2,1)S(1)}, u32[]{:S(2)}, u32[]{:S(2)}) collective-permute-start(bf16[512,128]{1,0:T(8,128)(2,1)S(1)} %get-tuple-element.16), channel_id=1, source_target_pairs={{0,3},{1,2},{2,1},{3,0},{4,7},{5,6},{6,5},{7,4},{8,11},{9,10},{10,... | collective-permute-start | bytes 393224 | tf_op jit(solution)/shard_map/ppermute | solution.py:233
  151.3 0.1 pad_maximum_fusion.1
  151.4 0.1 copy.13
  151.5 0.4 select_reduce_fusion
  151.9 0.1 copy.15
  152.0 0.1 reshape.41.slot_ref
  152.1 0.0 copy-start.2
  152.1 28.0 %all-to-all-done.2.t_ref = bf16[128,64,128]{2,1,0:T(8,128)(2,1)S(1)} async-done(((bf16[128,64,128]{2,1,0:T(8,128)(2,1)}), bf16[128,64,128]{2,1,0:T(8,128)(2,1)S(1)}, u32[]{:S(2)}, u32[]{:S(2)}) %all-to-all-start.2) | async-done | bytes 2097184 | tf_op jit(solution)/shard_map/all_to_all | solution.py:268
  180.1 0.0 copy-start
  180.1 1.4 turn.1.refs_2_
  181.5 0.0 collective-permute-done.7.refs_4_
  181.5 0.0 collective-permute-done.6.refs_1_
  181.5 0.0 copy-done.2
  181.5 0.5 copy-done
  182.0 4.3 %ladder.2.refs_7_ = bf16[2,512,128]{2,1,0:T(8,128)(2,1)S(1)} custom-call(s32[192]{0:T(256)S(1)} %reshape.41.slot_ref, s32[2]{0:T(128)S(1)} %pad_add_fusion.blk_ref, f32[4,12,128,128]{3,2,1,0:T(8,128)S(1)} %copy-done, f32[4,12,128,128]{3,2,1,0:T(8,128)} %collective-permute-done.6.refs_1_, bf16[64,128,128]{2,1,0:T(8,128)(2,1)S(1)} %turn.1.refs_2_, ...), custom_call_target="tpu_custom_call" | custom-call | tf_op jit(solution)/shard_map/ladder/pallas_call | solution.py:210
  186.3 0.0 collective-permute-done.4.refs_3_
  186.3 0.0 collective-permute-done.5.refs_4_
  186.3 0.0 collective-permute-done.3.refs_1_
  186.3 6.0 %ladder.3 = bf16[4,512,128]{2,1,0:T(8,128)(2,1)} custom-call(s32[192]{0:T(256)S(1)} %reshape.41.slot_ref, s32[2]{0:T(128)S(1)} %pad_add_fusion.blk_ref, f32[4,12,128,128]{3,2,1,0:T(8,128)} %collective-permute-done.2.refs_0_, f32[4,12,128,128]{3,2,1,0:T(8,128)} %collective-permute-done.3.refs_1_, bf16[64,128,128]{2,1,0:T(8,128)(2,1)S(1)} %turn.1.refs_2_, ...), custom_call_target="tpu_custom_call" | custom-call | tf_op jit(solution)/shard_map/ladder/pallas_call | solution.py:210
  192.3 6.5 %all-to-all-start.3 = ((bf16[4,512,128]{2,1,0:T(8,128)(2,1)}), bf16[4,512,128]{2,1,0:T(8,128)(2,1)S(1)}, u32[]{:S(2)}, u32[]{:S(2)}) async-start(bf16[4,512,128]{2,1,0:T(8,128)(2,1)} %ladder.3), calls=%async_computation.3 | async-start | bytes 1048576 | tf_op jit(solution)/shard_map/all_to_all | solution.py:313
  198.8 9.3 %all-to-all-done.3 = bf16[4,512,128]{2,1,0:T(8,128)(2,1)S(1)} async-done(((bf16[4,512,128]{2,1,0:T(8,128)(2,1)}), bf16[4,512,128]{2,1,0:T(8,128)(2,1)S(1)}, u32[]{:S(2)}, u32[]{:S(2)}) %all-to-all-start.3) | async-done | bytes 524320 | tf_op jit(solution)/shard_map/all_to_all | solution.py:313
  208.2 0.9 pad_maximum_fusion
  (6 shorter events, 0.1 us)
Async XLA Ops:
  0.0 132.7 %collective-permute-start.2 = (f32[4,12,128,128]{3,2,1,0:T(8,128)}, f32[4,12,128,128]{3,2,1,0:T(8,128)}, u32[]{:S(2)}, u32[]{:S(2)}) collective-permute-start(f32[4,12,128,128]{3,2,1,0:T(8,128)} %refs_0_.1), channel_id=1, source_target_pairs={{0,2},{1,3},{2,0},{3,1},{4,6},{5,7},{6,4},{7,5},{8,10},{9,11},{10,... | collective-permute-start | bytes 9437192 | tf_op jit(solution)/shard_map/ppermute | solution.py:233
  5.5 1.0 copy-start.1
  6.5 90.6 %copy-start.4 = (s32[2048,4]{0,1:T(4,128)S(1)}, s32[2048,4]{0,1:T(4,128)}, u32[]{:S(2)}) copy-start(s32[2048,4]{0,1:T(4,128)} %param.10) | copy-start | bytes 98308
  80.8 32.8 %all-to-all-start.1 = ((bf16[64,32,128]{2,1,0:T(8,128)(2,1)}), bf16[64,32,128]{2,1,0:T(8,128)(2,1)S(1)}, u32[]{:S(2)}, u32[]{:S(2)}) async-start(bf16[64,32,128]{2,1,0:T(8,128)(2,1)} %bitcast.8), calls=%async_computation.1 | async-start | bytes 1048576 | tf_op jit(solution)/shard_map/all_to_all | solution.py:258
  119.4 15.2 %copy-start.6 = (s32[4,12]{1,0:T(4,128)S(1)}, s32[4,12]{1,0:T(4,128)}, u32[]{:S(2)}) copy-start(s32[4,12]{1,0:T(4,128)} %param.9) | copy-start | bytes 580
  119.4 15.2 %copy-start.5 = (f32[512]{0:T(512)S(1)}, f32[512]{0:T(512)}, u32[]{:S(2)}) copy-start(f32[512]{0:T(512)} %param.13) | copy-start | bytes 6148
  119.4 18.9 %copy-start.3 = (bf16[512,512]{1,0:T(8,128)(2,1)S(1)}, bf16[512,512]{1,0:T(8,128)(2,1)}, u32[]{:S(2)}) copy-start(bf16[512,512]{1,0:T(8,128)(2,1)} %param.11) | copy-start | bytes 1572868
  119.4 60.6 %all-to-all-start.2 = ((bf16[128,64,128]{2,1,0:T(8,128)(2,1)}), bf16[128,64,128]{2,1,0:T(8,128)(2,1)S(1)}, u32[]{:S(2)}, u32[]{:S(2)}) async-start(bf16[128,64,128]{2,1,0:T(8,128)(2,1)} %bitcast.10), calls=%async_computation.2 | async-start | bytes 4194304 | tf_op jit(solution)/shard_map/all_to_all | solution.py:268
  129.2 52.3 %collective-permute-start.6 = (f32[4,12,128,128]{3,2,1,0:T(8,128)}, f32[4,12,128,128]{3,2,1,0:T(8,128)}, u32[]{:S(2)}, u32[]{:S(2)}) collective-permute-start(f32[4,12,128,128]{3,2,1,0:T(8,128)} %refs_0_.1), channel_id=1, source_target_pairs={{0,1},{1,0},{2,3},{3,2},{4,5},{5,4},{6,7},{7,6},{8,9},{9,8},{10,11... | collective-permute-start | bytes 9437192 | tf_op jit(solution)/shard_map/ppermute | solution.py:233
  132.7 53.6 %collective-permute-start.3 = (f32[4,12,128,128]{3,2,1,0:T(8,128)}, f32[4,12,128,128]{3,2,1,0:T(8,128)}, u32[]{:S(2)}, u32[]{:S(2)}) collective-permute-start(f32[4,12,128,128]{3,2,1,0:T(8,128)} %collective-permute-done.2.refs_0_), channel_id=1, source_target_pairs={{0,1},{1,0},{2,3},{3,2},{4,5},{5,4},{6,7},{7,6},{8,9},{9,8},{10,11... | collective-permute-start | bytes 9437192 | tf_op jit(solution)/shard_map/ppermute | solution.py:233
  134.7 9.6 %collective-permute-start = (f32[4,256]{1,0:T(4,128)S(1)}, f32[4,256]{1,0:T(4,128)S(1)}, u32[]{:S(2)}, u32[]{:S(2)}) collective-permute-start(f32[4,256]{1,0:T(4,128)S(1)} %pad_maximum_fusion.3), channel_id=1, source_target_pairs={{0,2},{1,3},{2,0},{3,1},{4,6},{5,7},{6,4},{7,5},{8,10},{9,11},{10,... | collective-permute-start | bytes 12296 | tf_op jit(solution)/shard_map/ppermute | solution.py:233
  138.5 43.0 %collective-permute-start.7 = (bf16[512,128]{1,0:T(8,128)(2,1)S(1)}, bf16[512,128]{1,0:T(8,128)(2,1)S(1)}, u32[]{:S(2)}, u32[]{:S(2)}) collective-permute-start(bf16[512,128]{1,0:T(8,128)(2,1)S(1)} %get-tuple-element.15), channel_id=1, source_target_pairs={{0,1},{1,0},{2,3},{3,2},{4,5},{5,4},{6,7},{7,6},{8,9},{9,8},{10,11... | collective-permute-start | bytes 393224 | tf_op jit(solution)/shard_map/ppermute | solution.py:233
  141.2 45.1 %collective-permute-start.4 = (bf16[512,128]{1,0:T(8,128)(2,1)S(1)}, bf16[512,128]{1,0:T(8,128)(2,1)S(1)}, u32[]{:S(2)}, u32[]{:S(2)}) collective-permute-start(bf16[512,128]{1,0:T(8,128)(2,1)S(1)} %get-tuple-element.17), channel_id=1, source_target_pairs={{0,2},{1,3},{2,0},{3,1},{4,6},{5,7},{6,4},{7,5},{8,10},{9,11},{10,... | collective-permute-start | bytes 393224 | tf_op jit(solution)/shard_map/ppermute | solution.py:233
  144.5 3.1 %collective-permute-start.1 = (f32[8,256]{1,0:T(8,128)S(1)}, f32[8,256]{1,0:T(8,128)S(1)}, u32[]{:S(2)}, u32[]{:S(2)}) collective-permute-start(f32[8,256]{1,0:T(8,128)S(1)} %pad_maximum_fusion.2), channel_id=1, source_target_pairs={{0,1},{1,0},{2,3},{3,2},{4,5},{5,4},{6,7},{7,6},{8,9},{9,8},{10,11... | collective-permute-start | bytes 24584 | tf_op jit(solution)/shard_map/ppermute | solution.py:233
  147.5 38.8 %collective-permute-start.5 = (bf16[512,128]{1,0:T(8,128)(2,1)S(1)}, bf16[512,128]{1,0:T(8,128)(2,1)S(1)}, u32[]{:S(2)}, u32[]{:S(2)}) collective-permute-start(bf16[512,128]{1,0:T(8,128)(2,1)S(1)} %get-tuple-element.16), channel_id=1, source_target_pairs={{0,3},{1,2},{2,1},{3,0},{4,7},{5,6},{6,5},{7,4},{8,11},{9,10},{10,... | collective-permute-start | bytes 393224 | tf_op jit(solution)/shard_map/ppermute | solution.py:233
  152.1 29.4 %copy-start.2 = (f32[512]{0:T(512)S(1)}, f32[512]{0:T(512)}, u32[]{:S(2)}) copy-start(f32[512]{0:T(512)} %param.12) | copy-start | bytes 6148
  180.1 1.9 copy-start
  192.3 15.8 %all-to-all-start.3 = ((bf16[4,512,128]{2,1,0:T(8,128)(2,1)}), bf16[4,512,128]{2,1,0:T(8,128)(2,1)S(1)}, u32[]{:S(2)}, u32[]{:S(2)}) async-start(bf16[4,512,128]{2,1,0:T(8,128)(2,1)} %ladder.3), calls=%async_computation.3 | async-start | bytes 1048576 | tf_op jit(solution)/shard_map/all_to_all | solution.py:313

commit v9 on v8

--- a/solution.py
+++ b/solution.py
@@ -153,38 +153,32 @@
     )(incoming)
 
 
-def ladder_call(slot, blk, first, weights, turned, sources, occ, virt, ready=None, places=None):
+def ladder_call(slot, blk, flips, weights, turned, sources, occ, virt):
     columns, listed, depth, size = weights[0].shape
     width = turned.shape[1]
     owners = len(weights)
     some = 2
-    total = owners if places is None else len(places)
 
     def body(slot_ref, blk_ref, *refs):
         w_refs = refs[:owners]
         t_ref = refs[owners]
         s_refs = refs[owners + 1 : 2 * owners + 1]
-        o_ref, v_ref = refs[2 * owners + 1 : 2 * owners + 3]
-        out_ref, held_ref, sems = refs[-3:]
+        o_ref, v_ref, out_ref, held_ref, sems = refs[2 * owners + 1 :]
         for m in range(owners):
             for n in range(columns):
                 at = m * columns + n
                 pltpu.make_async_copy(w_refs[m].at[n], held_ref.at[at], sems.at[at]).start()
-        if places is not None:
-            for m in range(first):
-                out_ref[blk_ref[0] ^ places[m]] = refs[-4][m]
         for m in range(owners):
-            to = m if places is None else blk_ref[0] ^ places[first + m]
+            to = blk_ref[0] ^ flips[m]
 
             def some_columns(i, _, m=m, to=to):
                 for u in range(some):
                     n = i * some + u
                     at = m * columns + n
-                    named = first * columns + at
                     pltpu.make_async_copy(w_refs[m].at[n], held_ref.at[at], sems.at[at]).wait()
                     right, left = [], []
                     for r in range(listed):
-                        s = slot_ref[named * listed + r]
+                        s = slot_ref[at * listed + r]
                         w = held_ref[at, r]
                         hi = w.astype(BF)
                         lo = (w - hi.astype(F32)).astype(BF)
@@ -196,9 +190,9 @@
                     acc = jnp.dot(left, right, preferred_element_type=F32)
                     part = (acc[:, :size] + acc[:, size:]).T
                     rows = pl.ds(n * size, size)
-                    summed = s_refs[m][rows, :].astype(F32) + part
-                    v = jnp.broadcast_to(v_ref[pl.ds(named, 1), :], (size, size)).T
-                    out_ref[to, rows, :] = (summed / (v + o_ref[...])).astype(BF)
+                    total = s_refs[m][rows, :].astype(F32) + part
+                    v = jnp.broadcast_to(v_ref[pl.ds(at, 1), :], (size, size)).T
+                    out_ref[to, rows, :] = (total / (v + o_ref[...])).astype(BF)
                 return 0
 
             lax.fori_loop(0, columns // some, some_columns, 0)
@@ -206,7 +200,6 @@
     def whole(x):
         return pl.BlockSpec(x.shape, lambda i, s, b: (0,) * x.ndim)
 
-    extra = () if ready is None else (ready,)
     return pl.pallas_call(
         body,
         grid_spec=pltpu.PrefetchScalarGridSpec(
@@ -215,18 +208,17 @@
             in_specs=[pl.BlockSpec(memory_space=pl.ANY)] * owners
             + [whole(turned)]
             + [whole(x) for x in sources]
-            + [pl.BlockSpec((1, width), lambda i, s, b: (0, b[1])), whole(virt)]
-            + [whole(x) for x in extra],
-            out_specs=pl.BlockSpec((total, columns * size, width), lambda i, s, b: (0, 0, 0)),
+            + [pl.BlockSpec((1, width), lambda i, s, b: (0, b[1])), whole(virt)],
+            out_specs=pl.BlockSpec((owners, columns * size, width), lambda i, s, b: (0, 0, 0)),
             scratch_shapes=[
                 pltpu.VMEM((owners * columns, listed, depth, size), F32),
                 pltpu.SemaphoreType.DMA((owners * columns,)),
             ],
         ),
-        out_shape=jax.ShapeDtypeStruct((total, columns * size, width), BF),
-        compiler_params=PARAMS,
+        out_shape=jax.ShapeDtypeStruct((owners, columns * size, width), BF),
+        compiler_params=pltpu.CompilerParams(vmem_limit_bytes=48 * 1024 * 1024),
         name="ladder",
-    )(slot, blk, *weights, turned, *sources, occ, virt, *extra)
+    )(slot, blk, *weights, turned, *sources, occ, virt)
 
 
 def swap(x, flip, n):
@@ -295,22 +287,18 @@
     occ = occ_energy.reshape(1, full_width)
     virt = facts[:, :size]
     mine = jnp.stack([blk, quarter_of(x_lo, blk)])
-    local = ladder_call(
-        slot, mine, 0, (integrals, beside), turned, (quarter(0), source_near), occ, virt
-    )
     done = ladder_call(
         slot,
         mine,
-        2,
-        (across, diagonal),
+        (0, 1, 2, 3),
+        (integrals, beside, across, diagonal),
         turned,
-        (source_far, source_diagonal),
+        (quarter(0), source_near, source_far, source_diagonal),
         occ,
         virt,
-        ready=local,
-        places=(0, 1, 2, 3),
     )
     done = lax.all_to_all(done, BLK, 0, 0, tiled=True)
+    x_lo, done = lax.optimization_barrier((x_lo, done))
     parts = []
     for q in range(nblk):
         usual, other = done[q], done[quarter_of(1, q)]

time: 210 us -> 207 us (0.986)
  blocking collectives: 73.3 us -> 88.8 us
  waiting for transfers between devices: 53.2 us -> 44 us
  starting transfers between devices: 58.8 us -> 52.2 us
    all_to_all x0 -> x1, blocking collectives: none -> 15.6 us  [per_device(): done = lax.all_to_all(done, BLK, 0, 0, tiled=True)]
    all_to_all x1 -> x0, waiting for transfers between devices: 9.35 us -> none  [per_device(): done = lax.all_to_all(done, BLK, 0, 0, tiled=True)]
    all_to_all x1 -> x0, starting transfers between devices: 6.5 us -> none  [per_device(): done = lax.all_to_all(done, BLK, 0, 0, tiled=True)]
    pallas_call x2 -> x1, Pallas kernels: 10.3 us -> 8.7 us  [ladder_call(): pl.pallas_call(body, grid_spec=pltpu.PrefetchScalarGridSpec(num_scalar_pr...]
  transfers between devices with their start and end apart: 11 -> 10, of which waited for: 4 -> 3; matrix products, arithmetic and copies ran while one was open for 1% -> 1% of each run, Pallas kernels for 6% -> 4%
where the time goes in v9:
time: 207 us
  blocking collectives  88.8 us (43%)
  starting transfers between devices  52.2 us (25%)
  waiting for transfers between devices  44 us (21%)
  Pallas kernels  16.8 us (8%)
  local copies, waits for them, and re-layouts  2.87 us (1%)
    all_to_all x1, blocking collectives, per_device(): x = lax.all_to_all(x, LINE, 0, 0, tiled=True)  73.3 us
    all_to_all x1, waiting for transfers between devices, per_device(): lax.all_to_all(outgoing, GRP + BLK, 0, 0, axis_index_groups=holders, tile...  28.1 us
    ppermute x8, starting transfers between devices, swap(): return lax.ppermute(x, BLK, [(b, b ^ flip) for b in range(n)])  26.2 us
    all_to_all x1, starting transfers between devices, per_device(): lax.all_to_all(x.reshape(ny * nz, nx * owned, width), PLANE, 0, 0, tiled=...  16.3 us
    all_to_all x1, blocking collectives, per_device(): done = lax.all_to_all(done, BLK, 0, 0, tiled=True)  15.6 us
    all_to_all x1, waiting for transfers between devices, per_device(): lax.all_to_all(x.reshape(ny * nz, nx * owned, width), PLANE, 0, 0, tiled=...  15.1 us
    all_to_all x1, starting transfers between devices, per_device(): lax.all_to_all(outgoing, GRP + BLK, 0, 0, axis_index_groups=holders, tile...  9.73 us
    pallas_call x1, Pallas kernels, ladder_call(): pl.pallas_call(body, grid_spec=pltpu.PrefetchScalarGridSpec(num_scalar_pr...  8.7 us
  transfers between devices with their start and end apart: 10, of which 3 were waited for; matrix products, arithmetic and copies ran while one was open for 1% of the time, Pallas kernels for 4%

profile of v9, /device:TPU:1, one launch (start us, length us, event | category | flops | bytes accessed | tf_op | source)
XLA Modules:
  0.0 206.7 jit_solution(3621599938064214428)
XLA Ops:
  0.0 5.5 %collective-permute-start.3 = (f32[4,12,128,128]{3,2,1,0:T(8,128)}, f32[4,12,128,128]{3,2,1,0:T(8,128)}, u32[]{:S(2)}, u32[]{:S(2)}) collective-permute-start(f32[4,12,128,128]{3,2,1,0:T(8,128)} %refs_0_.1), channel_id=1, source_target_pairs={{0,2},{1,3},{2,0},{3,1},{4,6},{5,7},{6,4},{7,5},{8,10},{9,11},{10,... | collective-permute-start | bytes 9437192 | tf_op jit(solution)/shard_map/ppermute | solution.py:225
  5.5 0.0 copy-start
  5.5 1.0 copy-done
  6.5 0.0 copy-start.3
  6.5 0.2 cut.1
  6.7 73.3 %all_to_all.20 = bf16[8,16,16,128]{3,2,1,0:T(8,128)(2,1)S(1)} all-to-all(bf16[8,16,16,128]{3,2,1,0:T(8,128)(2,1)S(1)} %cut.1), channel_id=1, replica_groups=mesh['y'=8,'xl'=2,'z'=8,'xh'=2,'k'=2] {'xl','xh','k'}, dimensions={0} | all-to-all | bytes 1048576 | tf_op jit(solution)/shard_map/all_to_all | solution.py:243
  79.9 0.8 copy.16
  80.8 16.3 %all-to-all-start.1 = ((bf16[64,32,128]{2,1,0:T(8,128)(2,1)}), bf16[64,32,128]{2,1,0:T(8,128)(2,1)S(1)}, u32[]{:S(2)}, u32[]{:S(2)}) async-start(bf16[64,32,128]{2,1,0:T(8,128)(2,1)} %bitcast.8), calls=%async_computation.1 | async-start | bytes 1048576 | tf_op jit(solution)/shard_map/all_to_all | solution.py:250
  97.1 0.0 copy-done.3
  97.1 0.1 reshape.39
  97.2 0.1 copy.18
  97.4 0.3 reshape.40.dest_ref
  97.7 0.7 rank.1
  98.4 15.1 %all-to-all-done.1 = bf16[64,32,128]{2,1,0:T(8,128)(2,1)S(1)} async-done(((bf16[64,32,128]{2,1,0:T(8,128)(2,1)}), bf16[64,32,128]{2,1,0:T(8,128)(2,1)S(1)}, u32[]{:S(2)}, u32[]{:S(2)}) %all-to-all-start.1) | async-done | bytes 524320 | tf_op jit(solution)/shard_map/all_to_all | solution.py:250
  113.5 5.9 %route.1 = bf16[8192,128]{1,0:T(8,128)(2,1)} custom-call(f32[128,2048]{1,0:T(8,128)S(1)} %get-tuple-element.11.slot_ref, f32[128,128]{1,0:T(8,128)S(1)} %get-tuple-element.12.early_ref, bf16[2048,128]{1,0:T(8,128)(2,1)S(1)} %bitcast.25), custom_call_target="tpu_custom_call" | custom-call | tf_op jit(solution)/shard_map/route/pallas_call | solution.py:95
  119.4 0.0 copy-start.5
  119.4 0.0 copy-start.4
  119.4 0.0 copy-start.2
  119.4 9.7 %all-to-all-start.2 = ((bf16[128,64,128]{2,1,0:T(8,128)(2,1)}), bf16[128,64,128]{2,1,0:T(8,128)(2,1)S(1)}, u32[]{:S(2)}, u32[]{:S(2)}) async-start(bf16[128,64,128]{2,1,0:T(8,128)(2,1)} %bitcast.10), calls=%async_computation.2 | async-start | bytes 4194304 | tf_op jit(solution)/shard_map/all_to_all | solution.py:260
  129.2 3.5 %collective-permute-start.2 = (f32[4,12,128,128]{3,2,1,0:T(8,128)}, f32[4,12,128,128]{3,2,1,0:T(8,128)}, u32[]{:S(2)}, u32[]{:S(2)}) collective-permute-start(f32[4,12,128,128]{3,2,1,0:T(8,128)} %refs_0_.1), channel_id=1, source_target_pairs={{0,1},{1,0},{2,3},{3,2},{4,5},{5,4},{6,7},{7,6},{8,9},{9,8},{10,11... | collective-permute-start | bytes 9437192 | tf_op jit(solution)/shard_map/ppermute | solution.py:225
  132.6 0.0 collective-permute-done.3.refs_2_
  132.7 1.9 collective-permute-start.4
  134.6 0.0 copy-done.5
  134.6 0.0 copy-done.4
  134.6 0.1 pad_maximum_fusion.3
  134.7 3.6 %collective-permute-start = (f32[4,256]{1,0:T(4,128)S(1)}, f32[4,256]{1,0:T(4,128)S(1)}, u32[]{:S(2)}, u32[]{:S(2)}) collective-permute-start(f32[4,256]{1,0:T(4,128)S(1)} %pad_maximum_fusion.3), channel_id=1, source_target_pairs={{0,2},{1,3},{2,0},{3,1},{4,6},{5,7},{6,4},{7,5},{8,10},{9,11},{10,... | collective-permute-start | bytes 12296 | tf_op jit(solution)/shard_map/ppermute | solution.py:225
  138.3 0.0 copy-done.2
  138.4 0.1 constant_dynamic-slice_fusion
  138.5 3.8 %collective-permute-start.7 = (bf16[512,128]{1,0:T(8,128)(2,1)S(1)}, bf16[512,128]{1,0:T(8,128)(2,1)S(1)}, u32[]{:S(2)}, u32[]{:S(2)}) collective-permute-start(bf16[512,128]{1,0:T(8,128)(2,1)S(1)} %get-tuple-element.19), channel_id=1, source_target_pairs={{0,3},{1,2},{2,1},{3,0},{4,7},{5,6},{6,5},{7,4},{8,11},{9,10},{10,... | collective-permute-start | bytes 393224 | tf_op jit(solution)/shard_map/ppermute | solution.py:225
  142.3 1.9 collective-permute-start.5
  144.2 0.0 collective-permute-done
  144.3 0.1 pad_maximum_fusion.2
  144.3 2.4 %collective-permute-start.1 = (f32[8,256]{1,0:T(8,128)S(1)}, f32[8,256]{1,0:T(8,128)S(1)}, u32[]{:S(2)}, u32[]{:S(2)}) collective-permute-start(f32[8,256]{1,0:T(8,128)S(1)} %pad_maximum_fusion.2), channel_id=1, source_target_pairs={{0,1},{1,0},{2,3},{3,2},{4,5},{5,4},{6,7},{7,6},{8,9},{9,8},{10,11... | collective-permute-start | bytes 24584 | tf_op jit(solution)/shard_map/ppermute | solution.py:225
  146.7 0.1 pad_add_fusion.blk_ref
  146.8 0.7 collective-permute-done.1
  147.5 3.6 %collective-permute-start.6 = (bf16[512,128]{1,0:T(8,128)(2,1)S(1)}, bf16[512,128]{1,0:T(8,128)(2,1)S(1)}, u32[]{:S(2)}, u32[]{:S(2)}) collective-permute-start(bf16[512,128]{1,0:T(8,128)(2,1)S(1)} %get-tuple-element.22), channel_id=1, source_target_pairs={{0,2},{1,3},{2,0},{3,1},{4,6},{5,7},{6,4},{7,5},{8,10},{9,11},{10,... | collective-permute-start | bytes 393224 | tf_op jit(solution)/shard_map/ppermute | solution.py:225
  151.2 0.1 pad_maximum_fusion.1
  151.3 0.1 copy.13
  151.4 0.4 select_reduce_fusion
  151.8 0.1 copy.15
  151.9 0.1 reshape.41.slot_ref
  151.9 0.0 copy-start.1
  152.0 28.1 %all-to-all-done.2.t_ref = bf16[128,64,128]{2,1,0:T(8,128)(2,1)S(1)} async-done(((bf16[128,64,128]{2,1,0:T(8,128)(2,1)}), bf16[128,64,128]{2,1,0:T(8,128)(2,1)S(1)}, u32[]{:S(2)}, u32[]{:S(2)}) %all-to-all-start.2) | async-done | bytes 2097184 | tf_op jit(solution)/shard_map/all_to_all | solution.py:260
  180.1 1.4 turn.1.refs_4_
  181.4 0.0 collective-permute-done.7.refs_8_
  181.4 0.0 collective-permute-done.5.refs_6_
  181.5 0.0 collective-permute-done.6.refs_7_
  181.5 0.0 collective-permute-done.2.refs_1_
  181.5 0.0 collective-permute-done.4.refs_3_
  181.5 0.0 copy-done.1
  181.5 8.7 %ladder.1 = bf16[4,512,128]{2,1,0:T(8,128)(2,1)S(1)} custom-call(s32[192]{0:T(256)S(1)} %reshape.41.slot_ref, s32[2]{0:T(128)S(1)} %pad_add_fusion.blk_ref, f32[4,12,128,128]{3,2,1,0:T(8,128)} %refs_0_.1, f32[4,12,128,128]{3,2,1,0:T(8,128)} %collective-permute-done.2.refs_1_, f32[4,12,128,128]{3,2,1,0:T(8,128)} %collective-permute-done.3.refs_2_, ...), custom_call_target="tpu_custom_call" | custom-call | tf_op jit(solution)/shard_map/ladder/pallas_call | solution.py:203
  190.2 15.6 %all_to_all.21 = bf16[4,512,128]{2,1,0:T(8,128)(2,1)S(1)} all-to-all(bf16[4,512,128]{2,1,0:T(8,128)(2,1)S(1)} %ladder.1), channel_id=1, replica_groups=mesh['y'=8,'xl'=2,'z'=8,'xh'=2,'k'=2] {'xh','k'}, dimensions={0} | all-to-all | bytes 1048576 | tf_op jit(solution)/shard_map/all_to_all | solution.py:300
  205.8 0.9 pad_maximum_fusion
  (6 shorter events, 0.1 us)
Async XLA Ops:
  0.0 132.7 %collective-permute-start.3 = (f32[4,12,128,128]{3,2,1,0:T(8,128)}, f32[4,12,128,128]{3,2,1,0:T(8,128)}, u32[]{:S(2)}, u32[]{:S(2)}) collective-permute-start(f32[4,12,128,128]{3,2,1,0:T(8,128)} %refs_0_.1), channel_id=1, source_target_pairs={{0,2},{1,3},{2,0},{3,1},{4,6},{5,7},{6,4},{7,5},{8,10},{9,11},{10,... | collective-permute-start | bytes 9437192 | tf_op jit(solution)/shard_map/ppermute | solution.py:225
  5.5 1.0 copy-start
  6.5 90.6 %copy-start.3 = (s32[2048,4]{0,1:T(4,128)S(1)}, s32[2048,4]{0,1:T(4,128)}, u32[]{:S(2)}) copy-start(s32[2048,4]{0,1:T(4,128)} %param.10) | copy-start | bytes 98308
  80.8 32.8 %all-to-all-start.1 = ((bf16[64,32,128]{2,1,0:T(8,128)(2,1)}), bf16[64,32,128]{2,1,0:T(8,128)(2,1)S(1)}, u32[]{:S(2)}, u32[]{:S(2)}) async-start(bf16[64,32,128]{2,1,0:T(8,128)(2,1)} %bitcast.8), calls=%async_computation.1 | async-start | bytes 1048576 | tf_op jit(solution)/shard_map/all_to_all | solution.py:250
  119.4 15.2 %copy-start.5 = (s32[4,12]{1,0:T(4,128)S(1)}, s32[4,12]{1,0:T(4,128)}, u32[]{:S(2)}) copy-start(s32[4,12]{1,0:T(4,128)} %param.9) | copy-start | bytes 580
  119.4 15.2 %copy-start.4 = (f32[512]{0:T(512)S(1)}, f32[512]{0:T(512)}, u32[]{:S(2)}) copy-start(f32[512]{0:T(512)} %param.13) | copy-start | bytes 6148
  119.4 18.9 %copy-start.2 = (bf16[512,512]{1,0:T(8,128)(2,1)S(1)}, bf16[512,512]{1,0:T(8,128)(2,1)}, u32[]{:S(2)}) copy-start(bf16[512,512]{1,0:T(8,128)(2,1)} %param.11) | copy-start | bytes 1572868
  119.4 60.6 %all-to-all-start.2 = ((bf16[128,64,128]{2,1,0:T(8,128)(2,1)}), bf16[128,64,128]{2,1,0:T(8,128)(2,1)S(1)}, u32[]{:S(2)}, u32[]{:S(2)}) async-start(bf16[128,64,128]{2,1,0:T(8,128)(2,1)} %bitcast.10), calls=%async_computation.2 | async-start | bytes 4194304 | tf_op jit(solution)/shard_map/all_to_all | solution.py:260
  129.2 52.3 %collective-permute-start.2 = (f32[4,12,128,128]{3,2,1,0:T(8,128)}, f32[4,12,128,128]{3,2,1,0:T(8,128)}, u32[]{:S(2)}, u32[]{:S(2)}) collective-permute-start(f32[4,12,128,128]{3,2,1,0:T(8,128)} %refs_0_.1), channel_id=1, source_target_pairs={{0,1},{1,0},{2,3},{3,2},{4,5},{5,4},{6,7},{7,6},{8,9},{9,8},{10,11... | collective-permute-start | bytes 9437192 | tf_op jit(solution)/shard_map/ppermute | solution.py:225
  132.7 48.8 %collective-permute-start.4 = (f32[4,12,128,128]{3,2,1,0:T(8,128)}, f32[4,12,128,128]{3,2,1,0:T(8,128)}, u32[]{:S(2)}, u32[]{:S(2)}) collective-permute-start(f32[4,12,128,128]{3,2,1,0:T(8,128)} %collective-permute-done.3.refs_2_), channel_id=1, source_target_pairs={{0,1},{1,0},{2,3},{3,2},{4,5},{5,4},{6,7},{7,6},{8,9},{9,8},{10,11... | collective-permute-start | bytes 9437192 | tf_op jit(solution)/shard_map/ppermute | solution.py:225
  134.7 9.5 %collective-permute-start = (f32[4,256]{1,0:T(4,128)S(1)}, f32[4,256]{1,0:T(4,128)S(1)}, u32[]{:S(2)}, u32[]{:S(2)}) collective-permute-start(f32[4,256]{1,0:T(4,128)S(1)} %pad_maximum_fusion.3), channel_id=1, source_target_pairs={{0,2},{1,3},{2,0},{3,1},{4,6},{5,7},{6,4},{7,5},{8,10},{9,11},{10,... | collective-permute-start | bytes 12296 | tf_op jit(solution)/shard_map/ppermute | solution.py:225
  138.5 43.0 %collective-permute-start.7 = (bf16[512,128]{1,0:T(8,128)(2,1)S(1)}, bf16[512,128]{1,0:T(8,128)(2,1)S(1)}, u32[]{:S(2)}, u32[]{:S(2)}) collective-permute-start(bf16[512,128]{1,0:T(8,128)(2,1)S(1)} %get-tuple-element.19), channel_id=1, source_target_pairs={{0,3},{1,2},{2,1},{3,0},{4,7},{5,6},{6,5},{7,4},{8,11},{9,10},{10,... | collective-permute-start | bytes 393224 | tf_op jit(solution)/shard_map/ppermute | solution.py:225
  142.3 39.1 %collective-permute-start.5 = (bf16[512,128]{1,0:T(8,128)(2,1)S(1)}, bf16[512,128]{1,0:T(8,128)(2,1)S(1)}, u32[]{:S(2)}, u32[]{:S(2)}) collective-permute-start(bf16[512,128]{1,0:T(8,128)(2,1)S(1)} %get-tuple-element.20), channel_id=1, source_target_pairs={{0,1},{1,0},{2,3},{3,2},{4,5},{5,4},{6,7},{7,6},{8,9},{9,8},{10,11... | collective-permute-start | bytes 393224 | tf_op jit(solution)/shard_map/ppermute | solution.py:225
  144.3 3.2 %collective-permute-start.1 = (f32[8,256]{1,0:T(8,128)S(1)}, f32[8,256]{1,0:T(8,128)S(1)}, u32[]{:S(2)}, u32[]{:S(2)}) collective-permute-start(f32[8,256]{1,0:T(8,128)S(1)} %pad_maximum_fusion.2), channel_id=1, source_target_pairs={{0,1},{1,0},{2,3},{3,2},{4,5},{5,4},{6,7},{7,6},{8,9},{9,8},{10,11... | collective-permute-start | bytes 24584 | tf_op jit(solution)/shard_map/ppermute | solution.py:225
  147.5 33.9 %collective-permute-start.6 = (bf16[512,128]{1,0:T(8,128)(2,1)S(1)}, bf16[512,128]{1,0:T(8,128)(2,1)S(1)}, u32[]{:S(2)}, u32[]{:S(2)}) collective-permute-start(bf16[512,128]{1,0:T(8,128)(2,1)S(1)} %get-tuple-element.22), channel_id=1, source_target_pairs={{0,2},{1,3},{2,0},{3,1},{4,6},{5,7},{6,4},{7,5},{8,10},{9,11},{10,... | collective-permute-start | bytes 393224 | tf_op jit(solution)/shard_map/ppermute | solution.py:225
  151.9 29.5 %copy-start.1 = (f32[512]{0:T(512)S(1)}, f32[512]{0:T(512)}, u32[]{:S(2)}) copy-start(f32[512]{0:T(512)} %param.12) | copy-start | bytes 6148

commit v10 on v9

--- a/solution.py
+++ b/solution.py
@@ -163,22 +163,25 @@
         w_refs = refs[:owners]
         t_ref = refs[owners]
         s_refs = refs[owners + 1 : 2 * owners + 1]
-        o_ref, v_ref, out_ref, held_ref, sems = refs[2 * owners + 1 :]
+        o_ref, v_ref = refs[2 * owners + 1 : 2 * owners + 3]
+        out_refs = refs[2 * owners + 3 : 3 * owners + 3]
+        held_ref, sems = refs[-2:]
         for m in range(owners):
             for n in range(columns):
                 at = m * columns + n
                 pltpu.make_async_copy(w_refs[m].at[n], held_ref.at[at], sems.at[at]).start()
         for m in range(owners):
-            to = blk_ref[0] ^ flips[m]
-
-            def some_columns(i, _, m=m, to=to):
+            owner = flips[m]
+
+            def some_columns(i, _, m=m, owner=owner):
                 for u in range(some):
                     n = i * some + u
                     at = m * columns + n
                     pltpu.make_async_copy(w_refs[m].at[n], held_ref.at[at], sems.at[at]).wait()
+                    named = owner * columns + n
                     right, left = [], []
                     for r in range(listed):
-                        s = slot_ref[at * listed + r]
+                        s = slot_ref[named * listed + r]
                         w = held_ref[at, r]
                         hi = w.astype(BF)
                         lo = (w - hi.astype(F32)).astype(BF)
@@ -191,8 +194,8 @@
                     part = (acc[:, :size] + acc[:, size:]).T
                     rows = pl.ds(n * size, size)
                     total = s_refs[m][rows, :].astype(F32) + part
-                    v = jnp.broadcast_to(v_ref[pl.ds(at, 1), :], (size, size)).T
-                    out_ref[to, rows, :] = (total / (v + o_ref[...])).astype(BF)
+                    v = jnp.broadcast_to(v_ref[pl.ds(named, 1), :], (size, size)).T
+                    out_refs[m][rows, :] = (total / (v + o_ref[...])).astype(BF)
                 return 0
 
             lax.fori_loop(0, columns // some, some_columns, 0)
@@ -209,16 +212,41 @@
             + [whole(turned)]
             + [whole(x) for x in sources]
             + [pl.BlockSpec((1, width), lambda i, s, b: (0, b[1])), whole(virt)],
-            out_specs=pl.BlockSpec((owners, columns * size, width), lambda i, s, b: (0, 0, 0)),
+            out_specs=[pl.BlockSpec((columns * size, width), lambda i, s, b: (0, 0))] * owners,
             scratch_shapes=[
                 pltpu.VMEM((owners * columns, listed, depth, size), F32),
                 pltpu.SemaphoreType.DMA((owners * columns,)),
             ],
         ),
-        out_shape=jax.ShapeDtypeStruct((owners, columns * size, width), BF),
+        out_shape=[jax.ShapeDtypeStruct((columns * size, width), BF)] * owners,
         compiler_params=pltpu.CompilerParams(vmem_limit_bytes=48 * 1024 * 1024),
         name="ladder",
     )(slot, blk, *weights, turned, *sources, occ, virt)
+
+
+def place_call(at, pieces):
+    rows, width = pieces[0].shape
+    count = len(pieces)
+
+    def body(at_ref, *refs):
+        for j in range(count):
+
+            @pl.when(pl.program_id(0) == j)
+            def _(j=j):
+                refs[-1][...] = refs[j][...]
+
+    return pl.pallas_call(
+        body,
+        grid_spec=pltpu.PrefetchScalarGridSpec(
+            num_scalar_prefetch=1,
+            grid=(count,),
+            in_specs=[pl.BlockSpec((rows, width), lambda i, b: (0, 0))] * count,
+            out_specs=pl.BlockSpec((rows, width), lambda i, b: (0, b[i])),
+        ),
+        out_shape=jax.ShapeDtypeStruct((rows, width * count), BF),
+        compiler_params=PARAMS,
+        name="place",
+    )(at, *pieces)
 
 
 def swap(x, flip, n):
@@ -287,23 +315,18 @@
     occ = occ_energy.reshape(1, full_width)
     virt = facts[:, :size]
     mine = jnp.stack([blk, quarter_of(x_lo, blk)])
-    done = ladder_call(
-        slot,
-        mine,
-        (0, 1, 2, 3),
-        (integrals, beside, across, diagonal),
-        turned,
-        (quarter(0), source_near, source_far, source_diagonal),
-        occ,
-        virt,
-    )
-    done = lax.all_to_all(done, BLK, 0, 0, tiled=True)
-    x_lo, done = lax.optimization_barrier((x_lo, done))
-    parts = []
-    for q in range(nblk):
-        usual, other = done[q], done[quarter_of(1, q)]
-        parts.append(usual if quarter_of(1, q) == q else jnp.where(x_lo == 1, other, usual))
-    return jnp.concatenate(parts, axis=1)
+    one, two = ladder_call(
+        slot, mine, (2, 3), (across, diagonal), turned, (source_far, source_diagonal), occ, virt
+    )
+    mine, one, two = lax.optimization_barrier((mine, one, two))
+    far = swap(one, 2, nblk)
+    farther = swap(two, 3, nblk)
+    home, near = ladder_call(
+        slot, mine, (0, 1), (integrals, beside), turned, (quarter(0), source_near), occ, virt
+    )
+    near = swap(near, 1, nblk)
+    at = jnp.stack([quarter_of(x_lo, blk ^ flip) for flip in range(nblk)])
+    return place_call(at, (home, near, far, farther))
 
 
 def solution(mesh):

time: 207 us -> 207 us (level)
  blocking collectives: 88.8 us -> 73.3 us
  starting transfers between devices: 52.2 us -> 63.6 us
  Pallas kernels: 16.8 us -> 19.8 us
    all_to_all x1 -> x0, blocking collectives: 15.6 us -> none  [per_device(): done = lax.all_to_all(done, BLK, 0, 0, tiled=True)]
    ppermute x8 -> x11, starting transfers between devices: 26.2 us -> 37.5 us  [swap(): return lax.ppermute(x, BLK, [(b, b ^ flip) for b in range(n)])]
    pallas_call x1 -> x2, Pallas kernels: 8.7 us -> 9.76 us  [ladder_call(): pl.pallas_call(body, grid_spec=pltpu.PrefetchScalarGridSpec(num_scalar_pr...]
  transfers between devices with their start and end apart: 10 -> 13, of which waited for: 3 -> 4; matrix products, arithmetic and copies ran while one was open for 1% -> 1% of each run, Pallas kernels for 4% -> 9%
where the time goes in v10:
time: 207 us; the launch traced here: 206 us
  blocking collectives  73.3 us (35%)
  starting transfers between devices  63.6 us (31%)
  waiting for transfers between devices  45.2 us (22%)
  Pallas kernels  19.8 us (10%)
  local copies, waits for them, and re-layouts  2.88 us (1%)
    all_to_all x1, blocking collectives, per_device(): x = lax.all_to_all(x, LINE, 0, 0, tiled=True)  73.3 us
    ppermute x11, starting transfers between devices, swap(): return lax.ppermute(x, BLK, [(b, b ^ flip) for b in range(n)])  37.5 us
    all_to_all x1, waiting for transfers between devices, per_device(): lax.all_to_all(outgoing, GRP + BLK, 0, 0, axis_index_groups=holders, tile...  28.1 us
    all_to_all x1, starting transfers between devices, per_device(): lax.all_to_all(x.reshape(ny * nz, nx * owned, width), PLANE, 0, 0, tiled=...  16.3 us
    all_to_all x1, waiting for transfers between devices, per_device(): lax.all_to_all(x.reshape(ny * nz, nx * owned, width), PLANE, 0, 0, tiled=...  15.1 us
    pallas_call x2, Pallas kernels, ladder_call(): pl.pallas_call(body, grid_spec=pltpu.PrefetchScalarGridSpec(num_scalar_pr...  9.76 us
    all_to_all x1, starting transfers between devices, per_device(): lax.all_to_all(outgoing, GRP + BLK, 0, 0, axis_index_groups=holders, tile...  9.73 us
    pallas_call x1, Pallas kernels, route_call(): pl.pallas_call(body, grid=(groups // step,), in_specs=[pl.BlockSpec((step...  5.89 us
  transfers between devices with their start and end apart: 13, of which 4 were waited for; matrix products, arithmetic and copies ran while one was open for 1% of the time, Pallas kernels for 9%

profile of v10, /device:TPU:1, one launch (start us, length us, event | category | flops | bytes accessed | tf_op | source)
XLA Modules:
  0.0 205.9 jit_solution(1396407132185376416)
XLA Ops:
  0.0 5.5 %collective-permute-start.2 = (f32[4,12,128,128]{3,2,1,0:T(8,128)}, f32[4,12,128,128]{3,2,1,0:T(8,128)}, u32[]{:S(2)}, u32[]{:S(2)}) collective-permute-start(f32[4,12,128,128]{3,2,1,0:T(8,128)} %refs_0_.1), channel_id=1, source_target_pairs={{0,2},{1,3},{2,0},{3,1},{4,6},{5,7},{6,4},{7,5},{8,10},{9,11},{10,... | collective-permute-start | bytes 9437192 | tf_op jit(solution)/shard_map/ppermute | solution.py:253
  5.5 0.0 copy-start.1
  5.5 1.0 copy-done.1
  6.5 0.0 copy-start.4
  6.5 0.2 cut.1
  6.7 73.3 %all_to_all.15 = bf16[8,16,16,128]{3,2,1,0:T(8,128)(2,1)S(1)} all-to-all(bf16[8,16,16,128]{3,2,1,0:T(8,128)(2,1)S(1)} %cut.1), channel_id=1, replica_groups=mesh['y'=8,'xl'=2,'z'=8,'xh'=2,'k'=2] {'xl','xh','k'}, dimensions={0} | all-to-all | bytes 1048576 | tf_op jit(solution)/shard_map/all_to_all | solution.py:271
  79.9 0.8 copy.16
  80.8 16.3 %all-to-all-start.1 = ((bf16[64,32,128]{2,1,0:T(8,128)(2,1)}), bf16[64,32,128]{2,1,0:T(8,128)(2,1)S(1)}, u32[]{:S(2)}, u32[]{:S(2)}) async-start(bf16[64,32,128]{2,1,0:T(8,128)(2,1)} %bitcast.11), calls=%async_computation.1 | async-start | bytes 1048576 | tf_op jit(solution)/shard_map/all_to_all | solution.py:278
  97.1 0.0 copy-done.4
  97.1 0.1 reshape.35
  97.2 0.1 copy.18
  97.4 0.3 reshape.36.dest_ref
  97.7 0.7 rank.1
  98.4 15.1 %all-to-all-done.1 = bf16[64,32,128]{2,1,0:T(8,128)(2,1)S(1)} async-done(((bf16[64,32,128]{2,1,0:T(8,128)(2,1)}), bf16[64,32,128]{2,1,0:T(8,128)(2,1)S(1)}, u32[]{:S(2)}, u32[]{:S(2)}) %all-to-all-start.1) | async-done | bytes 524320 | tf_op jit(solution)/shard_map/all_to_all | solution.py:278
  113.5 5.9 %route.1 = bf16[8192,128]{1,0:T(8,128)(2,1)} custom-call(f32[128,2048]{1,0:T(8,128)S(1)} %get-tuple-element.16.slot_ref, f32[128,128]{1,0:T(8,128)S(1)} %get-tuple-element.17.early_ref, bf16[2048,128]{1,0:T(8,128)(2,1)S(1)} %bitcast.20), custom_call_target="tpu_custom_call" | custom-call | tf_op jit(solution)/shard_map/route/pallas_call | solution.py:95
  119.4 0.0 copy-start.6
  119.4 0.0 copy-start.5
  119.4 0.0 copy-start.3
  119.4 9.7 %all-to-all-start.2 = ((bf16[128,64,128]{2,1,0:T(8,128)(2,1)}), bf16[128,64,128]{2,1,0:T(8,128)(2,1)S(1)}, u32[]{:S(2)}, u32[]{:S(2)}) async-start(bf16[128,64,128]{2,1,0:T(8,128)(2,1)} %bitcast.13), calls=%async_computation.2 | async-start | bytes 4194304 | tf_op jit(solution)/shard_map/all_to_all | solution.py:288
  129.2 0.0 collective-permute-done.2.refs_0_
  129.2 3.5 %collective-permute-start.3 = (f32[4,12,128,128]{3,2,1,0:T(8,128)}, f32[4,12,128,128]{3,2,1,0:T(8,128)}, u32[]{:S(2)}, u32[]{:S(2)}) collective-permute-start(f32[4,12,128,128]{3,2,1,0:T(8,128)} %collective-permute-done.2.refs_0_), channel_id=1, source_target_pairs={{0,1},{1,0},{2,3},{3,2},{4,5},{5,4},{6,7},{7,6},{8,9},{9,8},{10,11... | collective-permute-start | bytes 9437192 | tf_op jit(solution)/shard_map/ppermute | solution.py:253
  132.7 1.9 collective-permute-start.6
  134.6 0.0 copy-done.6
  134.6 0.0 copy-done.5
  134.6 0.1 pad_maximum_fusion.2
  134.7 3.6 %collective-permute-start = (f32[4,256]{1,0:T(4,128)S(1)}, f32[4,256]{1,0:T(4,128)S(1)}, u32[]{:S(2)}, u32[]{:S(2)}) collective-permute-start(f32[4,256]{1,0:T(4,128)S(1)} %pad_maximum_fusion.2), channel_id=1, source_target_pairs={{0,2},{1,3},{2,0},{3,1},{4,6},{5,7},{6,4},{7,5},{8,10},{9,11},{10,... | collective-permute-start | bytes 12296 | tf_op jit(solution)/shard_map/ppermute | solution.py:253
  138.4 0.0 copy-done.3
  138.4 0.1 constant_dynamic-slice_fusion
  138.5 2.7 %collective-permute-start.7 = (bf16[512,128]{1,0:T(8,128)(2,1)S(1)}, bf16[512,128]{1,0:T(8,128)(2,1)S(1)}, u32[]{:S(2)}, u32[]{:S(2)}) collective-permute-start(bf16[512,128]{1,0:T(8,128)(2,1)S(1)} %get-tuple-element.25), channel_id=1, source_target_pairs={{0,1},{1,0},{2,3},{3,2},{4,5},{5,4},{6,7},{7,6},{8,9},{9,8},{10,11... | collective-permute-start | bytes 393224 | tf_op jit(solution)/shard_map/ppermute | solution.py:253
  141.2 3.1 %collective-permute-start.5 = (bf16[512,128]{1,0:T(8,128)(2,1)S(1)}, bf16[512,128]{1,0:T(8,128)(2,1)S(1)}, u32[]{:S(2)}, u32[]{:S(2)}) collective-permute-start(bf16[512,128]{1,0:T(8,128)(2,1)S(1)} %get-tuple-element.26), channel_id=1, source_target_pairs={{0,3},{1,2},{2,1},{3,0},{4,7},{5,6},{6,5},{7,4},{8,11},{9,10},{10,... | collective-permute-start | bytes 393224 | tf_op jit(solution)/shard_map/ppermute | solution.py:253
  144.3 0.0 collective-permute-done
  144.3 0.1 pad_maximum_fusion.1
  144.4 2.4 %collective-permute-start.1 = (f32[8,256]{1,0:T(8,128)S(1)}, f32[8,256]{1,0:T(8,128)S(1)}, u32[]{:S(2)}, u32[]{:S(2)}) collective-permute-start(f32[8,256]{1,0:T(8,128)S(1)} %pad_maximum_fusion.1), channel_id=1, source_target_pairs={{0,1},{1,0},{2,3},{3,2},{4,5},{5,4},{6,7},{7,6},{8,9},{9,8},{10,11... | collective-permute-start | bytes 24584 | tf_op jit(solution)/shard_map/ppermute | solution.py:253
  146.8 0.1 pad_add_fusion.1.blk_ref
  146.8 0.7 collective-permute-done.1
  147.6 3.6 %collective-permute-start.4 = (bf16[512,128]{1,0:T(8,128)(2,1)S(1)}, bf16[512,128]{1,0:T(8,128)(2,1)S(1)}, u32[]{:S(2)}, u32[]{:S(2)}) collective-permute-start(bf16[512,128]{1,0:T(8,128)(2,1)S(1)} %get-tuple-element.27), channel_id=1, source_target_pairs={{0,2},{1,3},{2,0},{3,1},{4,6},{5,7},{6,4},{7,5},{8,10},{9,11},{10,... | collective-permute-start | bytes 393224 | tf_op jit(solution)/shard_map/ppermute | solution.py:253
  151.2 0.1 pad_maximum_fusion
  151.3 0.1 copy.13
  151.4 0.4 select_reduce_fusion
  151.8 0.1 copy.15
  151.9 0.1 reshape.37.slot_ref
  152.0 0.0 copy-start.2
  152.0 28.1 %all-to-all-done.2.t_ref = bf16[128,64,128]{2,1,0:T(8,128)(2,1)S(1)} async-done(((bf16[128,64,128]{2,1,0:T(8,128)(2,1)}), bf16[128,64,128]{2,1,0:T(8,128)(2,1)S(1)}, u32[]{:S(2)}, u32[]{:S(2)}) %all-to-all-start.2) | async-done | bytes 2097184 | tf_op jit(solution)/shard_map/all_to_all | solution.py:288
  180.1 1.4 turn.1.refs_2_
  181.4 0.0 collective-permute-done.5.refs_4_
  181.5 0.0 collective-permute-done.4.refs_3_
  181.5 0.0 collective-permute-done.3.refs_1_
  181.5 0.0 copy-done.2
  181.5 0.0 copy-start
  181.5 5.5 %ladder.2 = (bf16[512,128]{1,0:T(8,128)(2,1)S(1)}, bf16[512,128]{1,0:T(8,128)(2,1)S(1)}) custom-call(s32[192]{0:T(256)S(1)} %reshape.37.slot_ref, s32[2]{0:T(128)S(1)} %pad_add_fusion.1.blk_ref, f32[4,12,128,128]{3,2,1,0:T(8,128)} %collective-permute-done.2.refs_0_, f32[4,12,128,128]{3,2,1,0:T(8,128)} %collective-permute-done.3.refs_1_, ...), custom_call_target="tpu_custom_call" | custom-call | tf_op jit(solution)/shard_map/ladder/pallas_call | solution.py:206
  187.0 2.2 %collective-permute-start.9 = (bf16[512,128]{1,0:T(8,128)(2,1)S(1)}, bf16[512,128]{1,0:T(8,128)(2,1)S(1)}, u32[]{:S(2)}, u32[]{:S(2)}) collective-permute-start(bf16[512,128]{1,0:T(8,128)(2,1)S(1)} %get-tuple-element.23), channel_id=1, source_target_pairs={{0,2},{1,3},{2,0},{3,1},{4,6},{5,7},{6,4},{7,5},{8,10},{9,11},{10,... | collective-permute-start | bytes 393224 | tf_op jit(solution)/shard_map/ppermute | solution.py:253
  189.2 7.2 %collective-permute-start.10 = (bf16[512,128]{1,0:T(8,128)(2,1)S(1)}, bf16[512,128]{1,0:T(8,128)(2,1)S(1)}, u32[]{:S(2)}, u32[]{:S(2)}) collective-permute-start(bf16[512,128]{1,0:T(8,128)(2,1)S(1)} %get-tuple-element.24), channel_id=1, source_target_pairs={{0,3},{1,2},{2,1},{3,0},{4,7},{5,6},{6,5},{7,4},{8,11},{9,10},{10,... | collective-permute-start | bytes 393224 | tf_op jit(solution)/shard_map/ppermute | solution.py:253
  196.4 0.0 collective-permute-done.7.refs_4_
  196.4 0.0 collective-permute-done.6.refs_1_
  196.4 0.0 copy-done
  196.4 4.3 %ladder.3 = (bf16[512,128]{1,0:T(8,128)(2,1)S(1)}, bf16[512,128]{1,0:T(8,128)(2,1)S(1)}) custom-call(s32[192]{0:T(256)S(1)} %reshape.37.slot_ref, s32[2]{0:T(128)S(1)} %pad_add_fusion.1.blk_ref, f32[4,12,128,128]{3,2,1,0:T(8,128)S(1)} %copy-done, f32[4,12,128,128]{3,2,1,0:T(8,128)} %collective-permute-done.6.refs_1_, bf16[64,128,128]{2,1,0:T(8,128)(2,1)S(1)} %turn.1.refs_2_, ...), custom_call_target="tpu_custom_call" | custom-call | tf_op jit(solution)/shard_map/ladder/pallas_call | solution.py:206
  200.7 1.9 collective-permute-start.8
  202.6 0.1 pad_add_fusion.at_ref
  202.7 0.0 collective-permute-done.9.refs_2_
  202.7 0.0 collective-permute-done.10.refs_3_
  202.7 1.2 collective-permute-done.8.refs_1_
  204.0 2.0 place.1
  (5 shorter events, 0.0 us)
Async XLA Ops:
  0.0 129.2 %collective-permute-start.2 = (f32[4,12,128,128]{3,2,1,0:T(8,128)}, f32[4,12,128,128]{3,2,1,0:T(8,128)}, u32[]{:S(2)}, u32[]{:S(2)}) collective-permute-start(f32[4,12,128,128]{3,2,1,0:T(8,128)} %refs_0_.1), channel_id=1, source_target_pairs={{0,2},{1,3},{2,0},{3,1},{4,6},{5,7},{6,4},{7,5},{8,10},{9,11},{10,... | collective-permute-start | bytes 9437192 | tf_op jit(solution)/shard_map/ppermute | solution.py:253
  5.5 1.0 copy-start.1
  6.5 90.6 %copy-start.4 = (s32[2048,4]{0,1:T(4,128)S(1)}, s32[2048,4]{0,1:T(4,128)}, u32[]{:S(2)}) copy-start(s32[2048,4]{0,1:T(4,128)} %param.10) | copy-start | bytes 98308
  80.8 32.8 %all-to-all-start.1 = ((bf16[64,32,128]{2,1,0:T(8,128)(2,1)}), bf16[64,32,128]{2,1,0:T(8,128)(2,1)S(1)}, u32[]{:S(2)}, u32[]{:S(2)}) async-start(bf16[64,32,128]{2,1,0:T(8,128)(2,1)} %bitcast.11), calls=%async_computation.1 | async-start | bytes 1048576 | tf_op jit(solution)/shard_map/all_to_all | solution.py:278
  119.4 15.2 %copy-start.6 = (s32[4,12]{1,0:T(4,128)S(1)}, s32[4,12]{1,0:T(4,128)}, u32[]{:S(2)}) copy-start(s32[4,12]{1,0:T(4,128)} %param.9) | copy-start | bytes 580
  119.4 15.2 %copy-start.5 = (f32[512]{0:T(512)S(1)}, f32[512]{0:T(512)}, u32[]{:S(2)}) copy-start(f32[512]{0:T(512)} %param.13) | copy-start | bytes 6148
  119.4 18.9 %copy-start.3 = (bf16[512,512]{1,0:T(8,128)(2,1)S(1)}, bf16[512,512]{1,0:T(8,128)(2,1)}, u32[]{:S(2)}) copy-start(bf16[512,512]{1,0:T(8,128)(2,1)} %param.11) | copy-start | bytes 1572868
  119.4 60.6 %all-to-all-start.2 = ((bf16[128,64,128]{2,1,0:T(8,128)(2,1)}), bf16[128,64,128]{2,1,0:T(8,128)(2,1)S(1)}, u32[]{:S(2)}, u32[]{:S(2)}) async-start(bf16[128,64,128]{2,1,0:T(8,128)(2,1)} %bitcast.13), calls=%async_computation.2 | async-start | bytes 4194304 | tf_op jit(solution)/shard_map/all_to_all | solution.py:288
  129.2 52.3 %collective-permute-start.3 = (f32[4,12,128,128]{3,2,1,0:T(8,128)}, f32[4,12,128,128]{3,2,1,0:T(8,128)}, u32[]{:S(2)}, u32[]{:S(2)}) collective-permute-start(f32[4,12,128,128]{3,2,1,0:T(8,128)} %collective-permute-done.2.refs_0_), channel_id=1, source_target_pairs={{0,1},{1,0},{2,3},{3,2},{4,5},{5,4},{6,7},{7,6},{8,9},{9,8},{10,11... | collective-permute-start | bytes 9437192 | tf_op jit(solution)/shard_map/ppermute | solution.py:253
  132.7 63.7 %collective-permute-start.6 = (f32[4,12,128,128]{3,2,1,0:T(8,128)}, f32[4,12,128,128]{3,2,1,0:T(8,128)}, u32[]{:S(2)}, u32[]{:S(2)}) collective-permute-start(f32[4,12,128,128]{3,2,1,0:T(8,128)} %refs_0_.1), channel_id=1, source_target_pairs={{0,1},{1,0},{2,3},{3,2},{4,5},{5,4},{6,7},{7,6},{8,9},{9,8},{10,11... | collective-permute-start | bytes 9437192 | tf_op jit(solution)/shard_map/ppermute | solution.py:253
  134.7 9.5 %collective-permute-start = (f32[4,256]{1,0:T(4,128)S(1)}, f32[4,256]{1,0:T(4,128)S(1)}, u32[]{:S(2)}, u32[]{:S(2)}) collective-permute-start(f32[4,256]{1,0:T(4,128)S(1)} %pad_maximum_fusion.2), channel_id=1, source_target_pairs={{0,2},{1,3},{2,0},{3,1},{4,6},{5,7},{6,4},{7,5},{8,10},{9,11},{10,... | collective-permute-start | bytes 12296 | tf_op jit(solution)/shard_map/ppermute | solution.py:253
  138.5 57.9 %collective-permute-start.7 = (bf16[512,128]{1,0:T(8,128)(2,1)S(1)}, bf16[512,128]{1,0:T(8,128)(2,1)S(1)}, u32[]{:S(2)}, u32[]{:S(2)}) collective-permute-start(bf16[512,128]{1,0:T(8,128)(2,1)S(1)} %get-tuple-element.25), channel_id=1, source_target_pairs={{0,1},{1,0},{2,3},{3,2},{4,5},{5,4},{6,7},{7,6},{8,9},{9,8},{10,11... | collective-permute-start | bytes 393224 | tf_op jit(solution)/shard_map/ppermute | solution.py:253
  141.2 40.3 %collective-permute-start.5 = (bf16[512,128]{1,0:T(8,128)(2,1)S(1)}, bf16[512,128]{1,0:T(8,128)(2,1)S(1)}, u32[]{:S(2)}, u32[]{:S(2)}) collective-permute-start(bf16[512,128]{1,0:T(8,128)(2,1)S(1)} %get-tuple-element.26), channel_id=1, source_target_pairs={{0,3},{1,2},{2,1},{3,0},{4,7},{5,6},{6,5},{7,4},{8,11},{9,10},{10,... | collective-permute-start | bytes 393224 | tf_op jit(solution)/shard_map/ppermute | solution.py:253
  144.4 3.2 %collective-permute-start.1 = (f32[8,256]{1,0:T(8,128)S(1)}, f32[8,256]{1,0:T(8,128)S(1)}, u32[]{:S(2)}, u32[]{:S(2)}) collective-permute-start(f32[8,256]{1,0:T(8,128)S(1)} %pad_maximum_fusion.1), channel_id=1, source_target_pairs={{0,1},{1,0},{2,3},{3,2},{4,5},{5,4},{6,7},{7,6},{8,9},{9,8},{10,11... | collective-permute-start | bytes 24584 | tf_op jit(solution)/shard_map/ppermute | solution.py:253
  147.6 33.9 %collective-permute-start.4 = (bf16[512,128]{1,0:T(8,128)(2,1)S(1)}, bf16[512,128]{1,0:T(8,128)(2,1)S(1)}, u32[]{:S(2)}, u32[]{:S(2)}) collective-permute-start(bf16[512,128]{1,0:T(8,128)(2,1)S(1)} %get-tuple-element.27), channel_id=1, source_target_pairs={{0,2},{1,3},{2,0},{3,1},{4,6},{5,7},{6,4},{7,5},{8,10},{9,11},{10,... | collective-permute-start | bytes 393224 | tf_op jit(solution)/shard_map/ppermute | solution.py:253
  152.0 29.5 %copy-start.2 = (f32[512]{0:T(512)S(1)}, f32[512]{0:T(512)}, u32[]{:S(2)}) copy-start(f32[512]{0:T(512)} %param.12) | copy-start | bytes 6148
  181.5 14.9 %copy-start = (f32[4,12,128,128]{3,2,1,0:T(8,128)S(1)}, f32[4,12,128,128]{3,2,1,0:T(8,128)}, u32[]{:S(2)}) copy-start(f32[4,12,128,128]{3,2,1,0:T(8,128)} %refs_0_.1) | copy-start | bytes 9437188
  187.0 15.8 %collective-permute-start.9 = (bf16[512,128]{1,0:T(8,128)(2,1)S(1)}, bf16[512,128]{1,0:T(8,128)(2,1)S(1)}, u32[]{:S(2)}, u32[]{:S(2)}) collective-permute-start(bf16[512,128]{1,0:T(8,128)(2,1)S(1)} %get-tuple-element.23), channel_id=1, source_target_pairs={{0,2},{1,3},{2,0},{3,1},{4,6},{5,7},{6,4},{7,5},{8,10},{9,11},{10,... | collective-permute-start | bytes 393224 | tf_op jit(solution)/shard_map/ppermute | solution.py:253
  189.2 13.5 %collective-permute-start.10 = (bf16[512,128]{1,0:T(8,128)(2,1)S(1)}, bf16[512,128]{1,0:T(8,128)(2,1)S(1)}, u32[]{:S(2)}, u32[]{:S(2)}) collective-permute-start(bf16[512,128]{1,0:T(8,128)(2,1)S(1)} %get-tuple-element.24), channel_id=1, source_target_pairs={{0,3},{1,2},{2,1},{3,0},{4,7},{5,6},{6,5},{7,4},{8,11},{9,10},{10,... | collective-permute-start | bytes 393224 | tf_op jit(solution)/shard_map/ppermute | solution.py:253
  200.7 3.2 %collective-permute-start.8 = (bf16[512,128]{1,0:T(8,128)(2,1)S(1)}, bf16[512,128]{1,0:T(8,128)(2,1)S(1)}, u32[]{:S(2)}, u32[]{:S(2)}) collective-permute-start(bf16[512,128]{1,0:T(8,128)(2,1)S(1)} %get-tuple-element.22), channel_id=1, source_target_pairs={{0,1},{1,0},{2,3},{3,2},{4,5},{5,4},{6,7},{7,6},{8,9},{9,8},{10,11... | collective-permute-start | bytes 393224 | tf_op jit(solution)/shard_map/ppermute | solution.py:253

commit v11 on v10

--- a/solution.py
+++ b/solution.py
@@ -224,31 +224,6 @@
     )(slot, blk, *weights, turned, *sources, occ, virt)
 
 
-def place_call(at, pieces):
-    rows, width = pieces[0].shape
-    count = len(pieces)
-
-    def body(at_ref, *refs):
-        for j in range(count):
-
-            @pl.when(pl.program_id(0) == j)
-            def _(j=j):
-                refs[-1][...] = refs[j][...]
-
-    return pl.pallas_call(
-        body,
-        grid_spec=pltpu.PrefetchScalarGridSpec(
-            num_scalar_prefetch=1,
-            grid=(count,),
-            in_specs=[pl.BlockSpec((rows, width), lambda i, b: (0, 0))] * count,
-            out_specs=pl.BlockSpec((rows, width), lambda i, b: (0, b[i])),
-        ),
-        out_shape=jax.ShapeDtypeStruct((rows, width * count), BF),
-        compiler_params=PARAMS,
-        name="place",
-    )(at, *pieces)
-
-
 def swap(x, flip, n):
     return lax.ppermute(x, BLK, [(b, b ^ flip) for b in range(n)])
 
@@ -325,8 +300,13 @@
         slot, mine, (0, 1), (integrals, beside), turned, (quarter(0), source_near), occ, virt
     )
     near = swap(near, 1, nblk)
-    at = jnp.stack([quarter_of(x_lo, blk ^ flip) for flip in range(nblk)])
-    return place_call(at, (home, near, far, farther))
+    parts = []
+    for q in range(nblk):
+        flip = blk ^ quarter_of(x_lo, q)
+        low = jnp.where(flip == 0, home, near)
+        high = jnp.where(flip == 2, far, farther)
+        parts.append(jnp.where(flip < 2, low, high))
+    return jnp.concatenate(parts, axis=1)
 
 
 def solution(mesh):

time: 207 us -> 210 us (1.014)
  waiting for transfers between devices: 45.2 us -> 49.5 us
    ppermute x11, waiting for transfers between devices: 1.98 us -> 6.59 us  [swap(): return lax.ppermute(x, BLK, [(b, b ^ flip) for b in range(n)])]
  transfers between devices with their start and end apart: 13 -> 13, of which waited for: 4 -> 5; matrix products, arithmetic and copies ran while one was open for 1% -> 1% of each run, Pallas kernels for 9% -> 7%
where the time goes in v11:
time: 210 us; the launch traced here: 209 us
  blocking collectives  73.3 us (35%)
  starting transfers between devices  63.2 us (30%)
  waiting for transfers between devices  49.5 us (24%)
  Pallas kernels  17.9 us (9%)
  local copies, waits for them, and re-layouts  2.87 us (1%)
    all_to_all x1, blocking collectives, per_device(): x = lax.all_to_all(x, LINE, 0, 0, tiled=True)  73.3 us
    ppermute x11, starting transfers between devices, swap(): return lax.ppermute(x, BLK, [(b, b ^ flip) for b in range(n)])  37.2 us
    all_to_all x1, waiting for transfers between devices, per_device(): lax.all_to_all(outgoing, GRP + BLK, 0, 0, axis_index_groups=holders, tile...  27.8 us
    all_to_all x1, starting transfers between devices, per_device(): lax.all_to_all(x.reshape(ny * nz, nx * owned, width), PLANE, 0, 0, tiled=...  16.3 us
    all_to_all x1, waiting for transfers between devices, per_device(): lax.all_to_all(x.reshape(ny * nz, nx * owned, width), PLANE, 0, 0, tiled=...  15.1 us
    pallas_call x2, Pallas kernels, ladder_call(): pl.pallas_call(body, grid_spec=pltpu.PrefetchScalarGridSpec(num_scalar_pr...  9.76 us
    all_to_all x1, starting transfers between devices, per_device(): lax.all_to_all(outgoing, GRP + BLK, 0, 0, axis_index_groups=holders, tile...  9.73 us
    ppermute x11, waiting for transfers between devices, swap(): return lax.ppermute(x, BLK, [(b, b ^ flip) for b in range(n)])  6.59 us
  transfers between devices with their start and end apart: 13, of which 5 were waited for; matrix products, arithmetic and copies ran while one was open for 1% of the time, Pallas kernels for 7%

profile of v11, /device:TPU:1, one launch (start us, length us, event | category | flops | bytes accessed | tf_op | source)
XLA Modules:
  0.0 208.9 jit_solution(17148565511697408697)
XLA Ops:
  0.0 5.5 %collective-permute-start.2 = (f32[4,12,128,128]{3,2,1,0:T(8,128)}, f32[4,12,128,128]{3,2,1,0:T(8,128)}, u32[]{:S(2)}, u32[]{:S(2)}) collective-permute-start(f32[4,12,128,128]{3,2,1,0:T(8,128)} %refs_0_.1), channel_id=1, source_target_pairs={{0,2},{1,3},{2,0},{3,1},{4,6},{5,7},{6,4},{7,5},{8,10},{9,11},{10,... | collective-permute-start | bytes 9437192 | tf_op jit(solution)/shard_map/ppermute | solution.py:228
  5.5 0.0 copy-start.1
  5.5 1.0 copy-done.1
  6.5 0.0 copy-start.4
  6.5 0.2 cut.1
  6.7 73.3 %all_to_all.15 = bf16[8,16,16,128]{3,2,1,0:T(8,128)(2,1)S(1)} all-to-all(bf16[8,16,16,128]{3,2,1,0:T(8,128)(2,1)S(1)} %cut.1), channel_id=1, replica_groups=mesh['y'=8,'xl'=2,'z'=8,'xh'=2,'k'=2] {'xl','xh','k'}, dimensions={0} | all-to-all | bytes 1048576 | tf_op jit(solution)/shard_map/all_to_all | solution.py:246
  79.9 0.8 copy.16
  80.8 16.3 %all-to-all-start.1 = ((bf16[64,32,128]{2,1,0:T(8,128)(2,1)}), bf16[64,32,128]{2,1,0:T(8,128)(2,1)S(1)}, u32[]{:S(2)}, u32[]{:S(2)}) async-start(bf16[64,32,128]{2,1,0:T(8,128)(2,1)} %bitcast.8), calls=%async_computation.1 | async-start | bytes 1048576 | tf_op jit(solution)/shard_map/all_to_all | solution.py:253
  97.1 0.0 copy-done.4
  97.1 0.1 reshape.35
  97.2 0.1 copy.18
  97.4 0.3 reshape.36.dest_ref
  97.7 0.7 rank.1
  98.4 15.1 %all-to-all-done.1 = bf16[64,32,128]{2,1,0:T(8,128)(2,1)S(1)} async-done(((bf16[64,32,128]{2,1,0:T(8,128)(2,1)}), bf16[64,32,128]{2,1,0:T(8,128)(2,1)S(1)}, u32[]{:S(2)}, u32[]{:S(2)}) %all-to-all-start.1) | async-done | bytes 524320 | tf_op jit(solution)/shard_map/all_to_all | solution.py:253
  113.5 5.9 %route.1 = bf16[8192,128]{1,0:T(8,128)(2,1)} custom-call(f32[128,2048]{1,0:T(8,128)S(1)} %get-tuple-element.16.slot_ref, f32[128,128]{1,0:T(8,128)S(1)} %get-tuple-element.17.early_ref, bf16[2048,128]{1,0:T(8,128)(2,1)S(1)} %bitcast.17), custom_call_target="tpu_custom_call" | custom-call | tf_op jit(solution)/shard_map/route/pallas_call | solution.py:95
  119.5 0.0 copy-start.6
  119.5 0.0 copy-start.5
  119.5 0.0 copy-start.3
  119.5 9.7 %all-to-all-start.2 = ((bf16[128,64,128]{2,1,0:T(8,128)(2,1)}), bf16[128,64,128]{2,1,0:T(8,128)(2,1)S(1)}, u32[]{:S(2)}, u32[]{:S(2)}) async-start(bf16[128,64,128]{2,1,0:T(8,128)(2,1)} %bitcast.10), calls=%async_computation.2 | async-start | bytes 4194304 | tf_op jit(solution)/shard_map/all_to_all | solution.py:263
  129.2 0.0 collective-permute-done.2.refs_0_
  129.2 3.5 %collective-permute-start.3 = (f32[4,12,128,128]{3,2,1,0:T(8,128)}, f32[4,12,128,128]{3,2,1,0:T(8,128)}, u32[]{:S(2)}, u32[]{:S(2)}) collective-permute-start(f32[4,12,128,128]{3,2,1,0:T(8,128)} %collective-permute-done.2.refs_0_), channel_id=1, source_target_pairs={{0,1},{1,0},{2,3},{3,2},{4,5},{5,4},{6,7},{7,6},{8,9},{9,8},{10,11... | collective-permute-start | bytes 9437192 | tf_op jit(solution)/shard_map/ppermute | solution.py:228
  132.7 1.9 collective-permute-start.6
  134.6 0.0 copy-done.6
  134.7 0.0 copy-done.5
  134.7 0.1 pad_maximum_fusion.3
  134.8 3.6 %collective-permute-start = (f32[4,256]{1,0:T(4,128)S(1)}, f32[4,256]{1,0:T(4,128)S(1)}, u32[]{:S(2)}, u32[]{:S(2)}) collective-permute-start(f32[4,256]{1,0:T(4,128)S(1)} %pad_maximum_fusion.3), channel_id=1, source_target_pairs={{0,2},{1,3},{2,0},{3,1},{4,6},{5,7},{6,4},{7,5},{8,10},{9,11},{10,... | collective-permute-start | bytes 12296 | tf_op jit(solution)/shard_map/ppermute | solution.py:228
  138.4 0.0 copy-done.3
  138.4 0.1 constant_dynamic-slice_fusion
  138.5 3.2 %collective-permute-start.4 = (bf16[512,128]{1,0:T(8,128)(2,1)S(1)}, bf16[512,128]{1,0:T(8,128)(2,1)S(1)}, u32[]{:S(2)}, u32[]{:S(2)}) collective-permute-start(bf16[512,128]{1,0:T(8,128)(2,1)S(1)} %get-tuple-element.31), channel_id=1, source_target_pairs={{0,2},{1,3},{2,0},{3,1},{4,6},{5,7},{6,4},{7,5},{8,10},{9,11},{10,... | collective-permute-start | bytes 393224 | tf_op jit(solution)/shard_map/ppermute | solution.py:228
  141.7 4.5 %collective-permute-start.5 = (bf16[512,128]{1,0:T(8,128)(2,1)S(1)}, bf16[512,128]{1,0:T(8,128)(2,1)S(1)}, u32[]{:S(2)}, u32[]{:S(2)}) collective-permute-start(bf16[512,128]{1,0:T(8,128)(2,1)S(1)} %get-tuple-element.30), channel_id=1, source_target_pairs={{0,3},{1,2},{2,1},{3,0},{4,7},{5,6},{6,5},{7,4},{8,11},{9,10},{10,... | collective-permute-start | bytes 393224 | tf_op jit(solution)/shard_map/ppermute | solution.py:228
  146.3 0.0 collective-permute-done
  146.3 0.1 pad_maximum_fusion.2
  146.3 1.9 collective-permute-start.1
  148.3 0.1 pad_add_fusion.blk_ref
  148.3 1.1 collective-permute-done.1
  149.4 2.1 collective-permute-start.7
  151.5 0.1 pad_maximum_fusion.1
  151.6 0.1 copy.13
  151.7 0.4 select_reduce_fusion
  152.1 0.1 copy.15
  152.2 0.1 reshape.37.slot_ref
  152.3 0.0 copy-start.2
  152.3 27.8 %all-to-all-done.2.t_ref = bf16[128,64,128]{2,1,0:T(8,128)(2,1)S(1)} async-done(((bf16[128,64,128]{2,1,0:T(8,128)(2,1)}), bf16[128,64,128]{2,1,0:T(8,128)(2,1)S(1)}, u32[]{:S(2)}, u32[]{:S(2)}) %all-to-all-start.2) | async-done | bytes 2097184 | tf_op jit(solution)/shard_map/all_to_all | solution.py:263
  180.1 1.4 turn.1.refs_2_
  181.5 0.0 collective-permute-done.4.refs_3_
  181.5 0.0 collective-permute-done.5.refs_4_
  181.5 0.0 collective-permute-done.3.refs_1_
  181.5 0.0 copy-done.2
  181.5 0.0 copy-start
  181.5 5.5 %ladder.2 = (bf16[512,128]{1,0:T(8,128)(2,1)S(1)}, bf16[512,128]{1,0:T(8,128)(2,1)S(1)}) custom-call(s32[192]{0:T(256)S(1)} %reshape.37.slot_ref, s32[2]{0:T(128)S(1)} %pad_add_fusion.blk_ref, f32[4,12,128,128]{3,2,1,0:T(8,128)} %collective-permute-done.2.refs_0_, f32[4,12,128,128]{3,2,1,0:T(8,128)} %collective-permute-done.3.refs_1_, ...), custom_call_target="tpu_custom_call" | custom-call | tf_op jit(solution)/shard_map/ladder/pallas_call | solution.py:206
  187.0 0.0 collective-permute-done.7.refs_4_
  187.0 0.0 collective-permute-done.6.refs_1_
  187.0 0.0 copy-done
  187.1 4.3 %ladder.3 = (bf16[512,128]{1,0:T(8,128)(2,1)S(1)}, bf16[512,128]{1,0:T(8,128)(2,1)S(1)}) custom-call(s32[192]{0:T(256)S(1)} %reshape.37.slot_ref, s32[2]{0:T(128)S(1)} %pad_add_fusion.blk_ref, f32[4,12,128,128]{3,2,1,0:T(8,128)S(1)} %copy-done, f32[4,12,128,128]{3,2,1,0:T(8,128)} %collective-permute-done.6.refs_1_, bf16[64,128,128]{2,1,0:T(8,128)(2,1)S(1)} %turn.1.refs_2_, ...), custom_call_target="tpu_custom_call" | custom-call | tf_op jit(solution)/shard_map/ladder/pallas_call | solution.py:206
  191.3 4.4 %collective-permute-start.8 = (bf16[512,128]{1,0:T(8,128)(2,1)S(1)}, bf16[512,128]{1,0:T(8,128)(2,1)S(1)}, u32[]{:S(2)}, u32[]{:S(2)}) collective-permute-start(bf16[512,128]{1,0:T(8,128)(2,1)S(1)} %get-tuple-element.22), channel_id=1, source_target_pairs={{0,1},{1,0},{2,3},{3,2},{4,5},{5,4},{6,7},{7,6},{8,9},{9,8},{10,11... | collective-permute-start | bytes 393224 | tf_op jit(solution)/shard_map/ppermute | solution.py:228
  195.7 4.3 %collective-permute-start.10 = (bf16[512,128]{1,0:T(8,128)(2,1)S(1)}, bf16[512,128]{1,0:T(8,128)(2,1)S(1)}, u32[]{:S(2)}, u32[]{:S(2)}) collective-permute-start(bf16[512,128]{1,0:T(8,128)(2,1)S(1)} %get-tuple-element.24), channel_id=1, source_target_pairs={{0,3},{1,2},{2,1},{3,0},{4,7},{5,6},{6,5},{7,4},{8,11},{9,10},{10,... | collective-permute-start | bytes 393224 | tf_op jit(solution)/shard_map/ppermute | solution.py:228
  200.0 2.4 %collective-permute-start.9 = (bf16[512,128]{1,0:T(8,128)(2,1)S(1)}, bf16[512,128]{1,0:T(8,128)(2,1)S(1)}, u32[]{:S(2)}, u32[]{:S(2)}) collective-permute-start(bf16[512,128]{1,0:T(8,128)(2,1)S(1)} %get-tuple-element.23), channel_id=1, source_target_pairs={{0,2},{1,3},{2,0},{3,1},{4,6},{5,7},{6,4},{7,5},{8,10},{9,11},{10,... | collective-permute-start | bytes 393224 | tf_op jit(solution)/shard_map/ppermute | solution.py:228
  202.4 0.0 collective-permute-done.8
  202.4 1.8 collective-permute-done.10
  204.2 3.7 %collective-permute-done.9 = bf16[512,128]{1,0:T(8,128)(2,1)S(1)} collective-permute-done((bf16[512,128]{1,0:T(8,128)(2,1)S(1)}, bf16[512,128]{1,0:T(8,128)(2,1)S(1)}, u32[]{:S(2)}, u32[]{:S(2)}) %collective-permute-start.9) | collective-permute-done | bytes 131104 | tf_op jit(solution)/shard_map/ppermute | solution.py:228
  208.0 0.1 select_select_fusion.3
  208.0 0.9 pad_maximum_fusion
  (5 shorter events, 0.0 us)
Async XLA Ops:
  0.0 129.2 %collective-permute-start.2 = (f32[4,12,128,128]{3,2,1,0:T(8,128)}, f32[4,12,128,128]{3,2,1,0:T(8,128)}, u32[]{:S(2)}, u32[]{:S(2)}) collective-permute-start(f32[4,12,128,128]{3,2,1,0:T(8,128)} %refs_0_.1), channel_id=1, source_target_pairs={{0,2},{1,3},{2,0},{3,1},{4,6},{5,7},{6,4},{7,5},{8,10},{9,11},{10,... | collective-permute-start | bytes 9437192 | tf_op jit(solution)/shard_map/ppermute | solution.py:228
  5.5 1.0 copy-start.1
  6.5 90.6 %copy-start.4 = (s32[2048,4]{0,1:T(4,128)S(1)}, s32[2048,4]{0,1:T(4,128)}, u32[]{:S(2)}) copy-start(s32[2048,4]{0,1:T(4,128)} %param.10) | copy-start | bytes 98308
  80.8 32.8 %all-to-all-start.1 = ((bf16[64,32,128]{2,1,0:T(8,128)(2,1)}), bf16[64,32,128]{2,1,0:T(8,128)(2,1)S(1)}, u32[]{:S(2)}, u32[]{:S(2)}) async-start(bf16[64,32,128]{2,1,0:T(8,128)(2,1)} %bitcast.8), calls=%async_computation.1 | async-start | bytes 1048576 | tf_op jit(solution)/shard_map/all_to_all | solution.py:253
  119.5 15.2 %copy-start.6 = (s32[4,12]{1,0:T(4,128)S(1)}, s32[4,12]{1,0:T(4,128)}, u32[]{:S(2)}) copy-start(s32[4,12]{1,0:T(4,128)} %param.9) | copy-start | bytes 580
  119.5 15.2 %copy-start.5 = (f32[512]{0:T(512)S(1)}, f32[512]{0:T(512)}, u32[]{:S(2)}) copy-start(f32[512]{0:T(512)} %param.13) | copy-start | bytes 6148
  119.5 18.9 %copy-start.3 = (bf16[512,512]{1,0:T(8,128)(2,1)S(1)}, bf16[512,512]{1,0:T(8,128)(2,1)}, u32[]{:S(2)}) copy-start(bf16[512,512]{1,0:T(8,128)(2,1)} %param.11) | copy-start | bytes 1572868
  119.5 60.6 %all-to-all-start.2 = ((bf16[128,64,128]{2,1,0:T(8,128)(2,1)}), bf16[128,64,128]{2,1,0:T(8,128)(2,1)S(1)}, u32[]{:S(2)}, u32[]{:S(2)}) async-start(bf16[128,64,128]{2,1,0:T(8,128)(2,1)} %bitcast.10), calls=%async_computation.2 | async-start | bytes 4194304 | tf_op jit(solution)/shard_map/all_to_all | solution.py:263
  129.2 52.3 %collective-permute-start.3 = (f32[4,12,128,128]{3,2,1,0:T(8,128)}, f32[4,12,128,128]{3,2,1,0:T(8,128)}, u32[]{:S(2)}, u32[]{:S(2)}) collective-permute-start(f32[4,12,128,128]{3,2,1,0:T(8,128)} %collective-permute-done.2.refs_0_), channel_id=1, source_target_pairs={{0,1},{1,0},{2,3},{3,2},{4,5},{5,4},{6,7},{7,6},{8,9},{9,8},{10,11... | collective-permute-start | bytes 9437192 | tf_op jit(solution)/shard_map/ppermute | solution.py:228
  132.7 54.3 %collective-permute-start.6 = (f32[4,12,128,128]{3,2,1,0:T(8,128)}, f32[4,12,128,128]{3,2,1,0:T(8,128)}, u32[]{:S(2)}, u32[]{:S(2)}) collective-permute-start(f32[4,12,128,128]{3,2,1,0:T(8,128)} %refs_0_.1), channel_id=1, source_target_pairs={{0,1},{1,0},{2,3},{3,2},{4,5},{5,4},{6,7},{7,6},{8,9},{9,8},{10,11... | collective-permute-start | bytes 9437192 | tf_op jit(solution)/shard_map/ppermute | solution.py:228
  134.8 11.5 %collective-permute-start = (f32[4,256]{1,0:T(4,128)S(1)}, f32[4,256]{1,0:T(4,128)S(1)}, u32[]{:S(2)}, u32[]{:S(2)}) collective-permute-start(f32[4,256]{1,0:T(4,128)S(1)} %pad_maximum_fusion.3), channel_id=1, source_target_pairs={{0,2},{1,3},{2,0},{3,1},{4,6},{5,7},{6,4},{7,5},{8,10},{9,11},{10,... | collective-permute-start | bytes 12296 | tf_op jit(solution)/shard_map/ppermute | solution.py:228
  138.5 43.0 %collective-permute-start.4 = (bf16[512,128]{1,0:T(8,128)(2,1)S(1)}, bf16[512,128]{1,0:T(8,128)(2,1)S(1)}, u32[]{:S(2)}, u32[]{:S(2)}) collective-permute-start(bf16[512,128]{1,0:T(8,128)(2,1)S(1)} %get-tuple-element.31), channel_id=1, source_target_pairs={{0,2},{1,3},{2,0},{3,1},{4,6},{5,7},{6,4},{7,5},{8,10},{9,11},{10,... | collective-permute-start | bytes 393224 | tf_op jit(solution)/shard_map/ppermute | solution.py:228
  141.7 39.8 %collective-permute-start.5 = (bf16[512,128]{1,0:T(8,128)(2,1)S(1)}, bf16[512,128]{1,0:T(8,128)(2,1)S(1)}, u32[]{:S(2)}, u32[]{:S(2)}) collective-permute-start(bf16[512,128]{1,0:T(8,128)(2,1)S(1)} %get-tuple-element.30), channel_id=1, source_target_pairs={{0,3},{1,2},{2,1},{3,0},{4,7},{5,6},{6,5},{7,4},{8,11},{9,10},{10,... | collective-permute-start | bytes 393224 | tf_op jit(solution)/shard_map/ppermute | solution.py:228
  146.3 3.1 %collective-permute-start.1 = (f32[8,256]{1,0:T(8,128)S(1)}, f32[8,256]{1,0:T(8,128)S(1)}, u32[]{:S(2)}, u32[]{:S(2)}) collective-permute-start(f32[8,256]{1,0:T(8,128)S(1)} %pad_maximum_fusion.2), channel_id=1, source_target_pairs={{0,1},{1,0},{2,3},{3,2},{4,5},{5,4},{6,7},{7,6},{8,9},{9,8},{10,11... | collective-permute-start | bytes 24584 | tf_op jit(solution)/shard_map/ppermute | solution.py:228
  149.4 37.6 %collective-permute-start.7 = (bf16[512,128]{1,0:T(8,128)(2,1)S(1)}, bf16[512,128]{1,0:T(8,128)(2,1)S(1)}, u32[]{:S(2)}, u32[]{:S(2)}) collective-permute-start(bf16[512,128]{1,0:T(8,128)(2,1)S(1)} %get-tuple-element.29), channel_id=1, source_target_pairs={{0,1},{1,0},{2,3},{3,2},{4,5},{5,4},{6,7},{7,6},{8,9},{9,8},{10,11... | collective-permute-start | bytes 393224 | tf_op jit(solution)/shard_map/ppermute | solution.py:228
  152.3 29.2 %copy-start.2 = (f32[512]{0:T(512)S(1)}, f32[512]{0:T(512)}, u32[]{:S(2)}) copy-start(f32[512]{0:T(512)} %param.12) | copy-start | bytes 6148
  181.5 5.5 %copy-start = (f32[4,12,128,128]{3,2,1,0:T(8,128)S(1)}, f32[4,12,128,128]{3,2,1,0:T(8,128)}, u32[]{:S(2)}) copy-start(f32[4,12,128,128]{3,2,1,0:T(8,128)} %refs_0_.1) | copy-start | bytes 9437188
  191.3 11.1 %collective-permute-start.8 = (bf16[512,128]{1,0:T(8,128)(2,1)S(1)}, bf16[512,128]{1,0:T(8,128)(2,1)S(1)}, u32[]{:S(2)}, u32[]{:S(2)}) collective-permute-start(bf16[512,128]{1,0:T(8,128)(2,1)S(1)} %get-tuple-element.22), channel_id=1, source_target_pairs={{0,1},{1,0},{2,3},{3,2},{4,5},{5,4},{6,7},{7,6},{8,9},{9,8},{10,11... | collective-permute-start | bytes 393224 | tf_op jit(solution)/shard_map/ppermute | solution.py:228
  195.7 8.5 %collective-permute-start.10 = (bf16[512,128]{1,0:T(8,128)(2,1)S(1)}, bf16[512,128]{1,0:T(8,128)(2,1)S(1)}, u32[]{:S(2)}, u32[]{:S(2)}) collective-permute-start(bf16[512,128]{1,0:T(8,128)(2,1)S(1)} %get-tuple-element.24), channel_id=1, source_target_pairs={{0,3},{1,2},{2,1},{3,0},{4,7},{5,6},{6,5},{7,4},{8,11},{9,10},{10,... | collective-permute-start | bytes 393224 | tf_op jit(solution)/shard_map/ppermute | solution.py:228
  200.0 8.0 %collective-permute-start.9 = (bf16[512,128]{1,0:T(8,128)(2,1)S(1)}, bf16[512,128]{1,0:T(8,128)(2,1)S(1)}, u32[]{:S(2)}, u32[]{:S(2)}) collective-permute-start(bf16[512,128]{1,0:T(8,128)(2,1)S(1)} %get-tuple-element.23), channel_id=1, source_target_pairs={{0,2},{1,3},{2,0},{3,1},{4,6},{5,7},{6,4},{7,5},{8,10},{9,11},{10,... | collective-permute-start | bytes 393224 | tf_op jit(solution)/shard_map/ppermute | solution.py:228
